TPU v7x, 8 devices: a whole 2x2x1 slice. The times are simulated.
8 devices in a mesh: fsdp: 8 (over z, y, x, core).
Axes of the slice: x: 2, y: 2, z: 1, core: 2. Of those that a mesh axis runs over, the one named last changes fastest.
Arguments:
- tokens: int32 [96, 256], P('fsdp')
- positions: int32 [96, 256], P('fsdp')
- embed_table: bfloat16 [49152, 576], P('fsdp')
- attn_norm: bfloat16 [576], P('fsdp')
- w_query: bfloat16 [576, 576], P('fsdp')
- w_key: bfloat16 [576, 192], P('fsdp')
- w_value: bfloat16 [576, 192], P('fsdp')
- q_norm: bfloat16 [64], replicated
- k_norm: bfloat16 [64], replicated
- w_out: bfloat16 [576, 576], P('fsdp')
- mlp_norm: bfloat16 [576], P('fsdp')
- w_gate: bfloat16 [576, 1536], P('fsdp')
- w_up: bfloat16 [576, 1536], P('fsdp')
- w_down: bfloat16 [1536, 576], P('fsdp')
- dy_out: bfloat16 [96, 256, 576], P('fsdp')
Outputs:
- output 1: bfloat16 [96, 256, 576], P('fsdp')
- output 2: float32 [49152, 576], P('fsdp')
- output 3: float32 [576], P('fsdp')
- output 4: float32 [576, 576], P('fsdp')
- output 5: float32 [576, 192], P('fsdp')
- output 6: float32 [576, 192], P('fsdp')
- output 7: float32 [64], replicated
- output 8: float32 [64], replicated
- output 9: float32 [576, 576], P('fsdp')
- output 10: float32 [576], P('fsdp')
- output 11: float32 [576, 1536], P('fsdp')
- output 12: float32 [576, 1536], P('fsdp')
- output 13: float32 [1536, 576], P('fsdp')
All inputs are finite; a program needn't handle non-finite values.
Results may differ from a plain program's by a relative error of at most 0.02.
Values are sent between devices in bfloat16 or wider.
A program may use at most 1 GiB of HBM per device.

v0:
```python
import functools
import math
import jax
import jax.numpy as jnp
from jax import lax
from jax.experimental import pallas as pl
from jax.experimental.pallas import tpu as pltpu
from jax.sharding import PartitionSpec as P

NORM_EPS = 1e-6
ROPE_THETA = 1.0e6
AXIS_NAME = 'fsdp'
SEQ = 256
D = 576
FF = 1536
HEAD = 64
HEADS = 9
KV = 3
GRP = 3
C_OUT, C_GATE, C_UP, C_NORM, C_HEAD = 1024, 1664, 3200, 4736, 4864
W_COLS, G_COLS = 4864, 4992
X_K, X_V, X_COLS = HEADS * 128, (HEADS + KV) * 128, (HEADS + 2 * KV) * 128
FF_STEP = 512
CHUNKS = (4, 4, 4)
BF, F32 = jnp.bfloat16, jnp.float32


def mm(lhs, rhs, lhs_dim=1, rhs_dim=0):
    return lax.dot_general(lhs, rhs, (((lhs_dim,), (rhs_dim,)), ((), ())), preferred_element_type=F32)


def fold8(values):
    return jnp.sum(values.reshape(values.shape[0] // 8, 8, values.shape[1]), axis=0)


def norm_bwd(grad_out, normed, inv_rms, norm_gain):
    grad_normed = grad_out * norm_gain
    return inv_rms * (grad_normed - normed * jnp.mean(grad_normed * normed, axis=-1, keepdims=True))


def head_norm_rope(head_ext, gain_ext, cs):
    head_f = head_ext.astype(F32)
    inv = lax.rsqrt(jnp.sum(head_f * head_f, axis=-1, keepdims=True) * (1.0 / 128) + NORM_EPS)
    turned = head_f * inv * gain_ext * cs
    return turned + pltpu.roll(turned, 64, 1), inv


def head_norm_rope_bwd(grad_ext, head_ext, inv, gain_low, cs_bwd, low):
    turned = grad_ext * cs_bwd
    grad_t = turned + pltpu.roll(turned, 64, 1)
    normed = jnp.where(low, head_ext.astype(F32), 0.0) * inv
    grad_normed = grad_t * gain_low
    mean_term = jnp.sum(grad_normed * normed, axis=-1, keepdims=True) * (1.0 / HEAD)
    return inv * (grad_normed - normed * mean_term), fold8(grad_t * normed)


def pack_pairs(heads):
    tiles = []
    for idx in range(0, len(heads), 2):
        tile = heads[idx]
        if idx + 1 < len(heads):
            tile = tile + pltpu.roll(heads[idx + 1], 64, 1)
        tiles.append(tile.astype(BF))
    return tiles


def layer_kernel(first, last, steps, *refs):
    (x_ref, dy_ref, cs_ref, w_ref, wd_ref, gains_ref, head_gains_ref) = refs[:7]
    refs = refs[7:]
    if not first:
        acc_in, accd_in, _ = refs[:3]
        refs = refs[3:]
    (y_ref, dx_ref, acc_out, accd_out) = refs[:4]
    (acc, accd, norm_acc, head_acc, wx, wox, qkv_s, probs_s, tbuf, sems) = refs[4:]
    step = pl.program_id(0)
    low = lax.broadcasted_iota(jnp.int32, (1, 128), 1) < 64

    @pl.when(step == 0)
    def _():
        if first:
            acc[...] = jnp.zeros_like(acc)
            accd[...] = jnp.zeros_like(accd)
        else:
            load_acc = pltpu.make_async_copy(acc_in, acc, sems.at[0])
            load_accd = pltpu.make_async_copy(accd_in, accd, sems.at[1])
            load_acc.start()
            load_accd.start()
        norm_acc[...] = jnp.zeros_like(norm_acc)
        head_acc[...] = jnp.zeros_like(head_acc)
        for h in range(HEADS + 2 * KV):
            tile = w_ref[:, (h // 2) * 128:(h // 2) * 128 + 128].astype(F32)
            moved = pltpu.roll(tile, 64, 1)
            if h >= HEADS + KV:
                both = jnp.where(low, moved if h % 2 else tile, 0.0)
            else:
                twice = jnp.where(low, moved, tile) if h % 2 else jnp.where(low, tile, moved)
                both = jnp.where(low, twice, pltpu.roll(twice, 32, 1))
            wx[:, h * 128:h * 128 + 128] = both.astype(BF)
        for h in range(HEADS):
            wox[h * 128:h * 128 + 64, :] = w_ref[h * 64:h * 64 + 64, C_OUT:C_OUT + D]
            wox[h * 128 + 64:h * 128 + 128, :] = jnp.zeros((64, D), BF)
        if not first:
            load_acc.wait()
            load_accd.wait()

    gain1 = gains_ref[0:1, :]
    gain2 = gains_ref[1:2, :]
    gain_q, gain_k = head_gains_ref[0:1, :], head_gains_ref[1:2, :]
    low_q, low_k = jnp.where(low, gain_q, 0.0), jnp.where(low, gain_k, 0.0)
    cs = cs_ref[...]
    cs_bwd = jnp.where(low, cs, -cs)
    causal = ((lax.broadcasted_iota(jnp.int32, (GRP * SEQ, SEQ), 0) & (SEQ - 1))
              >= lax.broadcasted_iota(jnp.int32, (GRP * SEQ, SEQ), 1))

    x = x_ref[...].astype(F32)
    inv1 = lax.rsqrt(jnp.mean(x * x, axis=-1, keepdims=True) + NORM_EPS)
    m1 = (x * inv1 * gain1).astype(BF)
    qkv_s[...] = mm(m1, wx[...]).astype(BF)
    saved = []
    heads = []
    for g in range(KV):
        ke = qkv_s[:, X_K + g * 128:X_K + g * 128 + 128]
        v0 = qkv_s[:, X_V + g * 128:X_V + g * 128 + 128]
        k_rot, k_inv = head_norm_rope(ke, gain_k, cs)
        k0 = jnp.where(low, k_rot, 0.0).astype(BF)
        k_swap = jnp.where(low, k_rot, pltpu.roll(k_rot, 32, 1)).astype(BF)
        qs, q_swaps, q_invs = [], [], []
        for r in range(GRP):
            h = g * GRP + r
            q_rot, q_inv = head_norm_rope(qkv_s[:, h * 128:h * 128 + 128], gain_q, cs)
            qs.append(q_rot.astype(BF))
            q_swaps.append(jnp.where(low, q_rot, pltpu.roll(q_rot, 32, 1)).astype(BF))
            q_invs.append(q_inv)
        scores = mm(jnp.concatenate(qs, axis=0), k0, 1, 1) * (HEAD ** -0.5)
        scores = jnp.where(causal, scores, -1e30)
        expd = jnp.exp(scores - jnp.max(scores, axis=-1, keepdims=True))
        probs = expd / jnp.sum(expd, axis=-1, keepdims=True)
        probs_s[g] = probs
        o = mm(probs.astype(BF), v0)
        for r in range(GRP):
            heads.append(o[r * SEQ:(r + 1) * SEQ])
        saved.append((k_swap, jnp.concatenate(q_swaps, axis=0), q_invs, k_inv))
    attn = jnp.concatenate(pack_pairs(heads), axis=1)
    hidden_b = (x + mm(attn[:, :D], w_ref[:, C_OUT:C_OUT + D])).astype(BF)
    hidden = hidden_b.astype(F32)
    inv2 = lax.rsqrt(jnp.mean(hidden * hidden, axis=-1, keepdims=True) + NORM_EPS)
    m2 = (hidden * inv2 * gain2).astype(BF)

    dy = dy_ref[...]
    m2_t = m2.T
    dy_t = dy.T
    y = hidden
    dm2 = jnp.zeros((SEQ, D), F32)
    for f in range(0, FF, FF_STEP):
        wg = w_ref[:, C_GATE + f:C_GATE + f + FF_STEP]
        wu = w_ref[:, C_UP + f:C_UP + f + FF_STEP]
        wd = wd_ref[f:f + FF_STEP, :]
        gate = mm(m2, wg)
        up = mm(m2, wu)
        dact = mm(dy, wd, 1, 1)
        sig = 1.0 / (1.0 + jnp.exp(-gate))
        silu = gate * sig
        act = (silu * up).astype(BF)
        y = y + mm(act, wd)
        dgate = (dact * up * sig * (1.0 + gate * (1.0 - sig))).astype(BF)
        dup = (dact * silu).astype(BF)
        dm2 = dm2 + mm(dgate, wg, 1, 1) + mm(dup, wu, 1, 1)
        acc[:, C_GATE + f:C_GATE + f + FF_STEP] += mm(m2_t, dgate)
        acc[:, C_UP + f:C_UP + f + FF_STEP] += mm(m2_t, dup)
        accd[:, f:f + FF_STEP] += mm(dy_t, act)
    y_ref[...] = y.astype(BF)
    n2 = hidden * inv2
    norm_acc[1] += fold8(dm2 * n2)
    dh = dy.astype(F32) + norm_bwd(dm2, n2, inv2, gain2)
    dh_b = dh.astype(BF)
    acc[:, C_OUT:C_OUT + D] += mm(attn.T, dh_b)[:D]

    do = mm(dh_b, wox[...], 1, 1).astype(BF)
    dqs, dks, dvs = [], [], []
    for g in range(KV):
        k_swap, q_swap, q_invs, k_inv = saved[g]
        v0 = qkv_s[:, X_V + g * 128:X_V + g * 128 + 128]
        do_g = jnp.concatenate([do[:, h * 128:h * 128 + 128] for h in range(g * GRP, (g + 1) * GRP)], axis=0)
        probs = probs_s[g]
        dprobs = mm(do_g, v0, 1, 1)
        dvs.append(mm(do_g.T, probs.astype(BF)).T)
        dscores = probs * (dprobs - jnp.sum(dprobs * probs, axis=-1, keepdims=True)) * (HEAD ** -0.5)
        dscores = dscores.astype(BF)
        dq = mm(dscores, k_swap)
        dk = mm(q_swap.T, dscores).T
        dk, dk_gain = head_norm_rope_bwd(dk, qkv_s[:, X_K + g * 128:X_K + g * 128 + 128], k_inv, low_k, cs_bwd, low)
        dks.append(dk)
        head_acc[1] += dk_gain
        for r in range(GRP):
            h = g * GRP + r
            dq_h, dq_gain = head_norm_rope_bwd(dq[r * SEQ:(r + 1) * SEQ], qkv_s[:, h * 128:h * 128 + 128], q_invs[r], low_q, cs_bwd, low)
            dqs.append(dq_h)
            head_acc[0] += dq_gain
    dqkv = jnp.concatenate(pack_pairs(dqs + dks + dvs), axis=1)
    acc[:, 0:1024] += mm(m1.T, dqkv)
    dm1 = mm(dqkv, w_ref[:, 0:1024], 1, 1)
    n1 = x * inv1
    norm_acc[0] += fold8(dm1 * n1)
    dx = jnp.concatenate([dh + norm_bwd(dm1, n1, inv1, gain1), jnp.zeros((SEQ, 64), F32)], axis=1)
    for j in range(5):
        dx_ref[pl.ds(j, SEQ, stride=5), :] = dx[:, j * 128:j * 128 + 128]

    @pl.when(step == steps - 1)
    def _():
        top = lax.broadcasted_iota(jnp.int32, (128, 1), 0)
        rows1 = jnp.sum(norm_acc[0], axis=0, keepdims=True)
        rows2 = jnp.sum(norm_acc[1], axis=0, keepdims=True)
        both = jnp.where(top == 0, rows1, 0.0) + jnp.where(top == 1, rows2, 0.0)
        for c in range(0, D, 128):
            width = min(128, D - c)
            acc[c:c + width, C_NORM:C_NORM + 128] += both[:, c:c + width].T
        head_q = jnp.sum(head_acc[0], axis=0, keepdims=True)
        head_k = jnp.sum(head_acc[1], axis=0, keepdims=True)
        head_row = jnp.where(low, head_q, pltpu.roll(head_k, 64, 1))
        acc[:, C_HEAD:C_HEAD + 128] += jnp.broadcast_to(head_row, (D, 128))
        store_acc = pltpu.make_async_copy(acc, acc_out, sems.at[0])
        store_acc.start()
        if last:
            for f in range(0, FF, 512):
                for s in range(0, D, 64):
                    tbuf[:, s:s + 64] = accd[s:s + 64, f:f + 512].T
                store = pltpu.make_async_copy(tbuf, accd_out.at[pl.ds(f, 512), :], sems.at[1])
                store.start()
                store.wait()
        else:
            store_accd = pltpu.make_async_copy(accd, accd_out, sems.at[1])
            store_accd.start()
            store_accd.wait()
        store_acc.wait()


ROW_WORDS = 5
GROUP_ROWS = 16
PAD_ROWS = 16


def gather_kernel(blocks, ids_ref, tab_ref, *refs):
    outs, (lin, buf) = refs[:-2], refs[-2:]
    step = pl.program_id(0)
    rows = tab_ref.shape[1]

    @pl.when(step == 0)
    def _():
        def build(b, _):
            at = pl.multiple_of(b * 128, 128)
            for j in range(ROW_WORDS):
                part = tab_ref[j * 128:min(j * 128 + 128, D), pl.ds(at, 128)].astype(F32)
                if part.shape[0] < 128:
                    part = jnp.concatenate([part, jnp.zeros((128 - part.shape[0], 128), F32)], axis=0)
                lin[pl.ds(at * ROW_WORDS + j, 128, stride=ROW_WORDS), :] = part.T
            return 0

        lax.fori_loop(0, rows // 128, build, 0)
        lin[rows * ROW_WORDS:(rows + PAD_ROWS) * ROW_WORDS, :] = jnp.zeros((PAD_ROWS * ROW_WORDS, 128), F32)

    def pick(k, _):
        base = k * GROUP_ROWS
        got = [lin[pl.ds(ids_ref[step * SEQ + base + u], ROW_WORDS), :] for u in range(GROUP_ROWS)]
        for u in range(GROUP_ROWS):
            buf[pl.ds((base + u) * ROW_WORDS, ROW_WORDS), :] = got[u]
        return 0

    lax.fori_loop(0, SEQ // GROUP_ROWS, pick, 0)
    first = 0
    for out, count in zip(outs, blocks):
        @pl.when((step >= first) & (step < first + count))
        def _():
            for j in range(ROW_WORDS):
                width = min(128, D - j * 128)
                out[:, j * 128:j * 128 + width] = buf[pl.ds(j, SEQ, stride=ROW_WORDS), :][:, :width].astype(BF)

        first += count


def gather_rows(ids, table_t, blocks):
    starts = [sum(blocks[:c]) for c in range(len(blocks))]
    rows = table_t.shape[1]
    out_spec = lambda c: pl.BlockSpec((SEQ, D), lambda i, ids: (jnp.clip(i - starts[c], 0, blocks[c] - 1), 0))
    return pl.pallas_call(
        functools.partial(gather_kernel, blocks),
        grid_spec=pltpu.PrefetchScalarGridSpec(
            num_scalar_prefetch=1,
            grid=(sum(blocks),),
            in_specs=[pl.BlockSpec(table_t.shape, lambda i, ids: (0, 0), pipeline_mode=pl.Buffered(1))],
            out_specs=[out_spec(c) for c in range(len(blocks))],
            scratch_shapes=[pltpu.VMEM(((rows + PAD_ROWS) * ROW_WORDS, 128), F32), pltpu.VMEM((SEQ * ROW_WORDS, 128), F32)],
        ),
        out_shape=[jax.ShapeDtypeStruct((count * SEQ, D), BF) for count in blocks],
        compiler_params=pltpu.CompilerParams(dimension_semantics=('arbitrary',), vmem_limit_bytes=48 << 20),
        cost_estimate=pl.CostEstimate(flops=40_000_000_000, bytes_accessed=40_000_000, transcendentals=0),
        name='gather_rows',
    )(ids, table_t)


def scatter_kernel(first, last, blocks, ids_ref, clash_ref, rows_ref, *refs):
    if not first:
        acc_in, refs = refs[0], refs[1:]
    out_ref, acc, sem = refs[:3]
    tbuf = refs[3] if last else None
    step = pl.program_id(0)
    rows = acc.shape[0] // ROW_WORDS - PAD_ROWS

    @pl.when(step == 0)
    def _():
        if first:
            acc[...] = jnp.zeros_like(acc)
        else:
            load = pltpu.make_async_copy(acc_in, acc, sem)
            load.start()
            load.wait()

    groups = SCATTER_ROWS // GROUP_ROWS

    def add(k, _):
        base = k * GROUP_ROWS
        spots = [pl.ds(ids_ref[step * SCATTER_ROWS + base + u], ROW_WORDS) for u in range(GROUP_ROWS)]
        from_row = lambda u: rows_ref[pl.ds((base + u) * ROW_WORDS, ROW_WORDS), :]
        clash = clash_ref[step * groups + k]

        @pl.when(clash == 0)
        def _():
            sums = [acc[spots[u], :] + from_row(u) for u in range(GROUP_ROWS)]
            for u in range(GROUP_ROWS):
                acc[spots[u], :] = sums[u]

        @pl.when(clash != 0)
        def _():
            for u in range(GROUP_ROWS):
                acc[spots[u], :] += from_row(u)

        return 0

    lax.fori_loop(0, groups, add, 0)

    @pl.when(step == blocks - 1)
    def _():
        if last:
            def flush(b, _):
                slot = lax.rem(b, 2)
                at = pl.multiple_of(b * 128, 128)
                store = pltpu.make_async_copy(tbuf.at[slot], out_ref.at[:, pl.ds(at, 128)], sem)

                @pl.when(b >= 1)
                def _():
                    store.wait()

                for j in range(ROW_WORDS):
                    width = min(128, D - j * 128)
                    part = acc[pl.ds(at * ROW_WORDS + j, 128, stride=ROW_WORDS), :].T
                    tbuf[slot, j * 128:j * 128 + width, :] = part[:width]
                store.start()
                return 0

            lax.fori_loop(0, rows // 128, flush, 0)
            pltpu.make_async_copy(tbuf.at[0], out_ref.at[:, pl.ds(0, 128)], sem).wait()
        else:
            store = pltpu.make_async_copy(acc, out_ref, sem)
            store.start()
            store.wait()


SCATTER_ROWS = 512


def scatter_rows(ids, clash, rows_in, table_rows, carry, last):
    first = carry is None
    blocks = rows_in.shape[0] // (SCATTER_ROWS * ROW_WORDS)
    acc_shape = ((table_rows + PAD_ROWS) * ROW_WORDS, 128)
    anyspec = pl.BlockSpec(memory_space=pl.ANY)
    scratch = [pltpu.VMEM(acc_shape, F32), pltpu.SemaphoreType.DMA]
    if last:
        scratch.append(pltpu.VMEM((2, D, 128), F32))
    return pl.pallas_call(
        functools.partial(scatter_kernel, first, last, blocks),
        grid_spec=pltpu.PrefetchScalarGridSpec(
            num_scalar_prefetch=2,
            grid=(blocks,),
            in_specs=[pl.BlockSpec((SCATTER_ROWS * ROW_WORDS, 128), lambda i, *_: (i, 0))] + ([] if first else [anyspec]),
            out_specs=anyspec,
            scratch_shapes=scratch,
        ),
        out_shape=jax.ShapeDtypeStruct((D, table_rows) if last else acc_shape, F32),
        input_output_aliases={} if first or last else {3: 0},
        compiler_params=pltpu.CompilerParams(dimension_semantics=('arbitrary',), vmem_limit_bytes=40 << 20),
        cost_estimate=pl.CostEstimate(flops=20_000_000_000, bytes_accessed=60_000_000, transcendentals=0),
        name='scatter_rows',
    )(*([ids, clash, rows_in] + ([] if first else [carry])))


def layer_chunk(x, dy, cs, w_pack, w_down, gains, head_gains, start, carry, last, total):
    steps = x.shape[0] // SEQ
    first = carry is None
    whole = lambda shape: pl.BlockSpec(shape, lambda i: (0,) * len(shape), pipeline_mode=pl.Buffered(1))
    here = lambda cols: pl.BlockSpec((SEQ, cols), lambda i: (i + start, 0))
    anyspec = pl.BlockSpec(memory_space=pl.ANY)
    in_specs = [pl.BlockSpec((SEQ, D), lambda i: (i, 0)), here(D), here(128), whole(w_pack.shape), whole(w_down.shape), whole(gains.shape), whole(head_gains.shape)]
    args = [x, dy, cs, w_pack, w_down, gains, head_gains]
    aliases = {}
    if not first:
        in_specs += [anyspec] * 3
        args += list(carry)
        aliases = {7: 2, 9: 0} if last else {7: 2, 8: 3, 9: 0}
    out_shape = [
        jax.ShapeDtypeStruct((total, D), BF),
        jax.ShapeDtypeStruct((steps * SEQ * 5, 128), F32),
        jax.ShapeDtypeStruct((D, G_COLS), F32),
        jax.ShapeDtypeStruct((FF, D) if last else (D, FF), F32),
    ]
    y, dx, acc, accd = pl.pallas_call(
        functools.partial(layer_kernel, first, last, steps),
        grid=(steps,),
        in_specs=in_specs,
        out_specs=[here(D), pl.BlockSpec((SEQ * 5, 128), lambda i: (i, 0)), anyspec, anyspec],
        out_shape=out_shape,
        scratch_shapes=[
            pltpu.VMEM((D, G_COLS), F32),
            pltpu.VMEM((D, FF), F32),
            pltpu.VMEM((2, 8, D), F32),
            pltpu.VMEM((2, 8, 128), F32),
            pltpu.VMEM((D, X_COLS), BF),
            pltpu.VMEM((HEADS * 128, D), BF),
            pltpu.VMEM((SEQ, X_COLS), BF),
            pltpu.VMEM((KV, GRP * SEQ, SEQ), F32),
            pltpu.VMEM((512, D), F32),
            pltpu.SemaphoreType.DMA((2,)),
        ],
        input_output_aliases=aliases,
        compiler_params=pltpu.CompilerParams(dimension_semantics=('arbitrary',), vmem_limit_bytes=60 << 20),
        cost_estimate=pl.CostEstimate(flops=steps * 6_000_000_000, bytes_accessed=steps * 2_500_000 + 45_000_000, transcendentals=steps * 1_000_000),
        name='layer_chunk',
    )(*args)
    return dx, (acc, accd, y)


def solution(mesh):
    row_spec = P(AXIS_NAME, None)
    vec_spec = P(AXIS_NAME)
    full_spec = P(None)
    batch_spec = P(AXIS_NAME, None, None)
    weight_specs = (vec_spec, row_spec, row_spec, row_spec, full_spec, full_spec, row_spec, vec_spec, row_spec, row_spec, row_spec)

    def device_step(tokens, positions, table_shard, attn_norm, w_query, w_key, w_value, q_norm, k_norm, w_out, mlp_norm, w_gate, w_up, w_down, dy_out):
        batch_len, seq_len = tokens.shape
        devices = lax.axis_size(AXIS_NAME)
        rows_local = table_shard.shape[0]
        shard = w_query.shape[0]
        all_ids = lax.all_gather(tokens, AXIS_NAME)
        norms = jnp.concatenate([attn_norm[:, None], mlp_norm[:, None], jnp.zeros((shard, W_COLS - C_NORM - 2), BF)], axis=1)
        pad = jnp.zeros((shard, 64), BF)
        packed = jnp.concatenate([w_query, w_key, w_value, pad, w_out, pad, w_gate, w_up, norms], axis=1)
        w_pack = lax.all_gather(packed, AXIS_NAME, tiled=True)
        w_down_full = lax.all_gather(w_down, AXIS_NAME, tiled=True)
        gains = w_pack[:, C_NORM:C_NORM + 2].T.astype(F32)
        head_gains = jnp.stack([q_norm, k_norm]).astype(F32)
        swapped = jnp.concatenate([head_gains[:, 32:], head_gains[:, :32]], axis=1)
        head_gains = jnp.concatenate([head_gains, swapped], axis=1)

        inv_freq = jnp.exp(jnp.arange(HEAD // 2, dtype=F32) * (-2.0 * math.log(ROPE_THETA) / HEAD))
        angles = positions.reshape(-1, 1).astype(F32) * inv_freq
        cos_t, sin_t = jnp.cos(angles), jnp.sin(angles)
        cs = jnp.concatenate([cos_t, cos_t, -sin_t, sin_t], axis=1)
        dy = dy_out.reshape(-1, D)

        local_ids = all_ids - lax.axis_index(AXIS_NAME) * rows_local
        is_owner = (local_ids >= 0) & (local_ids < rows_local)
        starts = [sum(CHUNKS[:c]) for c in range(len(CHUNKS))]
        by_chunk = lambda values: [values[:, s:s + n].reshape(-1) for s, n in zip(starts, CHUNKS)]
        take_from = by_chunk(jnp.where(is_owner, local_ids, rows_local) * ROW_WORDS)
        spare = lax.broadcasted_iota(jnp.int32, all_ids.shape, 2) % GROUP_ROWS + rows_local
        add_to = jnp.where(is_owner, local_ids, spare)
        grouped = add_to.reshape(all_ids.shape[:2] + (seq_len // GROUP_ROWS, GROUP_ROWS))
        pairs = (grouped[..., :, None] == grouped[..., None, :]) & (jnp.arange(GROUP_ROWS)[:, None] > jnp.arange(GROUP_ROWS)[None, :])
        clashes = by_chunk(jnp.any(pairs, axis=(-1, -2)).astype(jnp.int32))
        add_to = by_chunk(add_to * ROW_WORDS)

        picked = gather_rows(jnp.concatenate(take_from), table_shard.T, tuple(devices * n for n in CHUNKS))
        xs = [lax.psum_scatter(rows, AXIS_NAME, scatter_dimension=0, tiled=True) for rows in picked]
        carry = None
        rows_of = []
        for idx in range(len(CHUNKS)):
            x_chunk = xs[idx]
            dx, carry = layer_chunk(x_chunk, dy, cs, w_pack, w_down_full, gains, head_gains, starts[idx], carry, idx == len(CHUNKS) - 1, batch_len * seq_len)
            rows_of.append(lax.all_gather(dx, AXIS_NAME, tiled=True))
        acc, d_w_down, y = carry
        d_table = None
        for idx in range(len(CHUNKS)):
            d_table = scatter_rows(add_to[idx], clashes[idx], rows_of[idx], rows_local, d_table, idx == len(CHUNKS) - 1)
        d_table = d_table.T
        g_pack = lax.optimization_barrier(lax.psum_scatter(acc, AXIS_NAME, scatter_dimension=0, tiled=True))
        d_w_down = lax.psum_scatter(d_w_down, AXIS_NAME, scatter_dimension=0, tiled=True)
        kv_cols = w_key.shape[1]
        return (y.reshape(batch_len, seq_len, D), d_table, g_pack[:, C_NORM], g_pack[:, :D], g_pack[:, D:D + kv_cols], g_pack[:, D + kv_cols:D + 2 * kv_cols],
                g_pack[0, C_HEAD:C_HEAD + HEAD], g_pack[0, C_HEAD + HEAD:C_HEAD + 2 * HEAD], g_pack[:, C_OUT:C_OUT + D], g_pack[:, C_NORM + 1],
                g_pack[:, C_GATE:C_GATE + FF], g_pack[:, C_UP:C_UP + FF], d_w_down)

    return jax.shard_map(device_step, mesh=mesh, in_specs=(row_spec, row_spec, row_spec) + weight_specs + (batch_spec,), out_specs=(batch_spec, row_spec) + weight_specs, check_vma=False)
```

profile of v0, /device:TPU:0, one launch (start us, length us, event | category | flops | bytes accessed | tf_op | source)
XLA Modules:
  0.0 935.4 jit_solution(13477485893495864666)
XLA Ops:
  7.2 0.0 all-gather.8.cloned.1.call-start
  7.2 0.8 copy.77
  8.0 0.8 copy.78
  8.8 2.1 concatenate.14
  10.9 0.0 all-gather.8.cloned.1.call-update
  10.9 0.0 all-gather.10.cloned.1.call-start
  11.0 0.7 all-gather.10.cloned.1.call-update
  11.7 0.0 reduce-scatter.12.cloned.1.call-start
  11.7 14.9 %all-gather.1 = s32[8,12,256]{2,1,0:T(8,128)S(1)} all-gather(s32[1,12,256]{2,1,0:T(8,128)} %bitcast.42), channel_id=2, replica_groups=mesh['fsdp'=8] {'fsdp'}, dimensions={0}, use_global_device_ids=true | all-gather | bytes 110592 | tf_op jit(solution)/shard_map/all_gather | solution.py:452
  26.6 0.7 broadcast_multiply_fusion
  27.4 0.7 slice_bitcast_fusion
  28.1 65.5 %gather_rows.1 = (bf16[8192,576]{1,0:T(8,128)(2,1)}, bf16[8192,576]{1,0:T(8,128)(2,1)}, bf16[8192,576]{1,0:T(8,128)(2,1)}) custom-call(s32[24576]{0:T(1024)S(1)} %pad_add_fusion.ids_ref, bf16[576,6144]{1,0:T(8,128)(2,1)} %bitcast.50), custom_call_target="tpu_custom_call" | custom-call | flops 40000000000 | bytes 40000000 | tf_op jit(solution)/shard_map/gather_rows/pallas_call | solution.py:284
  93.6 0.0 reduce-scatter.12.cloned.1.call-update
  93.6 0.0 reduce-scatter.10.cloned.1.call-start
  93.7 0.5 reduce-scatter.10.cloned.1.call-update
  94.2 0.0 reduce-scatter.8.cloned.1.call-start
  94.2 0.0 copy-start
  94.2 0.5 reduce-scatter.8.cloned.1.call-update
  94.8 0.0 reduce-scatter.16.cloned.1.call-start
  94.8 1.7 convert_element_type.22
  96.5 0.6 convert_element_type.23
  97.1 0.0 copy-done
  97.1 3.9 copy.75
  101.0 0.7 maximum_convert_fusion
  101.7 0.1 fusion.6
  101.8 0.6 pad_maximum_fusion.1.refs_6_
  102.4 5.8 multiply_cosine_fusion
  108.2 2.5 pad_maximum_fusion.refs_2_
  110.6 0.9 slice_convert_fusion
  111.6 0.7 copy.92
  112.3 54.2 %reduce-scatter.12.cloned.1.call-done.refs_0_ = bf16[1024,576]{1,0:T(8,128)(2,1)} async-done(((bf16[8192,576]{1,0:T(8,128)(2,1)}), bf16[1024,576]{1,0:T(8,128)(2,1)}) %reduce-scatter.12.cloned.1.call-update) | async-done | bytes 1179664 | tf_op jit(solution)/shard_map/reduce_scatter | solution.py:482
  166.5 92.8 %layer_chunk.3 = (bf16[3072,576]{1,0:T(8,128)(2,1)}, f32[5120,128]{1,0:T(8,128)}, f32[576,4992]{1,0:T(8,128)}, f32[576,1536]{1,0:T(8,128)}) custom-call(bf16[1024,576]{1,0:T(8,128)(2,1)} %reduce-scatter.12.cloned.1.call-done.refs_0_, bf16[3072,576]{1,0:T(8,128)(2,1)} %bitcast.35, f32[3072,128]{1,0:T(8,128)} %pad_maximum_fusion.refs_2_, ...), custom_call_target="tpu_custom_call" | custom-call | flops 24000000000 | bytes 55000000 | tf_op jit(solution)/shard_map/layer_chunk/pallas_call | solution.py:414
  259.3 0.0 reduce-scatter.10.cloned.1.call-done.refs_0_
  259.4 94.2 %layer_chunk.4 = (bf16[3072,576]{1,0:T(8,128)(2,1)}, f32[5120,128]{1,0:T(8,128)}, f32[576,4992]{1,0:T(8,128)}, f32[576,1536]{1,0:T(8,128)}) custom-call(bf16[1024,576]{1,0:T(8,128)(2,1)} %reduce-scatter.10.cloned.1.call-done.refs_0_, bf16[3072,576]{1,0:T(8,128)(2,1)} %bitcast.36, ...), custom_call_target="tpu_custom_call", output_to_operand_aliasing={{2}: (7, {}), {3}: (8, {}), {0}: (9, {})} | custom-call | flops 24000000000 | bytes 55000000 | tf_op jit(solution)/shard_map/layer_chunk/pallas_call | solution.py:414
  353.6 0.0 reduce-scatter.8.cloned.1.call-done.refs_0_
  353.6 110.2 %layer_chunk.5 = (bf16[3072,576]{1,0:T(8,128)(2,1)}, f32[5120,128]{1,0:T(8,128)}, f32[576,4992]{1,0:T(8,128)}, f32[1536,576]{1,0:T(8,128)}) custom-call(bf16[1024,576]{1,0:T(8,128)(2,1)} %reduce-scatter.8.cloned.1.call-done.refs_0_, bf16[3072,576]{1,0:T(8,128)(2,1)} %bitcast.37, ...), custom_call_target="tpu_custom_call", output_to_operand_aliasing={{2}: (7, {}), {0}: (9, {})} | custom-call | flops 24000000000 | bytes 55000000 | tf_op jit(solution)/shard_map/layer_chunk/pallas_call | solution.py:414
  463.8 0.0 reduce-scatter.16.cloned.1.call-update
  463.8 0.0 all-gather.16.cloned.1.call-start
  463.9 0.7 all-gather.16.cloned.1.call-update
  464.6 0.0 all-gather.14.cloned.1.call-start
  464.7 0.6 all-gather.14.cloned.1.call-update
  465.3 0.0 all-gather.12.cloned.1.call-start
  465.4 0.7 all-gather.12.cloned.1.call-update
  466.1 0.0 reduce-scatter.14.cloned.1.call-start
  466.2 0.3 reshape.106
  466.5 32.3 %and_reduce_fusion = pred[8,12,16]{2,1,0:T(8,128)(4,1)S(1)} fusion(s32[8,12,16,16]{3,2,1,0:T(8,128)S(1)} %reshape.106, pred[16,16]{1,0:T(8,128)(4,1)S(1)} %iota_compare_fusion), kind=kLoop, calls=%fused_computation | loop fusion | flops 1178112 | bytes 100096 | tf_op jit(solution)/shard_map/reduce_or | solution.py:478
  498.9 0.1 reshape.97.clash_ref
  498.9 0.1 reshape.95.clash_ref
  499.0 0.1 reshape.93.clash_ref
  499.1 6.3 copy.83
  505.4 0.0 reduce-scatter.14.cloned.1.call-update
  505.4 37.0 %reduce-scatter.16.cloned.1.call-done = f32[72,4992]{1,0:T(8,128)} async-done(((f32[576,4992]{1,0:T(8,128)}), f32[72,4992]{1,0:T(8,128)}) %reduce-scatter.16.cloned.1.call-update) | async-done | bytes 1437712
  542.4 1.5 slice_reduce_fusion
  544.0 1.3 slice_bitcast_fusion.6
  545.3 1.7 fusion.4
  547.0 1.9 fusion.3
  548.9 2.3 fusion.2
  551.2 95.0 %all-gather.16.cloned.1.call-done.rows_ref = f32[40960,128]{1,0:T(8,128)} async-done(((f32[5120,128]{1,0:T(8,128)}), f32[40960,128]{1,0:T(8,128)}) %all-gather.16.cloned.1.call-update) | async-done | bytes 20971536 | tf_op jit(solution)/shard_map/all_gather | solution.py:488
  646.2 33.9 %scatter_rows.3.refs_0_ = f32[30800,128]{1,0:T(8,128)} custom-call(s32[8192]{0:T(1024)S(1)} %bitcast.34, s32[512]{0:T(512)S(1)} %reshape.97.clash_ref, f32[40960,128]{1,0:T(8,128)} %all-gather.16.cloned.1.call-done.rows_ref), custom_call_target="tpu_custom_call" | custom-call | flops 20000000000 | bytes 60000000 | tf_op jit(solution)/shard_map/scatter_rows/pallas_call | solution.py:378
  680.1 69.8 %all-gather.14.cloned.1.call-done.rows_ref = f32[40960,128]{1,0:T(8,128)} async-done(((f32[5120,128]{1,0:T(8,128)}), f32[40960,128]{1,0:T(8,128)}) %all-gather.14.cloned.1.call-update) | async-done | bytes 20971536 | tf_op jit(solution)/shard_map/all_gather | solution.py:488
  749.9 40.0 %scatter_rows.4.refs_0_ = f32[30800,128]{1,0:T(8,128)} custom-call(s32[8192]{0:T(1024)S(1)} %bitcast.33, s32[512]{0:T(512)S(1)} %reshape.95.clash_ref, f32[40960,128]{1,0:T(8,128)} %all-gather.14.cloned.1.call-done.rows_ref, f32[30800,128]{1,0:T(8,128)} %scatter_rows.3.refs_0_), custom_call_target="tpu_custom_call", output_to_operand_aliasing={{}: (3, {})} | custom-call | flops 20000000000 | bytes 60000000 | tf_op jit(solution)/shard_map/scatter_rows/pallas_call | solution.py:378
  789.9 63.8 %all-gather.12.cloned.1.call-done.rows_ref = f32[40960,128]{1,0:T(8,128)} async-done(((f32[5120,128]{1,0:T(8,128)}), f32[40960,128]{1,0:T(8,128)}) %all-gather.12.cloned.1.call-update) | async-done | bytes 20971536 | tf_op jit(solution)/shard_map/all_gather | solution.py:488
  853.7 74.7 %scatter_rows.5 = f32[576,6144]{1,0:T(8,128)} custom-call(s32[8192]{0:T(1024)S(1)} %bitcast.32, s32[512]{0:T(512)S(1)} %reshape.93.clash_ref, f32[40960,128]{1,0:T(8,128)} %all-gather.12.cloned.1.call-done.rows_ref, f32[30800,128]{1,0:T(8,128)} %scatter_rows.4.refs_0_), custom_call_target="tpu_custom_call" | custom-call | flops 20000000000 | bytes 60000000 | tf_op jit(solution)/shard_map/scatter_rows/pallas_call | solution.py:378
  928.3 0.0 reduce-scatter.14.cloned.1.call-done
  (30 shorter events, 0.2 us)
Async XLA Ops:
  7.2 103.5 %all-gather.8.cloned.1.call-start = ((), (), s32[]{:S(2)}) async-start(), calls=%async_computation.6 | async-start | bytes 6303744 | tf_op jit(solution)/shard_map/all_gather | solution.py:456
  10.9 101.4 %all-gather.10.cloned.1.call-start = ((), (), s32[]{:S(2)}) async-start(), calls=%async_computation.7 | async-start | bytes 2211840 | tf_op jit(solution)/shard_map/all_gather | solution.py:457
  11.7 154.9 %reduce-scatter.12.cloned.1.call-start = ((), (), s32[]{:S(2)}) async-start(), calls=%async_computation.9 | async-start | bytes 11796480 | tf_op jit(solution)/shard_map/reduce_scatter | solution.py:482
  93.6 165.8 %reduce-scatter.10.cloned.1.call-start = ((), (), s32[]{:S(2)}) async-start(), calls=%async_computation.8 | async-start | bytes 11796480 | tf_op jit(solution)/shard_map/reduce_scatter | solution.py:482
  94.2 259.4 %reduce-scatter.8.cloned.1.call-start = ((), (), s32[]{:S(2)}) async-start(), calls=%async_computation.5 | async-start | bytes 11796480 | tf_op jit(solution)/shard_map/reduce_scatter | solution.py:482
  94.2 2.9 copy-start
  94.8 447.7 %reduce-scatter.16.cloned.1.call-start = ((), (), s32[]{:S(2)}) async-start(), calls=%async_computation.14 | async-start | bytes 12939264
  97.1 3.9 copy-start.6
  97.1 5.3 copy-start.5
  463.8 182.3 %all-gather.16.cloned.1.call-start = ((), (), s32[]{:S(2)}) async-start(), calls=%async_computation.12 | async-start | bytes 23592960 | tf_op jit(solution)/shard_map/all_gather | solution.py:488
  464.6 285.3 %all-gather.14.cloned.1.call-start = ((), (), s32[]{:S(2)}) async-start(), calls=%async_computation.11 | async-start | bytes 23592960 | tf_op jit(solution)/shard_map/all_gather | solution.py:488
  464.6 1.5 copy-start.4
  464.6 1.5 copy-start.3
  464.6 1.5 copy-start.2
  464.7 1.6 copy-start.1
  465.3 388.3 %all-gather.12.cloned.1.call-start = ((), (), s32[]{:S(2)}) async-start(), calls=%async_computation.10 | async-start | bytes 23592960 | tf_op jit(solution)/shard_map/all_gather | solution.py:488
  466.1 462.3 %reduce-scatter.14.cloned.1.call-start = ((), (), s32[]{:S(2)}) async-start(), calls=%async_computation.13 | async-start | bytes 4423680 | tf_op jit(solution)/shard_map/reduce_scatter | solution.py:495
Sparse Core Ops, SparseCore 0:
  11.0 40.1 all-gather.7
  53.0 21.6 all-gather.9
  93.7 72.7 reduce-scatter.11
  169.8 73.6 reduce-scatter.9
  246.8 73.6 reduce-scatter.7
  463.9 78.4 reduce-scatter.15
  544.2 101.8 all-gather.15
  648.0 101.8 all-gather.13
  751.7 101.8 all-gather.11
  857.5 41.4 reduce-scatter.13
where the time goes:
time: 941 us; the launch traced here: 935 us
  Pallas kernels  511 us (54%)
  waiting for transfers between devices  324 us (34%)
  other arithmetic  45.2 us (5%)
  local copies, waits for them, and re-layouts  25.3 us (3%)
  blocking collectives  14.9 us (2%)
  between operations  14.7 us (2%)
    pallas_call x3, Pallas kernels, layer_chunk(): pl.pallas_call(functools.partial(layer_kernel, first, last, steps), grid=...  297 us
    all_gather x3, waiting for transfers between devices, device_step(): rows_of.append(lax.all_gather(dx, AXIS_NAME, tiled=True))  229 us
    pallas_call x3, Pallas kernels, scatter_rows(): pl.pallas_call(functools.partial(scatter_kernel, first, last, blocks), gr...  149 us
    pallas_call x1, Pallas kernels, gather_rows(): pl.pallas_call(functools.partial(gather_kernel, blocks), grid_spec=pltpu....  65.5 us
    reduce_scatter x3, waiting for transfers between devices, device_step(): lax.psum_scatter(rows, AXIS_NAME, scatter_dimension=0, tiled=True)  54.3 us
    unnamed x11, waiting for transfers between devices  40.8 us
    reduce_or x1, other arithmetic, device_step(): clashes = by_chunk(jnp.any(pairs, axis=(-1, -2)).astype(jnp.int32))  32.3 us
  transfers between devices with their start and end apart: 10, of which 5 were waited for; matrix products, arithmetic and copies ran while one was open for 7% of the time, Pallas kernels for 43%

commit v1 on v0

v1 whole, which is shorter than its diff:
```python
import functools
import math
import jax
import jax.numpy as jnp
from jax import lax
from jax.experimental import pallas as pl
from jax.experimental.pallas import tpu as pltpu
from jax.sharding import PartitionSpec as P

NORM_EPS = 1e-6
ROPE_THETA = 1.0e6
AXIS_NAME = 'fsdp'
SEQ = 256
HALF_SEQ = SEQ // 2
LANES = 128
D = 576
FF = 1536
HEAD = 64
HEADS = 9
KV = 3
GRP = 3
C_OUT, C_GATE, C_UP, C_NORM, C_HEAD = 1024, 1664, 3200, 4736, 4864
W_COLS, G_COLS = 4864, 4992
X_K, X_V, X_COLS = HEADS * LANES, (HEADS + KV) * LANES, (HEADS + 2 * KV) * LANES
FF_STEP = 512
CHUNKS = (4, 4, 4)
PAIR_WORDS = 9
BF, F32 = jnp.bfloat16, jnp.float32


def mm(lhs, rhs, lhs_dim=1, rhs_dim=0):
    return lax.dot_general(lhs, rhs, (((lhs_dim,), (rhs_dim,)), ((), ())), preferred_element_type=F32)


def fold8(values):
    return jnp.sum(values.reshape(values.shape[0] // 8, 8, values.shape[1]), axis=0)


def norm_bwd(grad_out, normed, inv_rms, norm_gain):
    grad_normed = grad_out * norm_gain
    return inv_rms * (grad_normed - normed * jnp.mean(grad_normed * normed, axis=-1, keepdims=True))


def head_norm_rope(head_ext, gain_ext, cs):
    head_f = head_ext.astype(F32)
    inv = lax.rsqrt(jnp.sum(head_f * head_f, axis=-1, keepdims=True) * (1.0 / LANES) + NORM_EPS)
    turned = head_f * inv * gain_ext * cs
    return turned + pltpu.roll(turned, 64, 1), inv


def head_norm_rope_bwd(grad_ext, head_ext, inv, gain_low, cs_bwd, low):
    turned = grad_ext * cs_bwd
    grad_t = turned + pltpu.roll(turned, 64, 1)
    normed = jnp.where(low, head_ext.astype(F32), 0.0) * inv
    grad_normed = grad_t * gain_low
    mean_term = jnp.sum(grad_normed * normed, axis=-1, keepdims=True) * (1.0 / HEAD)
    return inv * (grad_normed - normed * mean_term), fold8(grad_t * normed)


def pack_pairs(heads):
    tiles = []
    for idx in range(0, len(heads), 2):
        tile = heads[idx]
        if idx + 1 < len(heads):
            tile = tile + pltpu.roll(heads[idx + 1], 64, 1)
        tiles.append(tile.astype(BF))
    return tiles


def layer_kernel(first, last, steps, *refs):
    (x_ref, dy_ref, cs_ref, w_ref, wd_ref, gains_ref, head_gains_ref, core_ref) = refs[:8]
    refs = refs[8:]
    if not first:
        acc_in, accd_in, _ = refs[:3]
        refs = refs[3:]
    y_ref, dx_ref = refs[:2]
    outs = refs[2:6] if last else refs[2:4]
    (acc, accd, norm_acc, head_acc, wx, wox, qkv_s, probs_s, tbuf, sems) = refs[2 + len(outs):]
    step = pl.program_id(0)
    low = lax.broadcasted_iota(jnp.int32, (1, LANES), 1) < 64

    @pl.when(step == 0)
    def _():
        if first:
            acc[...] = jnp.zeros_like(acc)
            accd[...] = jnp.zeros_like(accd)
        else:
            load_acc = pltpu.make_async_copy(acc_in, acc, sems.at[0])
            load_accd = pltpu.make_async_copy(accd_in, accd, sems.at[1])
            load_acc.start()
            load_accd.start()
        norm_acc[...] = jnp.zeros_like(norm_acc)
        head_acc[...] = jnp.zeros_like(head_acc)
        for h in range(HEADS + 2 * KV):
            tile = w_ref[:, (h // 2) * LANES:(h // 2) * LANES + LANES].astype(F32)
            moved = pltpu.roll(tile, 64, 1)
            if h >= HEADS + KV:
                both = jnp.where(low, moved if h % 2 else tile, 0.0)
            else:
                twice = jnp.where(low, moved, tile) if h % 2 else jnp.where(low, tile, moved)
                both = jnp.where(low, twice, pltpu.roll(twice, 32, 1))
            wx[:, h * LANES:h * LANES + LANES] = both.astype(BF)
        for h in range(HEADS):
            wox[h * LANES:h * LANES + 64, :] = w_ref[h * 64:h * 64 + 64, C_OUT:C_OUT + D]
            wox[h * LANES + 64:h * LANES + LANES, :] = jnp.zeros((64, D), BF)
        if not first:
            load_acc.wait()
            load_accd.wait()

    gain1 = gains_ref[0:1, :]
    gain2 = gains_ref[1:2, :]
    gain_q, gain_k = head_gains_ref[0:1, :], head_gains_ref[1:2, :]
    low_q, low_k = jnp.where(low, gain_q, 0.0), jnp.where(low, gain_k, 0.0)
    cs = cs_ref[...]
    cs_bwd = jnp.where(low, cs, -cs)
    causal = ((lax.broadcasted_iota(jnp.int32, (GRP * SEQ, SEQ), 0) & (SEQ - 1))
              >= lax.broadcasted_iota(jnp.int32, (GRP * SEQ, SEQ), 1))

    pairs = x_ref[...].astype(F32)
    tails = pairs[:, 512:640]
    x = jnp.concatenate([
        jnp.concatenate([pairs[:, :512], tails[:, :64]], axis=1),
        jnp.concatenate([pairs[:, 640:], pltpu.roll(tails, 64, 1)[:, :64]], axis=1)], axis=0)
    inv1 = lax.rsqrt(jnp.mean(x * x, axis=-1, keepdims=True) + NORM_EPS)
    m1 = (x * inv1 * gain1).astype(BF)
    qkv_s[...] = mm(m1, wx[...]).astype(BF)
    saved = []
    heads = []
    for g in range(KV):
        ke = qkv_s[:, X_K + g * LANES:X_K + g * LANES + LANES]
        v0 = qkv_s[:, X_V + g * LANES:X_V + g * LANES + LANES]
        k_rot, k_inv = head_norm_rope(ke, gain_k, cs)
        k0 = jnp.where(low, k_rot, 0.0).astype(BF)
        k_swap = jnp.where(low, k_rot, pltpu.roll(k_rot, 32, 1)).astype(BF)
        qs, q_swaps, q_invs = [], [], []
        for r in range(GRP):
            h = g * GRP + r
            q_rot, q_inv = head_norm_rope(qkv_s[:, h * LANES:h * LANES + LANES], gain_q, cs)
            qs.append(q_rot.astype(BF))
            q_swaps.append(jnp.where(low, q_rot, pltpu.roll(q_rot, 32, 1)).astype(BF))
            q_invs.append(q_inv)
        scores = mm(jnp.concatenate(qs, axis=0), k0, 1, 1) * (HEAD ** -0.5)
        scores = jnp.where(causal, scores, -1e30)
        expd = jnp.exp(scores - jnp.max(scores, axis=-1, keepdims=True))
        probs = expd / jnp.sum(expd, axis=-1, keepdims=True)
        probs_s[g] = probs
        o = mm(probs.astype(BF), v0)
        for r in range(GRP):
            heads.append(o[r * SEQ:(r + 1) * SEQ])
        saved.append((k_swap, jnp.concatenate(q_swaps, axis=0), q_invs, k_inv))
    attn = jnp.concatenate(pack_pairs(heads), axis=1)
    hidden_b = (x + mm(attn[:, :D], w_ref[:, C_OUT:C_OUT + D])).astype(BF)
    hidden = hidden_b.astype(F32)
    inv2 = lax.rsqrt(jnp.mean(hidden * hidden, axis=-1, keepdims=True) + NORM_EPS)
    m2 = (hidden * inv2 * gain2).astype(BF)

    dy = dy_ref[...]
    m2_t = m2.T
    dy_t = dy.T
    y = hidden
    dm2 = jnp.zeros((SEQ, D), F32)
    for f in range(0, FF, FF_STEP):
        wg = w_ref[:, C_GATE + f:C_GATE + f + FF_STEP]
        wu = w_ref[:, C_UP + f:C_UP + f + FF_STEP]
        wd = wd_ref[f:f + FF_STEP, :]
        gate = mm(m2, wg)
        up = mm(m2, wu)
        dact = mm(dy, wd, 1, 1)
        sig = 1.0 / (1.0 + jnp.exp(-gate))
        silu = gate * sig
        act = (silu * up).astype(BF)
        y = y + mm(act, wd)
        dgate = (dact * up * sig * (1.0 + gate * (1.0 - sig))).astype(BF)
        dup = (dact * silu).astype(BF)
        dm2 = dm2 + mm(dgate, wg, 1, 1) + mm(dup, wu, 1, 1)
        acc[:, C_GATE + f:C_GATE + f + FF_STEP] += mm(m2_t, dgate)
        acc[:, C_UP + f:C_UP + f + FF_STEP] += mm(m2_t, dup)
        accd[:, f:f + FF_STEP] += mm(dy_t, act)
    y_ref[...] = y.astype(BF)
    n2 = hidden * inv2
    norm_acc[1] += fold8(dm2 * n2)
    dh = dy.astype(F32) + norm_bwd(dm2, n2, inv2, gain2)
    dh_b = dh.astype(BF)
    acc[:, C_OUT:C_OUT + D] += mm(attn.T, dh_b)[:D]

    do = mm(dh_b, wox[...], 1, 1).astype(BF)
    dqs, dks, dvs = [], [], []
    for g in range(KV):
        k_swap, q_swap, q_invs, k_inv = saved[g]
        v0 = qkv_s[:, X_V + g * LANES:X_V + g * LANES + LANES]
        do_g = jnp.concatenate([do[:, h * LANES:h * LANES + LANES] for h in range(g * GRP, (g + 1) * GRP)], axis=0)
        probs = probs_s[g]
        dprobs = mm(do_g, v0, 1, 1)
        dvs.append(mm(do_g.T, probs.astype(BF)).T)
        dscores = probs * (dprobs - jnp.sum(dprobs * probs, axis=-1, keepdims=True)) * (HEAD ** -0.5)
        dscores = dscores.astype(BF)
        dq = mm(dscores, k_swap)
        dk = mm(q_swap.T, dscores).T
        dk, dk_gain = head_norm_rope_bwd(dk, qkv_s[:, X_K + g * LANES:X_K + g * LANES + LANES], k_inv, low_k, cs_bwd, low)
        dks.append(dk)
        head_acc[1] += dk_gain
        for r in range(GRP):
            h = g * GRP + r
            dq_h, dq_gain = head_norm_rope_bwd(dq[r * SEQ:(r + 1) * SEQ], qkv_s[:, h * LANES:h * LANES + LANES], q_invs[r], low_q, cs_bwd, low)
            dqs.append(dq_h)
            head_acc[0] += dq_gain
    dqkv = jnp.concatenate(pack_pairs(dqs + dks + dvs), axis=1)
    acc[:, 0:1024] += mm(m1.T, dqkv)
    dm1 = mm(dqkv, w_ref[:, 0:1024], 1, 1)
    n1 = x * inv1
    norm_acc[0] += fold8(dm1 * n1)
    dx = dh + norm_bwd(dm1, n1, inv1, gain1)
    upper, lower = dx[:HALF_SEQ], dx[HALF_SEQ:]
    for j in range(4):
        dx_ref[pl.ds(j, HALF_SEQ, stride=PAIR_WORDS), :] = upper[:, j * LANES:j * LANES + LANES]
        dx_ref[pl.ds(5 + j, HALF_SEQ, stride=PAIR_WORDS), :] = lower[:, j * LANES:j * LANES + LANES]
    dx_ref[pl.ds(4, HALF_SEQ, stride=PAIR_WORDS), :] = jnp.concatenate([upper[:, 512:], lower[:, 512:]], axis=1)

    @pl.when(step == steps - 1)
    def _():
        top = lax.broadcasted_iota(jnp.int32, (LANES, 1), 0)
        rows1 = jnp.sum(norm_acc[0], axis=0, keepdims=True)
        rows2 = jnp.sum(norm_acc[1], axis=0, keepdims=True)
        both = jnp.where(top == 0, rows1, 0.0) + jnp.where(top == 1, rows2, 0.0)
        for c in range(0, D, LANES):
            width = min(LANES, D - c)
            acc[c:c + width, C_NORM:C_NORM + LANES] += both[:, c:c + width].T
        head_q = jnp.sum(head_acc[0], axis=0, keepdims=True)
        head_k = jnp.sum(head_acc[1], axis=0, keepdims=True)
        head_row = jnp.where(low, head_q, pltpu.roll(head_k, 64, 1))
        acc[:, C_HEAD:C_HEAD + LANES] += jnp.broadcast_to(head_row, (D, LANES))
        if last:
            mine = core_ref[0]
            for f in range(0, FF, 192):
                for t in range(0, D, LANES):
                    width = min(LANES, D - t)
                    tbuf[f:f + 192, t:t + width] = accd[t:t + width, f:f + 192].T
            stores = []
            for d in range(8):
                for src, keep, send in ((acc.at[pl.ds(d * 72, 72), :], outs[0], outs[1]), (tbuf.at[pl.ds(d * 192, 192), :], outs[2], outs[3])):
                    stores.append(pltpu.make_async_copy(src, keep.at[d // 2], sems.at[0]))

                    @pl.when(mine == d % 2)
                    def _():
                        stores[-1].start()

                    @pl.when(mine != d % 2)
                    def _():
                        pltpu.make_async_copy(src, send.at[d // 2], sems.at[0]).start()
        else:
            stores = [pltpu.make_async_copy(acc, outs[0], sems.at[0]), pltpu.make_async_copy(accd, outs[1], sems.at[0])]
            for store in stores:
                store.start()
        for store in stores:
            store.wait()


ROW_WORDS = 5
ACC_WORDS = 6
GROUP_ROWS = 16
PAD_ROWS = 16


def gather_kernel(blocks, ids_ref, tab_ref, *refs):
    outs, (lin, buf) = refs[:-2], refs[-2:]
    step = pl.program_id(0)
    rows = tab_ref.shape[1]

    @pl.when(step == 0)
    def _():
        def build(b, _):
            at = pl.multiple_of(b * LANES, LANES)
            for j in range(ROW_WORDS):
                part = tab_ref[j * LANES:min(j * LANES + LANES, D), pl.ds(at, LANES)].astype(F32)
                if part.shape[0] < LANES:
                    part = jnp.concatenate([part, jnp.zeros((LANES - part.shape[0], LANES), F32)], axis=0)
                lin[pl.ds(at * ROW_WORDS + j, LANES, stride=ROW_WORDS), :] = part.T
            return 0

        lax.fori_loop(0, rows // LANES, build, 0)
        lin[rows * ROW_WORDS:(rows + PAD_ROWS) * ROW_WORDS, :] = jnp.zeros((PAD_ROWS * ROW_WORDS, LANES), F32)

    def pick(k, _):
        base = k * GROUP_ROWS
        got = [lin[pl.ds(ids_ref[step * SEQ + base + u], ROW_WORDS), :] for u in range(GROUP_ROWS)]
        for u in range(GROUP_ROWS):
            buf[pl.ds((base + u) * ROW_WORDS, ROW_WORDS), :] = got[u]
        return 0

    lax.fori_loop(0, SEQ // GROUP_ROWS, pick, 0)
    first = 0
    half = HALF_SEQ * ROW_WORDS
    for out, count in zip(outs, blocks):
        @pl.when((step >= first) & (step < first + count))
        def _():
            for j in range(4):
                out[:, j * LANES:j * LANES + LANES] = buf[pl.ds(j, HALF_SEQ, stride=ROW_WORDS), :].astype(BF)
                out[:, 640 + j * LANES:768 + j * LANES] = buf[pl.ds(half + j, HALF_SEQ, stride=ROW_WORDS), :].astype(BF)
            tails = buf[pl.ds(4, HALF_SEQ, stride=ROW_WORDS), :] + pltpu.roll(buf[pl.ds(half + 4, HALF_SEQ, stride=ROW_WORDS), :], 64, 1)
            out[:, 512:640] = tails.astype(BF)

        first += count


def gather_rows(ids, table_t, blocks):
    starts = [sum(blocks[:c]) for c in range(len(blocks))]
    rows = table_t.shape[1]
    out_spec = lambda c: pl.BlockSpec((HALF_SEQ, 2 * D), lambda i, ids: (jnp.clip(i - starts[c], 0, blocks[c] - 1), 0))
    return pl.pallas_call(
        functools.partial(gather_kernel, blocks),
        grid_spec=pltpu.PrefetchScalarGridSpec(
            num_scalar_prefetch=1,
            grid=(sum(blocks),),
            in_specs=[pl.BlockSpec(table_t.shape, lambda i, ids: (0, 0), pipeline_mode=pl.Buffered(1))],
            out_specs=[out_spec(c) for c in range(len(blocks))],
            scratch_shapes=[pltpu.VMEM(((rows + PAD_ROWS) * ROW_WORDS, LANES), F32), pltpu.VMEM((SEQ * ROW_WORDS, LANES), F32)],
        ),
        out_shape=[jax.ShapeDtypeStruct((count * HALF_SEQ, 2 * D), BF) for count in blocks],
        compiler_params=pltpu.CompilerParams(dimension_semantics=('arbitrary',), vmem_limit_bytes=48 << 20),
        cost_estimate=pl.CostEstimate(flops=40_000_000_000, bytes_accessed=40_000_000, transcendentals=0),
        name='gather_rows',
    )(ids, table_t)


def scatter_kernel(first, last, blocks, ids_ref, clash_ref, rows_ref, *refs):
    if not first:
        acc_in, refs = refs[0], refs[1:]
    out_ref, acc, sem = refs[:3]
    tbuf = refs[3] if last else None
    step = pl.program_id(0)
    rows = acc.shape[0] // ACC_WORDS - PAD_ROWS

    @pl.when(step == 0)
    def _():
        if first:
            acc[...] = jnp.zeros_like(acc)
        else:
            load = pltpu.make_async_copy(acc_in, acc, sem.at[0])
            load.start()
            load.wait()

    groups = SCATTER_ROWS // GROUP_ROWS

    def add(k, _):
        spots = [pl.ds(ids_ref[step * SCATTER_ROWS + u * LANES + k], ROW_WORDS) for u in range(GROUP_ROWS)]
        from_row = lambda u: rows_ref[pl.ds((u // 2 * LANES + k) * PAIR_WORDS + (u % 2) * 4, ROW_WORDS), :]
        clash = clash_ref[step * groups + k]

        @pl.when(clash == 0)
        def _():
            sums = [acc[spots[u], :] + from_row(u) for u in range(GROUP_ROWS)]
            for u in range(GROUP_ROWS):
                acc[spots[u], :] = sums[u]

        @pl.when(clash != 0)
        def _():
            for u in range(GROUP_ROWS):
                acc[spots[u], :] += from_row(u)

        return 0

    lax.fori_loop(0, groups, add, 0)

    @pl.when(step == blocks - 1)
    def _():
        if last:
            wide = FLUSH_ROWS

            def flush(b, _):
                slot = lax.rem(b, 2)
                at = pl.multiple_of(b * wide, wide)
                store = pltpu.make_async_copy(tbuf.at[slot], out_ref.at[:, pl.ds(at, wide)], sem.at[slot])

                @pl.when(b >= 2)
                def _():
                    store.wait()

                word = lambda w, r: acc[pl.ds((at + r) * ACC_WORDS + w, LANES, stride=ACC_WORDS), :]
                for r in range(0, wide, LANES):
                    for j in range(4):
                        tbuf[slot, j * LANES:j * LANES + LANES, r:r + LANES] = word(1 + j, r).T
                    tail = word(5, r) + pltpu.roll(word(0, r), 64, 1)
                    tbuf[slot, 512:D, r:r + LANES] = tail.T[:64]
                store.start()
                return 0

            lax.fori_loop(0, rows // wide, flush, 0)
            for slot in range(2):
                pltpu.make_async_copy(tbuf.at[slot], out_ref.at[:, pl.ds(0, wide)], sem.at[slot]).wait()
        else:
            store = pltpu.make_async_copy(acc, out_ref, sem.at[0])
            store.start()
            store.wait()


SCATTER_ROWS = LANES * GROUP_ROWS
FLUSH_ROWS = 512


def scatter_rows(ids, clash, rows_in, table_rows, carry, last):
    first = carry is None
    blocks = rows_in.shape[0] // (SCATTER_ROWS // 2 * PAIR_WORDS)
    acc_shape = ((table_rows + PAD_ROWS) * ACC_WORDS, LANES)
    anyspec = pl.BlockSpec(memory_space=pl.ANY)
    scratch = [pltpu.VMEM(acc_shape, F32), pltpu.SemaphoreType.DMA((2,))]
    if last:
        scratch.append(pltpu.VMEM((2, D, FLUSH_ROWS), F32))
    return pl.pallas_call(
        functools.partial(scatter_kernel, first, last, blocks),
        grid_spec=pltpu.PrefetchScalarGridSpec(
            num_scalar_prefetch=2,
            grid=(blocks,),
            in_specs=[pl.BlockSpec((SCATTER_ROWS // 2 * PAIR_WORDS, LANES), lambda i, *_: (i, 0))] + ([] if first else [anyspec]),
            out_specs=anyspec,
            scratch_shapes=scratch,
        ),
        out_shape=jax.ShapeDtypeStruct((D, table_rows) if last else acc_shape, F32),
        input_output_aliases={} if first or last else {3: 0},
        compiler_params=pltpu.CompilerParams(dimension_semantics=('arbitrary',), vmem_limit_bytes=48 << 20),
        cost_estimate=pl.CostEstimate(flops=20_000_000_000, bytes_accessed=60_000_000, transcendentals=0),
        name='scatter_rows',
    )(*([ids, clash, rows_in] + ([] if first else [carry])))


def layer_chunk(x, dy, cs, w_pack, w_down, gains, head_gains, core, start, carry, last, total):
    steps = x.shape[0] // (HALF_SEQ)
    first = carry is None
    whole = lambda shape: pl.BlockSpec(shape, lambda i: (0,) * len(shape), pipeline_mode=pl.Buffered(1))
    here = lambda cols: pl.BlockSpec((SEQ, cols), lambda i: (i + start, 0))
    anyspec = pl.BlockSpec(memory_space=pl.ANY)
    in_specs = [pl.BlockSpec((HALF_SEQ, 2 * D), lambda i: (i, 0)), here(D), here(LANES), whole(w_pack.shape), whole(w_down.shape), whole(gains.shape), whole(head_gains.shape), pl.BlockSpec(memory_space=pltpu.SMEM)]
    args = [x, dy, cs, w_pack, w_down, gains, head_gains, core]
    aliases = {}
    if not first:
        in_specs += [anyspec] * 3
        args += list(carry)
        aliases = {10: 0} if last else {8: 2, 9: 3, 10: 0}
    out_shape = [
        jax.ShapeDtypeStruct((total, D), BF),
        jax.ShapeDtypeStruct((steps * HALF_SEQ * PAIR_WORDS, LANES), F32),
    ]
    grad_shapes = [(4, 72, G_COLS)] * 2 + [(4, 192, D)] * 2 if last else [(D, G_COLS), (D, FF)]
    out_shape += [jax.ShapeDtypeStruct(shape, F32) for shape in grad_shapes]
    y, dx, *grads = pl.pallas_call(
        functools.partial(layer_kernel, first, last, steps),
        grid=(steps,),
        in_specs=in_specs,
        out_specs=[here(D), pl.BlockSpec((HALF_SEQ * PAIR_WORDS, LANES), lambda i: (i, 0))] + [anyspec] * len(grad_shapes),
        out_shape=out_shape,
        scratch_shapes=[
            pltpu.VMEM((D, G_COLS), F32),
            pltpu.VMEM((D, FF), F32),
            pltpu.VMEM((2, 8, D), F32),
            pltpu.VMEM((2, 8, LANES), F32),
            pltpu.VMEM((D, X_COLS), BF),
            pltpu.VMEM((HEADS * LANES, D), BF),
            pltpu.VMEM((SEQ, X_COLS), BF),
            pltpu.VMEM((KV, GRP * SEQ, SEQ), F32),
            pltpu.VMEM((FF, D) if last else (8, LANES), F32),
            pltpu.SemaphoreType.DMA((2,)),
        ],
        input_output_aliases=aliases,
        compiler_params=pltpu.CompilerParams(dimension_semantics=('arbitrary',), vmem_limit_bytes=60 << 20),
        cost_estimate=pl.CostEstimate(flops=steps * 6_000_000_000, bytes_accessed=steps * 2_500_000 + 45_000_000, transcendentals=steps * 1_000_000),
        name='layer_chunk',
    )(*args)
    return dx, (*grads, y)


def swap_with(bit, values):
    return lax.ppermute(values, AXIS_NAME, [(i, i ^ bit) for i in range(8)])


def reduce_grads(grads):
    index = lax.axis_index(AXIS_NAME)
    x, y = (index // 2) % 2, index // 4
    parts = [(grads[i], swap_with(1, grads[i + 1])) for i in (0, 2)]
    summed = [(kept + got).reshape(2, 2, *kept.shape[1:]) for kept, got in parts]
    at = lambda values, axis, idx: lax.dynamic_index_in_dim(values, idx, axis, keepdims=False)
    results = []
    for grads in summed:
        axis, cut = (-1, 2560) if grads.shape[-1] == G_COLS else (-2, 96)
        size = grads.shape[axis]
        one, two = lax.slice_in_dim(grads, 0, cut, axis=axis), lax.slice_in_dim(grads, cut, size, axis=axis)
        one_got = swap_with(2, at(one, 1, 1 - x))
        two_got = swap_with(4, at(two, 0, 1 - y))
        results.append((at(one, 1, x), one_got, at(two, 0, y), two_got, axis))
    finals = []
    for one, one_got, two, two_got, axis in results:
        one, two = one + one_got, two + two_got
        finals.append((at(one, 0, y), swap_with(4, at(one, 0, 1 - y)), at(two, 0, x), swap_with(2, at(two, 0, 1 - x)), axis))
    return [jnp.concatenate([one + one_got, two + two_got], axis=axis) for one, one_got, two, two_got, axis in finals]


def solution(mesh):
    row_spec = P(AXIS_NAME, None)
    vec_spec = P(AXIS_NAME)
    full_spec = P(None)
    batch_spec = P(AXIS_NAME, None, None)
    weight_specs = (vec_spec, row_spec, row_spec, row_spec, full_spec, full_spec, row_spec, vec_spec, row_spec, row_spec, row_spec)

    def device_step(tokens, positions, table_shard, attn_norm, w_query, w_key, w_value, q_norm, k_norm, w_out, mlp_norm, w_gate, w_up, w_down, dy_out):
        batch_len, seq_len = tokens.shape
        devices = lax.axis_size(AXIS_NAME)
        rows_local = table_shard.shape[0]
        shard = w_query.shape[0]
        all_ids = lax.all_gather(tokens, AXIS_NAME)
        norms = jnp.concatenate([attn_norm[:, None], mlp_norm[:, None], jnp.zeros((shard, W_COLS - C_NORM - 2), BF)], axis=1)
        pad = jnp.zeros((shard, 64), BF)
        packed = jnp.concatenate([w_query, w_key, w_value, pad, w_out, pad, w_gate, w_up, norms], axis=1)
        w_pack = lax.all_gather(packed, AXIS_NAME, tiled=True)
        w_down_full = lax.all_gather(w_down, AXIS_NAME, tiled=True)
        gains = w_pack[:, C_NORM:C_NORM + 2].T.astype(F32)
        head_gains = jnp.stack([q_norm, k_norm]).astype(F32)
        swapped = jnp.concatenate([head_gains[:, 32:], head_gains[:, :32]], axis=1)
        head_gains = jnp.concatenate([head_gains, swapped], axis=1)

        inv_freq = jnp.exp(jnp.arange(HEAD // 2, dtype=F32) * (-2.0 * math.log(ROPE_THETA) / HEAD))
        angles = positions.reshape(-1, 1).astype(F32) * inv_freq
        cos_t, sin_t = jnp.cos(angles), jnp.sin(angles)
        cs = jnp.concatenate([cos_t, cos_t, -sin_t, sin_t], axis=1)
        dy = dy_out.reshape(-1, D)

        starts = [sum(CHUNKS[:c]) for c in range(len(CHUNKS))]
        take_from, add_to, clashes = [], [], []
        for first, size in zip(starts, CHUNKS):
            local_ids = all_ids[:, first:first + size].reshape(-1, LANES) - lax.axis_index(AXIS_NAME) * rows_local
            is_owner = (local_ids >= 0) & (local_ids < rows_local)
            line = lax.broadcasted_iota(jnp.int32, local_ids.shape, 0)
            take_from.append((jnp.where(is_owner, local_ids, rows_local) * ROW_WORDS).reshape(-1))
            spot = jnp.where(is_owner, local_ids, rows_local + line % GROUP_ROWS)
            add_to.append((spot * ACC_WORDS + 1 - line % 2).reshape(-1))
            groups = spot.reshape(-1, GROUP_ROWS, LANES)
            twice = jnp.concatenate([groups, groups], axis=1)
            same = [jnp.any(groups == twice[:, shift:shift + GROUP_ROWS], axis=1) for shift in range(1, GROUP_ROWS // 2 + 1)]
            clashes.append(functools.reduce(jnp.logical_or, same).astype(jnp.int32).reshape(-1))

        table_t = table_shard.T
        picked = gather_rows(take_from[0], table_t, (devices * CHUNKS[0],))
        picked += gather_rows(jnp.concatenate(take_from[1:]), table_t, tuple(devices * n for n in CHUNKS[1:]))
        xs = [lax.psum_scatter(rows, AXIS_NAME, scatter_dimension=0, tiled=True) for rows in picked]
        core = lax.rem(lax.axis_index(AXIS_NAME), 2).reshape(1)
        carry = None
        rows_of = []
        for idx in range(len(CHUNKS)):
            x_chunk = xs[idx]
            dx, carry = layer_chunk(x_chunk, dy, cs, w_pack, w_down_full, gains, head_gains, core, starts[idx], carry, idx == len(CHUNKS) - 1, batch_len * seq_len)
            rows_of.append(lax.all_gather(dx, AXIS_NAME, tiled=True))
        *grads, y = carry
        d_table = None
        for idx in range(len(CHUNKS)):
            d_table = scatter_rows(add_to[idx], clashes[idx], rows_of[idx], rows_local, d_table, idx == len(CHUNKS) - 1)
        d_table = d_table.T
        g_pack, d_w_down = reduce_grads(grads)
        kv_cols = w_key.shape[1]
        return (y.reshape(batch_len, seq_len, D), d_table, g_pack[:, C_NORM], g_pack[:, :D], g_pack[:, D:D + kv_cols], g_pack[:, D + kv_cols:D + 2 * kv_cols],
                g_pack[0, C_HEAD:C_HEAD + HEAD], g_pack[0, C_HEAD + HEAD:C_HEAD + 2 * HEAD], g_pack[:, C_OUT:C_OUT + D], g_pack[:, C_NORM + 1],
                g_pack[:, C_GATE:C_GATE + FF], g_pack[:, C_UP:C_UP + FF], d_w_down)

    return jax.shard_map(device_step, mesh=mesh, in_specs=(row_spec, row_spec, row_spec) + weight_specs + (batch_spec,), out_specs=(batch_spec, row_spec) + weight_specs, check_vma=False)
```

time: 941 us -> 793 us (0.84)
  waiting for transfers between devices: 324 us -> 198 us
  other arithmetic: 45.2 us -> 19.6 us
  starting transfers between devices: 0.39 us -> 12.8 us
    all_gather x3, waiting for transfers between devices: 229 us -> 0.04 us  [device_step(): rows_of.append(lax.all_gather(dx, AXIS_NAME, tiled=True))]
    ppermute x0 -> x10, waiting for transfers between devices: none -> 170 us  [swap_with(): return lax.ppermute(values, AXIS_NAME, [(i, i ^ bit) for i in range(8)])]
    unnamed x11 -> x8, waiting for transfers between devices: 40.8 us -> 1.32 us
    reduce_or x1 -> x3, other arithmetic: 32.3 us -> 0.27 us  [device_step(): jnp.any(groups == twice[:, shift:shift + GROUP_ROWS], axis=1)]
    reduce_scatter x3, waiting for transfers between devices: 54.3 us -> 27.1 us  [device_step(): lax.psum_scatter(rows, AXIS_NAME, scatter_dimension=0, tiled=True)]
    pallas_call x3, Pallas kernels: 149 us -> 136 us  [scatter_rows(): pl.pallas_call(functools.partial(scatter_kernel, first, last, blocks), gr...]
    ppermute x0 -> x10, starting transfers between devices: none -> 12.5 us  [swap_with(): return lax.ppermute(values, AXIS_NAME, [(i, i ^ bit) for i in range(8)])]
    pallas_call x1 -> x2, Pallas kernels: 65.5 us -> 75.1 us  [gather_rows(): pl.pallas_call(functools.partial(gather_kernel, blocks), grid_spec=pltpu....]
  transfers between devices with their start and end apart: 10 -> 18, of which waited for: 5 -> 6; matrix products, arithmetic and copies ran while one was open for 7% -> 5% of each run, Pallas kernels for 43% -> 58%
where the time goes in v1:
time: 793 us; the launch traced here: 787 us
  Pallas kernels  505 us (64%)
  waiting for transfers between devices  198 us (25%)
  local copies, waits for them, and re-layouts  21.5 us (3%)
  other arithmetic  19.6 us (2%)
  blocking collectives  14.9 us (2%)
  between operations  14.9 us (2%)
  starting transfers between devices  12.8 us (2%)
    pallas_call x3, Pallas kernels, layer_chunk(): pl.pallas_call(functools.partial(layer_kernel, first, last, steps), grid=...  294 us
    ppermute x10, waiting for transfers between devices, swap_with(): return lax.ppermute(values, AXIS_NAME, [(i, i ^ bit) for i in range(8)])  170 us
    pallas_call x3, Pallas kernels, scatter_rows(): pl.pallas_call(functools.partial(scatter_kernel, first, last, blocks), gr...  136 us
    pallas_call x2, Pallas kernels, gather_rows(): pl.pallas_call(functools.partial(gather_kernel, blocks), grid_spec=pltpu....  75.1 us
    reduce_scatter x3, waiting for transfers between devices, device_step(): lax.psum_scatter(rows, AXIS_NAME, scatter_dimension=0, tiled=True)  27.1 us
  transfers between devices with their start and end apart: 18, of which 6 were waited for; matrix products, arithmetic and copies ran while one was open for 5% of the time, Pallas kernels for 58%

profile of v1, /device:TPU:0, one launch (start us, length us, event | category | flops | bytes accessed | tf_op | source)
XLA Modules:
  0.0 786.9 jit_solution(9698635491261440393)
XLA Ops:
  7.2 0.8 copy.62
  8.0 0.8 copy.63
  8.8 2.1 concatenate.29
  11.0 0.7 all-gather.10.cloned.1.call-update
  11.8 14.9 %all-gather.1 = s32[8,12,256]{2,1,0:T(8,128)S(1)} all-gather(s32[1,12,256]{2,1,0:T(8,128)S(1)} %bitcast.100), channel_id=2, replica_groups=mesh['fsdp'=8] {'fsdp'}, dimensions={0}, use_global_device_ids=true | all-gather | bytes 110592 | tf_op jit(solution)/shard_map/all_gather | solution.py:507
  26.8 0.5 copy-done.1
  27.3 0.1 bitcast_subtract_fusion
  27.5 28.4 %gather_rows.3 = bf16[4096,1152]{1,0:T(8,128)(2,1)} custom-call(s32[8192]{0:T(1024)S(1)} %get-tuple-element.137.ids_ref, bf16[576,6144]{1,0:T(8,128)(2,1)} %bitcast.108), custom_call_target="tpu_custom_call" | custom-call | flops 40000000000 | bytes 40000000 | tf_op jit(solution)/shard_map/gather_rows/pallas_call | solution.py:309
  56.0 46.7 %gather_rows.2 = (bf16[4096,1152]{1,0:T(8,128)(2,1)}, bf16[4096,1152]{1,0:T(8,128)(2,1)}) custom-call(s32[16384]{0:T(1024)S(1)} %pad_add_fusion.ids_ref, bf16[576,6144]{1,0:T(8,128)(2,1)} %bitcast.109), custom_call_target="tpu_custom_call" | custom-call | flops 40000000000 | bytes 40000000 | tf_op jit(solution)/shard_map/gather_rows/pallas_call | solution.py:309
  102.8 0.5 reduce-scatter.4.cloned.1.call-update
  103.3 0.1 copy-done.8
  103.5 6.0 copy.60
  109.6 0.1 fusion.83
  109.7 0.6 pad_maximum_fusion.3.refs_6_
  110.3 5.8 multiply_cosine_fusion
  116.1 2.5 pad_maximum_fusion.refs_2_
  118.6 0.9 slice_convert_fusion
  119.5 0.7 copy.70
  120.3 27.1 %reduce-scatter.8.cloned.1.call-done.refs_0_ = bf16[512,1152]{1,0:T(8,128)(2,1)} async-done(((bf16[4096,1152]{1,0:T(8,128)(2,1)}), bf16[512,1152]{1,0:T(8,128)(2,1)}) %reduce-scatter.8.cloned.1.call-update) | async-done | bytes 1179664 | tf_op jit(solution)/shard_map/reduce_scatter | solution.py:541
  147.3 92.1 %layer_chunk.3 = (bf16[3072,576]{1,0:T(8,128)(2,1)}, f32[4608,128]{1,0:T(8,128)}, f32[576,4992]{1,0:T(8,128)}, f32[576,1536]{1,0:T(8,128)}) custom-call(bf16[512,1152]{1,0:T(8,128)(2,1)} %reduce-scatter.8.cloned.1.call-done.refs_0_, bf16[3072,576]{1,0:T(8,128)(2,1)} %bitcast.90, f32[3072,128]{1,0:T(8,128)} %pad_maximum_fusion.refs_2_, ...), custom_call_target="tpu_custom_call" | custom-call | flops 24000000000 | bytes 55000000 | tf_op jit(solution)/shard_map/layer_chunk/pallas_call | solution.py:444
  239.5 94.2 %layer_chunk.4 = (bf16[3072,576]{1,0:T(8,128)(2,1)}, f32[4608,128]{1,0:T(8,128)}, f32[576,4992]{1,0:T(8,128)}, f32[576,1536]{1,0:T(8,128)}) custom-call(bf16[512,1152]{1,0:T(8,128)(2,1)} %reduce-scatter.6.cloned.1.call-done.refs_0_, bf16[3072,576]{1,0:T(8,128)(2,1)} %bitcast.91, ...), custom_call_target="tpu_custom_call", output_to_operand_aliasing={{2}: (8, {}), {3}: (9, {}), {0}: (10, {})} | custom-call | flops 24000000000 | bytes 55000000 | tf_op jit(solution)/shard_map/layer_chunk/pallas_call | solution.py:444
  333.8 107.9 %layer_chunk.5 = (bf16[3072,576]{1,0:T(8,128)(2,1)}, f32[4608,128]{1,0:T(8,128)}, f32[4,72,4992]{2,1,0:T(8,128)}, f32[4,72,4992]{2,1,0:T(8,128)}, f32[4,192,576]{2,1,0:T(8,128)}, /*index=5*/f32[4,192,576]{2,1,0:T(8,128)}) custom-call(bf16[512,1152]{1,0:T(8,128)(2,1)} %reduce-scatter.4.cloned.1.call-done.refs_0_, ...), custom_call_target="tpu_custom_call", output_to_operand_aliasing={{0}: (10, {})} | custom-call | flops 24000000000 | bytes 55000000 | tf_op jit(solution)/shard_map/layer_chunk/pallas_call | solution.py:444
  441.8 0.2 collective-permute-start
  442.0 0.3 collective-permute-start.5
  442.3 0.2 copy-done.6
  442.6 0.1 fusion.52
  442.7 0.1 fusion.76
  442.8 0.1 fusion.69
  442.9 13.1 %collective-permute-done.5 = f32[4,192,576]{2,1,0:T(8,128)} collective-permute-done((f32[4,192,576]{2,1,0:T(8,128)}, f32[4,192,576]{2,1,0:T(8,128)}, u32[]{:S(2)}, u32[]{:S(2)}) %collective-permute-start.5) | collective-permute-done | bytes 1769504 | tf_op jit(solution)/shard_map/ppermute | solution.py:471
  456.0 1.7 add.173
  457.8 0.1 fusion.79
  458.0 1.8 collective-permute-start.6
  459.7 0.1 fusion.62
  459.8 6.2 copy.65
  466.1 0.9 collective-permute-start.8
  467.0 15.4 %collective-permute-done.6 = f32[2,96,576]{2,1,0:T(8,128)S(1)} collective-permute-done((f32[2,96,576]{2,1,0:T(8,128)S(1)}, f32[2,96,576]{2,1,0:T(8,128)S(1)}, u32[]{:S(2)}, u32[]{:S(2)}) %collective-permute-start.6) | collective-permute-done | bytes 442400 | tf_op jit(solution)/shard_map/ppermute | solution.py:471
  482.4 4.9 add.163
  487.4 0.2 slice.222
  487.5 0.1 dynamic-slice_bitcast_fusion.1
  487.6 1.9 collective-permute-start.1
  489.6 0.2 collective-permute-start.7
  489.7 0.1 bitcast_add_fusion.4
  489.8 1.8 collective-permute-start.9
  491.6 58.1 %collective-permute-done.7 = f32[96,576]{1,0:T(8,128)S(1)} collective-permute-done((f32[96,576]{1,0:T(8,128)S(1)}, f32[96,576]{1,0:T(8,128)S(1)}, u32[]{:S(2)}, u32[]{:S(2)}) %collective-permute-start.7) | collective-permute-done | bytes 221216 | tf_op jit(solution)/shard_map/ppermute | solution.py:471
  549.7 0.4 slice.224
  550.1 0.1 dynamic-slice_bitcast_fusion
  550.2 1.5 collective-permute-start.3
  551.7 0.8 pad_maximum_fusion.1
  552.5 0.1 bitcast_add_fusion.1
  552.8 0.6 collective-permute-start.2
  553.4 61.7 %collective-permute-done.3 = f32[2,72,2560]{2,1,0:T(8,128)S(1)} collective-permute-done((f32[2,72,2560]{2,1,0:T(8,128)S(1)}, f32[2,72,2560]{2,1,0:T(8,128)S(1)}, u32[]{:S(2)}, u32[]{:S(2)}) %collective-permute-start.3) | collective-permute-done | bytes 1474592 | tf_op jit(solution)/shard_map/ppermute | solution.py:471
  615.1 0.2 bitcast_add_fusion
  615.3 3.4 collective-permute-start.4
  618.7 21.3 %collective-permute-done.2 = f32[72,2432]{1,0:T(8,128)S(1)} collective-permute-done((f32[72,2432]{1,0:T(8,128)S(1)}, f32[72,2432]{1,0:T(8,128)S(1)}, u32[]{:S(2)}, u32[]{:S(2)}) %collective-permute-start.2) | collective-permute-done | bytes 700448 | tf_op jit(solution)/shard_map/ppermute | solution.py:471
  640.0 0.1 bitcast_add_fusion.3
  640.1 0.7 slice_reduce_fusion
  640.8 0.6 slice_bitcast_fusion
  641.4 0.1 bitcast_add_fusion.2
  641.5 0.7 fusion.81
  642.2 0.8 fusion.80
  642.9 1.0 fusion.82
  643.9 40.4 %scatter_rows.3.refs_0_ = f32[36960,128]{1,0:T(8,128)} custom-call(s32[8192]{0:T(1024)S(1)} %get-tuple-element.136.ids_ref, s32[512]{0:T(512)S(1)} %convert_bitcast_fusion.clash_ref, f32[36864,128]{1,0:T(8,128)} %all-gather.16.cloned.1.call-done.rows_ref), custom_call_target="tpu_custom_call" | custom-call | flops 20000000000 | bytes 60000000 | tf_op jit(solution)/shard_map/scatter_rows/pallas_call | solution.py:408
  684.4 46.2 %scatter_rows.4.refs_0_ = f32[36960,128]{1,0:T(8,128)} custom-call(s32[8192]{0:T(1024)S(1)} %get-tuple-element.151.ids_ref, s32[512]{0:T(512)S(1)} %convert_bitcast_fusion.1.clash_ref, f32[36864,128]{1,0:T(8,128)} %all-gather.14.cloned.1.call-done.rows_ref, f32[36960,128]{1,0:T(8,128)} %scatter_rows.3.refs_0_), custom_call_target="tpu_custom_call", output_to_operand_aliasing={{}: (3, {})} | custom-call | flops 20000000000 | bytes 60000000 | tf_op jit(solution)/shard_map/scatter_rows/pallas_call | solution.py:408
  730.6 49.2 %scatter_rows.5 = f32[576,6144]{1,0:T(8,128)} custom-call(s32[8192]{0:T(1024)S(1)} %get-tuple-element.149.ids_ref, s32[512]{0:T(512)S(1)} %convert_bitcast_fusion.2.clash_ref, f32[36864,128]{1,0:T(8,128)} %all-gather.12.cloned.1.call-done.rows_ref, f32[36960,128]{1,0:T(8,128)} %scatter_rows.4.refs_0_), custom_call_target="tpu_custom_call" | custom-call | flops 20000000000 | bytes 60000000 | tf_op jit(solution)/shard_map/scatter_rows/pallas_call | solution.py:408
  (76 shorter events, 1.2 us)
Async XLA Ops:
  7.2 4.6 copy-start.7
  7.2 111.4 %all-gather.8.cloned.1.call-start = ((), (), s32[]{:S(2)}) async-start(), calls=%async_computation.4 | async-start | bytes 6303744 | tf_op jit(solution)/shard_map/all_gather | solution.py:511
  10.9 109.3 %all-gather.10.cloned.1.call-start = ((), (), s32[]{:S(2)}) async-start(), calls=%async_computation.5 | async-start | bytes 2211840 | tf_op jit(solution)/shard_map/all_gather | solution.py:512
  11.7 135.6 %reduce-scatter.8.cloned.1.call-start = ((), (), s32[]{:S(2)}) async-start(), calls=%async_computation.7 | async-start | bytes 10616832 | tf_op jit(solution)/shard_map/reduce_scatter | solution.py:541
  26.7 0.6 copy-start.1
  26.7 0.6 copy-start.3
  26.7 0.6 copy-start.5
  55.9 183.6 %reduce-scatter.6.cloned.1.call-start = ((), (), s32[]{:S(2)}) async-start(), calls=%async_computation.6 | async-start | bytes 10616832 | tf_op jit(solution)/shard_map/reduce_scatter | solution.py:541
  102.7 231.1 %reduce-scatter.4.cloned.1.call-start = ((), (), s32[]{:S(2)}) async-start(), calls=%async_computation.3 | async-start | bytes 10616832 | tf_op jit(solution)/shard_map/reduce_scatter | solution.py:541
  102.8 0.7 copy-start.8
  103.3 540.6 %all-gather.16.cloned.1.call-start = ((), (), s32[]{:S(2)}) async-start(), calls=%async_computation.10 | async-start | bytes 21233664 | tf_op jit(solution)/shard_map/all_gather | solution.py:548
  103.5 6.1 copy-start.9
  103.5 6.1 copy-start.10
  239.4 445.0 %all-gather.14.cloned.1.call-start = ((), (), s32[]{:S(2)}) async-start(), calls=%async_computation.9 | async-start | bytes 21233664 | tf_op jit(solution)/shard_map/all_gather | solution.py:548
  333.7 396.9 %all-gather.12.cloned.1.call-start = ((), (), s32[]{:S(2)}) async-start(), calls=%async_computation.8 | async-start | bytes 21233664 | tf_op jit(solution)/shard_map/all_gather | solution.py:548
  441.7 0.8 copy-start.6
  441.7 0.8 copy-start.4
  441.7 0.8 copy-start.2
  441.8 14.3 %copy-start = (f32[4,192,576]{2,1,0:T(8,128)S(1)}, f32[4,192,576]{2,1,0:T(8,128)}, u32[]{:S(2)}) copy-start(f32[4,192,576]{2,1,0:T(8,128)} %get-tuple-element.43) | copy-start | bytes 5308420
  441.8 40.7 %collective-permute-start = (f32[4,72,4992]{2,1,0:T(8,128)}, f32[4,72,4992]{2,1,0:T(8,128)}, u32[]{:S(2)}, u32[]{:S(2)}) collective-permute-start(f32[4,72,4992]{2,1,0:T(8,128)} %get-tuple-element.42), channel_id=1, source_target_pairs={{0,1},{1,0},{2,3},{3,2},{4,5},{5,4},{6,7},{7,6}} | collective-permute-start | bytes 17252360 | tf_op jit(solution)/shard_map/ppermute | solution.py:471
  442.0 14.0 %collective-permute-start.5 = (f32[4,192,576]{2,1,0:T(8,128)}, f32[4,192,576]{2,1,0:T(8,128)}, u32[]{:S(2)}, u32[]{:S(2)}) collective-permute-start(f32[4,192,576]{2,1,0:T(8,128)} %get-tuple-element.44), channel_id=1, source_target_pairs={{0,1},{1,0},{2,3},{3,2},{4,5},{5,4},{6,7},{7,6}} | collective-permute-start | bytes 5308424 | tf_op jit(solution)/shard_map/ppermute | solution.py:471
  458.0 24.4 %collective-permute-start.6 = (f32[2,96,576]{2,1,0:T(8,128)S(1)}, f32[2,96,576]{2,1,0:T(8,128)S(1)}, u32[]{:S(2)}, u32[]{:S(2)}) collective-permute-start(f32[2,96,576]{2,1,0:T(8,128)S(1)} %dynamic-slice_bitcast_fusion.5), channel_id=1, source_target_pairs={{0,2},{1,3},{2,0},{3,1},{4,6},{5,7},{6,4},{7,5}} | collective-permute-start | bytes 1327112 | tf_op jit(solution)/shard_map/ppermute | solution.py:471
  466.1 23.7 %collective-permute-start.8 = (f32[2,96,576]{2,1,0:T(8,128)S(1)}, f32[2,96,576]{2,1,0:T(8,128)S(1)}, u32[]{:S(2)}, u32[]{:S(2)}) collective-permute-start(f32[2,96,576]{2,1,0:T(8,128)S(1)} %dynamic-slice_bitcast_fusion.4), channel_id=1, source_target_pairs={{0,4},{1,5},{2,6},{3,7},{4,0},{5,1},{6,2},{7,3}} | collective-permute-start | bytes 1327112 | tf_op jit(solution)/shard_map/ppermute | solution.py:471
  487.6 64.9 %collective-permute-start.1 = (f32[2,72,2432]{2,1,0:T(8,128)S(1)}, f32[2,72,2432]{2,1,0:T(8,128)S(1)}, u32[]{:S(2)}, u32[]{:S(2)}) collective-permute-start(f32[2,72,2432]{2,1,0:T(8,128)S(1)} %dynamic-slice_bitcast_fusion.1), channel_id=1, source_target_pairs={{0,4},{1,5},{2,6},{3,7},{4,0},{5,1},{6,2},{7,3}} | collective-permute-start | bytes 4202504 | tf_op jit(solution)/shard_map/ppermute | solution.py:471
  489.6 60.1 %collective-permute-start.7 = (f32[96,576]{1,0:T(8,128)S(1)}, f32[96,576]{1,0:T(8,128)S(1)}, u32[]{:S(2)}, u32[]{:S(2)}) collective-permute-start(f32[96,576]{1,0:T(8,128)S(1)} %dynamic-slice_bitcast_fusion.7), channel_id=1, source_target_pairs={{0,4},{1,5},{2,6},{3,7},{4,0},{5,1},{6,2},{7,3}} | collective-permute-start | bytes 663560 | tf_op jit(solution)/shard_map/ppermute | solution.py:471
  489.8 61.9 %collective-permute-start.9 = (f32[96,576]{1,0:T(8,128)S(1)}, f32[96,576]{1,0:T(8,128)S(1)}, u32[]{:S(2)}, u32[]{:S(2)}) collective-permute-start(f32[96,576]{1,0:T(8,128)S(1)} %dynamic-slice_bitcast_fusion.6), channel_id=1, source_target_pairs={{0,2},{1,3},{2,0},{3,1},{4,6},{5,7},{6,4},{7,5}} | collective-permute-start | bytes 663560 | tf_op jit(solution)/shard_map/ppermute | solution.py:471
  550.2 64.8 %collective-permute-start.3 = (f32[2,72,2560]{2,1,0:T(8,128)S(1)}, f32[2,72,2560]{2,1,0:T(8,128)S(1)}, u32[]{:S(2)}, u32[]{:S(2)}) collective-permute-start(f32[2,72,2560]{2,1,0:T(8,128)S(1)} %dynamic-slice_bitcast_fusion), channel_id=1, source_target_pairs={{0,2},{1,3},{2,0},{3,1},{4,6},{5,7},{6,4},{7,5}} | collective-permute-start | bytes 4423688 | tf_op jit(solution)/shard_map/ppermute | solution.py:471
  552.8 87.2 %collective-permute-start.2 = (f32[72,2432]{1,0:T(8,128)S(1)}, f32[72,2432]{1,0:T(8,128)S(1)}, u32[]{:S(2)}, u32[]{:S(2)}) collective-permute-start(f32[72,2432]{1,0:T(8,128)S(1)} %dynamic-slice_bitcast_fusion.3), channel_id=1, source_target_pairs={{0,2},{1,3},{2,0},{3,1},{4,6},{5,7},{6,4},{7,5}} | collective-permute-start | bytes 2101256 | tf_op jit(solution)/shard_map/ppermute | solution.py:471
  615.3 26.1 %collective-permute-start.4 = (f32[72,2560]{1,0:T(8,128)S(1)}, f32[72,2560]{1,0:T(8,128)S(1)}, u32[]{:S(2)}, u32[]{:S(2)}) collective-permute-start(f32[72,2560]{1,0:T(8,128)S(1)} %dynamic-slice_bitcast_fusion.2), channel_id=1, source_target_pairs={{0,4},{1,5},{2,6},{3,7},{4,0},{5,1},{6,2},{7,3}} | collective-permute-start | bytes 2211848 | tf_op jit(solution)/shard_map/ppermute | solution.py:471
Sparse Core Ops, SparseCore 0:
  11.0 40.1 all-gather.7
  53.0 21.6 all-gather.9
  78.8 68.4 reduce-scatter.7
  150.6 68.4 reduce-scatter.5
  222.4 68.4 reduce-scatter.3
  292.6 93.0 all-gather.15
  387.5 102.7 all-gather.13
  492.1 155.7 all-gather.11

commit v2 on v1

--- a/solution.py
+++ b/solution.py
@@ -12,6 +12,7 @@
 AXIS_NAME = 'fsdp'
 SEQ = 256
 HALF_SEQ = SEQ // 2
+SEQS = 2
 LANES = 128
 D = 576
 FF = 1536
@@ -75,7 +76,7 @@
         refs = refs[3:]
     y_ref, dx_ref = refs[:2]
     outs = refs[2:6] if last else refs[2:4]
-    (acc, accd, norm_acc, head_acc, wx, wox, qkv_s, probs_s, tbuf, sems) = refs[2 + len(outs):]
+    (acc, accd, norm_acc, head_acc, wx, wox, qkv_s, upper_s, lower_s, tbuf, sems) = refs[2 + len(outs):]
     step = pl.program_id(0)
     low = lax.broadcasted_iota(jnp.int32, (1, LANES), 1) < 64
 
@@ -111,44 +112,61 @@
     gain2 = gains_ref[1:2, :]
     gain_q, gain_k = head_gains_ref[0:1, :], head_gains_ref[1:2, :]
     low_q, low_k = jnp.where(low, gain_q, 0.0), jnp.where(low, gain_k, 0.0)
-    cs = cs_ref[...]
-    cs_bwd = jnp.where(low, cs, -cs)
-    causal = ((lax.broadcasted_iota(jnp.int32, (GRP * SEQ, SEQ), 0) & (SEQ - 1))
-              >= lax.broadcasted_iota(jnp.int32, (GRP * SEQ, SEQ), 1))
-
-    pairs = x_ref[...].astype(F32)
-    tails = pairs[:, 512:640]
-    x = jnp.concatenate([
-        jnp.concatenate([pairs[:, :512], tails[:, :64]], axis=1),
-        jnp.concatenate([pairs[:, 640:], pltpu.roll(tails, 64, 1)[:, :64]], axis=1)], axis=0)
+    scale = HEAD ** -0.5
+    stacked = GRP * HALF_SEQ
+    row = lax.broadcasted_iota(jnp.int32, (stacked, SEQ), 0) & (HALF_SEQ - 1)
+    lower_mask = lax.broadcasted_iota(jnp.int32, (stacked, SEQ), 1) - HALF_SEQ <= row
+    upper_mask = lower_mask[:, HALF_SEQ:]
+
+    def halves(tiles):
+        return jnp.concatenate([t[:HALF_SEQ] for t in tiles], axis=0), jnp.concatenate([t[HALF_SEQ:] for t in tiles], axis=0)
+
+    def joined(upper, lower, r):
+        return jnp.concatenate([part[r * HALF_SEQ:(r + 1) * HALF_SEQ] for part in (upper, lower)], axis=0)
+
+    def softmax(scores, mask):
+        scores = jnp.where(mask, scores, -1e30)
+        expd = jnp.exp(scores - jnp.max(scores, axis=-1, keepdims=True))
+        return expd * (1.0 / jnp.sum(expd, axis=-1, keepdims=True))
+
+    parts = []
+    for s in range(SEQS):
+        pairs = x_ref[s * HALF_SEQ:(s + 1) * HALF_SEQ, :].astype(F32)
+        tails = pairs[:, 512:640]
+        parts.append(jnp.concatenate([pairs[:, :512], tails[:, :64]], axis=1))
+        parts.append(jnp.concatenate([pairs[:, 640:], pltpu.roll(tails, 64, 1)[:, :64]], axis=1))
+    x = jnp.concatenate(parts, axis=0)
     inv1 = lax.rsqrt(jnp.mean(x * x, axis=-1, keepdims=True) + NORM_EPS)
     m1 = (x * inv1 * gain1).astype(BF)
     qkv_s[...] = mm(m1, wx[...]).astype(BF)
-    saved = []
-    heads = []
-    for g in range(KV):
-        ke = qkv_s[:, X_K + g * LANES:X_K + g * LANES + LANES]
-        v0 = qkv_s[:, X_V + g * LANES:X_V + g * LANES + LANES]
-        k_rot, k_inv = head_norm_rope(ke, gain_k, cs)
-        k0 = jnp.where(low, k_rot, 0.0).astype(BF)
-        k_swap = jnp.where(low, k_rot, pltpu.roll(k_rot, 32, 1)).astype(BF)
-        qs, q_swaps, q_invs = [], [], []
-        for r in range(GRP):
-            h = g * GRP + r
-            q_rot, q_inv = head_norm_rope(qkv_s[:, h * LANES:h * LANES + LANES], gain_q, cs)
-            qs.append(q_rot.astype(BF))
-            q_swaps.append(jnp.where(low, q_rot, pltpu.roll(q_rot, 32, 1)).astype(BF))
-            q_invs.append(q_inv)
-        scores = mm(jnp.concatenate(qs, axis=0), k0, 1, 1) * (HEAD ** -0.5)
-        scores = jnp.where(causal, scores, -1e30)
-        expd = jnp.exp(scores - jnp.max(scores, axis=-1, keepdims=True))
-        probs = expd / jnp.sum(expd, axis=-1, keepdims=True)
-        probs_s[g] = probs
-        o = mm(probs.astype(BF), v0)
-        for r in range(GRP):
-            heads.append(o[r * SEQ:(r + 1) * SEQ])
-        saved.append((k_swap, jnp.concatenate(q_swaps, axis=0), q_invs, k_inv))
-    attn = jnp.concatenate(pack_pairs(heads), axis=1)
+    saved, packed = [], []
+    for s in range(SEQS):
+        rows = slice(s * SEQ, (s + 1) * SEQ)
+        cs = cs_ref[rows, :]
+        heads = []
+        for g in range(KV):
+            ke = qkv_s[rows, X_K + g * LANES:X_K + (g + 1) * LANES]
+            v0 = qkv_s[rows, X_V + g * LANES:X_V + (g + 1) * LANES]
+            k_rot, k_inv = head_norm_rope(ke, gain_k, cs)
+            k0 = jnp.where(low, k_rot, 0.0).astype(BF)
+            k_swap = (jnp.where(low, k_rot, pltpu.roll(k_rot, 32, 1)) * scale).astype(BF)
+            qs, q_swaps, q_invs = [], [], []
+            for r in range(GRP):
+                h = g * GRP + r
+                q_rot, q_inv = head_norm_rope(qkv_s[rows, h * LANES:(h + 1) * LANES], gain_q, cs * scale)
+                qs.append(q_rot.astype(BF))
+                q_swaps.append(jnp.where(low, q_rot, pltpu.roll(q_rot, 32, 1)).astype(BF))
+                q_invs.append(q_inv)
+            q_upper, q_lower = halves(qs)
+            upper = softmax(mm(q_upper, k0[:HALF_SEQ], 1, 1), upper_mask)
+            lower = softmax(mm(q_lower, k0, 1, 1), lower_mask)
+            upper_s[s * KV + g] = upper
+            lower_s[s * KV + g] = lower
+            o_upper, o_lower = mm(upper.astype(BF), v0[:HALF_SEQ]), mm(lower.astype(BF), v0)
+            heads += [joined(o_upper, o_lower, r) for r in range(GRP)]
+            saved.append((k_swap, halves(q_swaps), q_invs, k_inv))
+        packed.append(jnp.concatenate(pack_pairs(heads), axis=1))
+    attn = jnp.concatenate(packed, axis=0)
     hidden_b = (x + mm(attn[:, :D], w_ref[:, C_OUT:C_OUT + D])).astype(BF)
     hidden = hidden_b.astype(F32)
     inv2 = lax.rsqrt(jnp.mean(hidden * hidden, axis=-1, keepdims=True) + NORM_EPS)
@@ -158,7 +176,7 @@
     m2_t = m2.T
     dy_t = dy.T
     y = hidden
-    dm2 = jnp.zeros((SEQ, D), F32)
+    dm2 = jnp.zeros((SEQS * SEQ, D), F32)
     for f in range(0, FF, FF_STEP):
         wg = w_ref[:, C_GATE + f:C_GATE + f + FF_STEP]
         wu = w_ref[:, C_UP + f:C_UP + f + FF_STEP]
@@ -184,37 +202,50 @@
     acc[:, C_OUT:C_OUT + D] += mm(attn.T, dh_b)[:D]
 
     do = mm(dh_b, wox[...], 1, 1).astype(BF)
-    dqs, dks, dvs = [], [], []
-    for g in range(KV):
-        k_swap, q_swap, q_invs, k_inv = saved[g]
-        v0 = qkv_s[:, X_V + g * LANES:X_V + g * LANES + LANES]
-        do_g = jnp.concatenate([do[:, h * LANES:h * LANES + LANES] for h in range(g * GRP, (g + 1) * GRP)], axis=0)
-        probs = probs_s[g]
-        dprobs = mm(do_g, v0, 1, 1)
-        dvs.append(mm(do_g.T, probs.astype(BF)).T)
-        dscores = probs * (dprobs - jnp.sum(dprobs * probs, axis=-1, keepdims=True)) * (HEAD ** -0.5)
-        dscores = dscores.astype(BF)
-        dq = mm(dscores, k_swap)
-        dk = mm(q_swap.T, dscores).T
-        dk, dk_gain = head_norm_rope_bwd(dk, qkv_s[:, X_K + g * LANES:X_K + g * LANES + LANES], k_inv, low_k, cs_bwd, low)
-        dks.append(dk)
-        head_acc[1] += dk_gain
-        for r in range(GRP):
-            h = g * GRP + r
-            dq_h, dq_gain = head_norm_rope_bwd(dq[r * SEQ:(r + 1) * SEQ], qkv_s[:, h * LANES:h * LANES + LANES], q_invs[r], low_q, cs_bwd, low)
-            dqs.append(dq_h)
-            head_acc[0] += dq_gain
-    dqkv = jnp.concatenate(pack_pairs(dqs + dks + dvs), axis=1)
+    packed = []
+    for s in range(SEQS):
+        rows = slice(s * SEQ, (s + 1) * SEQ)
+        cs = cs_ref[rows, :]
+        cs_bwd = jnp.where(low, cs, -cs)
+        dqs, dks, dvs = [], [], []
+        for g in range(KV):
+            k_swap, (swap_upper, swap_lower), q_invs, k_inv = saved[s * KV + g]
+            v0 = qkv_s[rows, X_V + g * LANES:X_V + (g + 1) * LANES]
+            do_upper, do_lower = halves([do[rows, h * LANES:(h + 1) * LANES] for h in range(g * GRP, (g + 1) * GRP)])
+            upper, lower = upper_s[s * KV + g], lower_s[s * KV + g]
+            d_upper, d_lower = mm(do_upper, v0[:HALF_SEQ], 1, 1), mm(do_lower, v0, 1, 1)
+            ds_upper = (upper * (d_upper - jnp.sum(d_upper * upper, axis=-1, keepdims=True))).astype(BF)
+            ds_lower = (lower * (d_lower - jnp.sum(d_lower * lower, axis=-1, keepdims=True))).astype(BF)
+
+            def over_queries(left_upper, left_lower, right_upper, right_lower):
+                short, full = mm(left_upper.T, right_upper), mm(left_lower.T, right_lower)
+                return jnp.concatenate([(full[:, :HALF_SEQ] + short).T, full[:, HALF_SEQ:].T], axis=0)
+
+            dvs.append(over_queries(do_upper, do_lower, upper.astype(BF), lower.astype(BF)))
+            dk = over_queries(swap_upper, swap_lower, ds_upper, ds_lower)
+            dk, dk_gain = head_norm_rope_bwd(dk, qkv_s[rows, X_K + g * LANES:X_K + (g + 1) * LANES], k_inv, low_k, cs_bwd, low)
+            dks.append(dk)
+            head_acc[1] += dk_gain
+            dq_upper, dq_lower = mm(ds_upper, k_swap[:HALF_SEQ]), mm(ds_lower, k_swap)
+            for r in range(GRP):
+                h = g * GRP + r
+                dq_h, dq_gain = head_norm_rope_bwd(joined(dq_upper, dq_lower, r), qkv_s[rows, h * LANES:(h + 1) * LANES], q_invs[r], low_q, cs_bwd, low)
+                dqs.append(dq_h)
+                head_acc[0] += dq_gain
+        packed.append(jnp.concatenate(pack_pairs(dqs + dks + dvs), axis=1))
+    dqkv = jnp.concatenate(packed, axis=0)
     acc[:, 0:1024] += mm(m1.T, dqkv)
     dm1 = mm(dqkv, w_ref[:, 0:1024], 1, 1)
     n1 = x * inv1
     norm_acc[0] += fold8(dm1 * n1)
     dx = dh + norm_bwd(dm1, n1, inv1, gain1)
-    upper, lower = dx[:HALF_SEQ], dx[HALF_SEQ:]
-    for j in range(4):
-        dx_ref[pl.ds(j, HALF_SEQ, stride=PAIR_WORDS), :] = upper[:, j * LANES:j * LANES + LANES]
-        dx_ref[pl.ds(5 + j, HALF_SEQ, stride=PAIR_WORDS), :] = lower[:, j * LANES:j * LANES + LANES]
-    dx_ref[pl.ds(4, HALF_SEQ, stride=PAIR_WORDS), :] = jnp.concatenate([upper[:, 512:], lower[:, 512:]], axis=1)
+    for s in range(SEQS):
+        upper, lower = dx[s * SEQ:s * SEQ + HALF_SEQ], dx[s * SEQ + HALF_SEQ:(s + 1) * SEQ]
+        base = s * HALF_SEQ * PAIR_WORDS
+        for j in range(4):
+            dx_ref[pl.ds(base + j, HALF_SEQ, stride=PAIR_WORDS), :] = upper[:, j * LANES:(j + 1) * LANES]
+            dx_ref[pl.ds(base + 5 + j, HALF_SEQ, stride=PAIR_WORDS), :] = lower[:, j * LANES:(j + 1) * LANES]
+        dx_ref[pl.ds(base + 4, HALF_SEQ, stride=PAIR_WORDS), :] = jnp.concatenate([upper[:, 512:], lower[:, 512:]], axis=1)
 
     @pl.when(step == steps - 1)
     def _():
@@ -231,22 +262,29 @@
         acc[:, C_HEAD:C_HEAD + LANES] += jnp.broadcast_to(head_row, (D, LANES))
         if last:
             mine = core_ref[0]
-            for f in range(0, FF, 192):
-                for t in range(0, D, LANES):
-                    width = min(LANES, D - t)
-                    tbuf[f:f + 192, t:t + width] = accd[t:t + width, f:f + 192].T
-            stores = []
-            for d in range(8):
-                for src, keep, send in ((acc.at[pl.ds(d * 72, 72), :], outs[0], outs[1]), (tbuf.at[pl.ds(d * 192, 192), :], outs[2], outs[3])):
-                    stores.append(pltpu.make_async_copy(src, keep.at[d // 2], sems.at[0]))
-
-                    @pl.when(mine == d % 2)
-                    def _():
-                        stores[-1].start()
-
-                    @pl.when(mine != d % 2)
-                    def _():
-                        pltpu.make_async_copy(src, send.at[d // 2], sems.at[0]).start()
+
+            def send_block(d, src, keep, send, sem):
+                @pl.when(mine == d % 2)
+                def _():
+                    pltpu.make_async_copy(src, keep.at[d // 2], sem).start()
+
+                @pl.when(mine != d % 2)
+                def _():
+                    pltpu.make_async_copy(src, send.at[d // 2], sem).start()
+
+                return pltpu.make_async_copy(src, keep.at[d // 2], sem)
+
+            stores = [send_block(d, acc.at[pl.ds(d * 72, 72), :], outs[0], outs[1], sems.at[0]) for d in range(8)]
+            for part in range(0, 8, 4):
+                moved = []
+                for d in range(4):
+                    f = (part + d) * 192
+                    for t in range(0, D, LANES):
+                        width = min(LANES, D - t)
+                        tbuf[d * 192:d * 192 + 192, t:t + width] = accd[t:t + width, f:f + 192].T
+                    moved.append(send_block(part + d, tbuf.at[pl.ds(d * 192, 192), :], outs[2], outs[3], sems.at[1]))
+                for store in moved:
+                    store.wait()
         else:
             stores = [pltpu.make_async_copy(acc, outs[0], sems.at[0]), pltpu.make_async_copy(accd, outs[1], sems.at[0])]
             for store in stores:
@@ -423,12 +461,13 @@
 
 
 def layer_chunk(x, dy, cs, w_pack, w_down, gains, head_gains, core, start, carry, last, total):
-    steps = x.shape[0] // (HALF_SEQ)
+    steps = x.shape[0] // (SEQS * HALF_SEQ)
+    start = start // SEQS
     first = carry is None
     whole = lambda shape: pl.BlockSpec(shape, lambda i: (0,) * len(shape), pipeline_mode=pl.Buffered(1))
-    here = lambda cols: pl.BlockSpec((SEQ, cols), lambda i: (i + start, 0))
+    here = lambda cols: pl.BlockSpec((SEQS * SEQ, cols), lambda i: (i + start, 0))
     anyspec = pl.BlockSpec(memory_space=pl.ANY)
-    in_specs = [pl.BlockSpec((HALF_SEQ, 2 * D), lambda i: (i, 0)), here(D), here(LANES), whole(w_pack.shape), whole(w_down.shape), whole(gains.shape), whole(head_gains.shape), pl.BlockSpec(memory_space=pltpu.SMEM)]
+    in_specs = [pl.BlockSpec((SEQS * HALF_SEQ, 2 * D), lambda i: (i, 0)), here(D), here(LANES), whole(w_pack.shape), whole(w_down.shape), whole(gains.shape), whole(head_gains.shape), pl.BlockSpec(memory_space=pltpu.SMEM)]
     args = [x, dy, cs, w_pack, w_down, gains, head_gains, core]
     aliases = {}
     if not first:
@@ -437,7 +476,7 @@
         aliases = {10: 0} if last else {8: 2, 9: 3, 10: 0}
     out_shape = [
         jax.ShapeDtypeStruct((total, D), BF),
-        jax.ShapeDtypeStruct((steps * HALF_SEQ * PAIR_WORDS, LANES), F32),
+        jax.ShapeDtypeStruct((steps * SEQS * HALF_SEQ * PAIR_WORDS, LANES), F32),
     ]
     grad_shapes = [(4, 72, G_COLS)] * 2 + [(4, 192, D)] * 2 if last else [(D, G_COLS), (D, FF)]
     out_shape += [jax.ShapeDtypeStruct(shape, F32) for shape in grad_shapes]
@@ -445,7 +484,7 @@
         functools.partial(layer_kernel, first, last, steps),
         grid=(steps,),
         in_specs=in_specs,
-        out_specs=[here(D), pl.BlockSpec((HALF_SEQ * PAIR_WORDS, LANES), lambda i: (i, 0))] + [anyspec] * len(grad_shapes),
+        out_specs=[here(D), pl.BlockSpec((SEQS * HALF_SEQ * PAIR_WORDS, LANES), lambda i: (i, 0))] + [anyspec] * len(grad_shapes),
         out_shape=out_shape,
         scratch_shapes=[
             pltpu.VMEM((D, G_COLS), F32),
@@ -454,14 +493,15 @@
             pltpu.VMEM((2, 8, LANES), F32),
             pltpu.VMEM((D, X_COLS), BF),
             pltpu.VMEM((HEADS * LANES, D), BF),
-            pltpu.VMEM((SEQ, X_COLS), BF),
-            pltpu.VMEM((KV, GRP * SEQ, SEQ), F32),
-            pltpu.VMEM((FF, D) if last else (8, LANES), F32),
+            pltpu.VMEM((SEQS * SEQ, X_COLS), BF),
+            pltpu.VMEM((SEQS * KV, GRP * HALF_SEQ, HALF_SEQ), F32),
+            pltpu.VMEM((SEQS * KV, GRP * HALF_SEQ, SEQ), F32),
+            pltpu.VMEM((FF // 2, D) if last else (8, LANES), F32),
             pltpu.SemaphoreType.DMA((2,)),
         ],
         input_output_aliases=aliases,
-        compiler_params=pltpu.CompilerParams(dimension_semantics=('arbitrary',), vmem_limit_bytes=60 << 20),
-        cost_estimate=pl.CostEstimate(flops=steps * 6_000_000_000, bytes_accessed=steps * 2_500_000 + 45_000_000, transcendentals=steps * 1_000_000),
+        compiler_params=pltpu.CompilerParams(dimension_semantics=('arbitrary',), vmem_limit_bytes=62 << 20),
+        cost_estimate=pl.CostEstimate(flops=steps * SEQS * 6_000_000_000, bytes_accessed=steps * SEQS * 2_500_000 + 45_000_000, transcendentals=steps * SEQS * 1_000_000),
         name='layer_chunk',
     )(*args)
     return dx, (*grads, y)
@@ -469,6 +509,15 @@
 
 def swap_with(bit, values):
     return lax.ppermute(values, AXIS_NAME, [(i, i ^ bit) for i in range(8)])
+
+
+def gather_by_swaps(shard):
+    index = lax.axis_index(AXIS_NAME)
+    for bit in (1, 2, 4):
+        got = swap_with(bit, shard)
+        second = (index // bit) % 2 == 1
+        shard = jnp.where(second, jnp.concatenate([got, shard], axis=0), jnp.concatenate([shard, got], axis=0))
+    return shard
 
 
 def reduce_grads(grads):
@@ -509,7 +558,7 @@
         pad = jnp.zeros((shard, 64), BF)
         packed = jnp.concatenate([w_query, w_key, w_value, pad, w_out, pad, w_gate, w_up, norms], axis=1)
         w_pack = lax.all_gather(packed, AXIS_NAME, tiled=True)
-        w_down_full = lax.all_gather(w_down, AXIS_NAME, tiled=True)
+        w_down_full = gather_by_swaps(w_down)
         gains = w_pack[:, C_NORM:C_NORM + 2].T.astype(F32)
         head_gains = jnp.stack([q_norm, k_norm]).astype(F32)
         swapped = jnp.concatenate([head_gains[:, 32:], head_gains[:, :32]], axis=1)

time: 793 us -> 810 us (1.021)
  Pallas kernels: 505 us -> 547 us
  waiting for transfers between devices: 198 us -> 169 us
    pallas_call x3, Pallas kernels: 294 us -> 335 us  [layer_chunk(): pl.pallas_call(functools.partial(layer_kernel, first, last, steps), grid=...]
    reduce_scatter x3, waiting for transfers between devices: 27.1 us -> 0.04 us  [device_step(): lax.psum_scatter(rows, AXIS_NAME, scatter_dimension=0, tiled=True)]
    ppermute x10 -> x13, waiting for transfers between devices: 170 us -> 168 us  [swap_with(): return lax.ppermute(values, AXIS_NAME, [(i, i ^ bit) for i in range(8)])]
  transfers between devices with their start and end apart: 18 -> 20, of which waited for: 6 -> 8; matrix products, arithmetic and copies ran while one was open for 5% -> 5% of each run, Pallas kernels for 58% -> 62%
where the time goes in v2:
time: 810 us; the launch traced here: 803 us
  Pallas kernels  547 us (68%)
  waiting for transfers between devices  169 us (21%)
  local copies, waits for them, and re-layouts  23 us (3%)
  other arithmetic  22.3 us (3%)
  between operations  14.9 us (2%)
  blocking collectives  14.8 us (2%)
  starting transfers between devices  11.9 us (1%)
    pallas_call x3, Pallas kernels, layer_chunk(): pl.pallas_call(functools.partial(layer_kernel, first, last, steps), grid=...  335 us
    ppermute x13, waiting for transfers between devices, swap_with(): return lax.ppermute(values, AXIS_NAME, [(i, i ^ bit) for i in range(8)])  168 us
    pallas_call x3, Pallas kernels, scatter_rows(): pl.pallas_call(functools.partial(scatter_kernel, first, last, blocks), gr...  136 us
    pallas_call x2, Pallas kernels, gather_rows(): pl.pallas_call(functools.partial(gather_kernel, blocks), grid_spec=pltpu....  75.8 us
  transfers between devices with their start and end apart: 20, of which 8 were waited for; matrix products, arithmetic and copies ran while one was open for 5% of the time, Pallas kernels for 62%

profile of v2, /device:TPU:0, one launch (start us, length us, event | category | flops | bytes accessed | tf_op | source)
XLA Modules:
  0.0 803.0 jit_solution(9200871165554098198)
XLA Ops:
  7.2 0.8 copy.65
  8.0 0.8 copy.66
  8.8 2.1 concatenate.47
  11.0 14.8 %all-gather.1 = s32[8,12,256]{2,1,0:T(8,128)S(1)} all-gather(s32[1,12,256]{2,1,0:T(8,128)S(1)} %bitcast.100), channel_id=2, replica_groups=mesh['fsdp'=8] {'fsdp'}, dimensions={0}, use_global_device_ids=true | all-gather | bytes 110592 | tf_op jit(solution)/shard_map/all_gather | solution.py:556
  25.9 0.5 copy-done.1
  26.4 0.1 bitcast_subtract_fusion
  26.5 28.4 %gather_rows.3 = bf16[4096,1152]{1,0:T(8,128)(2,1)} custom-call(s32[8192]{0:T(1024)S(1)} %get-tuple-element.137.ids_ref, bf16[576,6144]{1,0:T(8,128)(2,1)} %bitcast.108), custom_call_target="tpu_custom_call" | custom-call | flops 40000000000 | bytes 40000000 | tf_op jit(solution)/shard_map/gather_rows/pallas_call | solution.py:347
  55.0 47.4 %gather_rows.2 = (bf16[4096,1152]{1,0:T(8,128)(2,1)}, bf16[4096,1152]{1,0:T(8,128)(2,1)}) custom-call(s32[16384]{0:T(1024)S(1)} %pad_add_fusion.ids_ref, bf16[576,6144]{1,0:T(8,128)(2,1)} %bitcast.109), custom_call_target="tpu_custom_call" | custom-call | flops 40000000000 | bytes 40000000 | tf_op jit(solution)/shard_map/gather_rows/pallas_call | solution.py:347
  102.6 0.5 reduce-scatter.4.cloned.1.call-update
  103.1 0.4 copy-done.7
  103.5 6.1 copy.63
  109.7 0.2 maximum_select_fusion.2
  109.9 0.6 pad_maximum_fusion.3.refs_6_
  110.6 22.0 %collective-permute-done.1 = bf16[384,576]{1,0:T(8,128)(2,1)S(1)} collective-permute-done((bf16[384,576]{1,0:T(8,128)(2,1)S(1)}, bf16[384,576]{1,0:T(8,128)(2,1)S(1)}, u32[]{:S(2)}, u32[]{:S(2)}) %collective-permute-start.1) | collective-permute-done | bytes 442400 | tf_op jit(solution)/shard_map/ppermute | solution.py:511
  132.6 0.4 maximum_select_fusion.1
  133.0 0.6 copy.67
  133.6 1.4 collective-permute-start.2
  135.0 5.8 multiply_cosine_fusion
  140.8 2.5 pad_maximum_fusion.refs_2_
  143.2 11.9 %collective-permute-done.2 = bf16[768,576]{0,1:T(8,128)(2,1)S(1)} collective-permute-done((bf16[768,576]{0,1:T(8,128)(2,1)S(1)}, bf16[768,576]{0,1:T(8,128)(2,1)S(1)}, u32[]{:S(2)}, u32[]{:S(2)}) %collective-permute-start.2) | collective-permute-done | bytes 884768 | tf_op jit(solution)/shard_map/ppermute | solution.py:511
  155.2 0.6 copy.68
  155.8 2.1 maximum_select_fusion.refs_4_
  157.9 1.0 slice_convert_fusion
  158.9 0.7 copy.76
  159.6 127.4 %layer_chunk.3 = (bf16[3072,576]{1,0:T(8,128)(2,1)}, f32[4608,128]{1,0:T(8,128)}, f32[576,4992]{1,0:T(8,128)}, f32[576,1536]{1,0:T(8,128)}) custom-call(bf16[512,1152]{1,0:T(8,128)(2,1)} %reduce-scatter.8.cloned.1.call-done.refs_0_, bf16[3072,576]{1,0:T(8,128)(2,1)} %bitcast.90, f32[3072,128]{1,0:T(8,128)} %pad_maximum_fusion.refs_2_, ...), custom_call_target="tpu_custom_call" | custom-call | flops 24000000000 | bytes 55000000 | tf_op jit(solution)/shard_map/layer_chunk/pallas_call | solution.py:483
  287.2 91.3 %layer_chunk.4 = (bf16[3072,576]{1,0:T(8,128)(2,1)}, f32[4608,128]{1,0:T(8,128)}, f32[576,4992]{1,0:T(8,128)}, f32[576,1536]{1,0:T(8,128)}) custom-call(bf16[512,1152]{1,0:T(8,128)(2,1)} %reduce-scatter.6.cloned.1.call-done.refs_0_, bf16[3072,576]{1,0:T(8,128)(2,1)} %bitcast.91, ...), custom_call_target="tpu_custom_call", output_to_operand_aliasing={{2}: (8, {}), {3}: (9, {}), {0}: (10, {})} | custom-call | flops 24000000000 | bytes 55000000 | tf_op jit(solution)/shard_map/layer_chunk/pallas_call | solution.py:483
  378.6 116.6 %layer_chunk.5 = (bf16[3072,576]{1,0:T(8,128)(2,1)}, f32[4608,128]{1,0:T(8,128)}, f32[4,72,4992]{2,1,0:T(8,128)}, f32[4,72,4992]{2,1,0:T(8,128)}, f32[4,192,576]{2,1,0:T(8,128)}, /*index=5*/f32[4,192,576]{2,1,0:T(8,128)}) custom-call(bf16[512,1152]{1,0:T(8,128)(2,1)} %reduce-scatter.4.cloned.1.call-done.refs_0_, ...), custom_call_target="tpu_custom_call", output_to_operand_aliasing={{0}: (10, {})} | custom-call | flops 24000000000 | bytes 55000000 | tf_op jit(solution)/shard_map/layer_chunk/pallas_call | solution.py:483
  495.3 0.5 collective-permute-start.8
  495.8 0.2 copy-done.6
  496.1 0.1 fusion.52
  496.2 0.1 fusion.76
  496.3 0.1 fusion.69
  496.5 11.4 %collective-permute-done.8 = f32[4,192,576]{2,1,0:T(8,128)} collective-permute-done((f32[4,192,576]{2,1,0:T(8,128)}, f32[4,192,576]{2,1,0:T(8,128)}, u32[]{:S(2)}, u32[]{:S(2)}) %collective-permute-start.8) | collective-permute-done | bytes 1769504 | tf_op jit(solution)/shard_map/ppermute | solution.py:511
  507.9 1.8 add.183
  509.7 0.1 fusion.79
  509.9 0.6 collective-permute-start.9
  510.6 6.1 copy.71
  516.8 1.6 collective-permute-start.11
  518.4 15.9 %collective-permute-done.9 = f32[2,96,576]{2,1,0:T(8,128)S(1)} collective-permute-done((f32[2,96,576]{2,1,0:T(8,128)S(1)}, f32[2,96,576]{2,1,0:T(8,128)S(1)}, u32[]{:S(2)}, u32[]{:S(2)}) %collective-permute-start.9) | collective-permute-done | bytes 442400 | tf_op jit(solution)/shard_map/ppermute | solution.py:511
  534.4 4.9 add.174
  539.3 0.2 slice.222
  539.5 0.1 dynamic-slice_bitcast_fusion.1
  539.6 1.6 collective-permute-start.4
  541.2 0.4 collective-permute-start.10
  541.8 0.8 collective-permute-start.12
  542.6 67.0 %collective-permute-done.10 = f32[96,576]{1,0:T(8,128)S(1)} collective-permute-done((f32[96,576]{1,0:T(8,128)S(1)}, f32[96,576]{1,0:T(8,128)S(1)}, u32[]{:S(2)}, u32[]{:S(2)}) %collective-permute-start.10) | collective-permute-done | bytes 221216 | tf_op jit(solution)/shard_map/ppermute | solution.py:511
  609.6 0.4 slice.224
  610.0 0.1 dynamic-slice_bitcast_fusion
  610.2 0.8 pad_maximum_fusion.1
  611.0 0.1 bitcast_add_fusion.1
  611.2 2.0 collective-permute-start.5
  613.3 32.1 %collective-permute-done.6 = f32[2,72,2560]{2,1,0:T(8,128)S(1)} collective-permute-done((f32[2,72,2560]{2,1,0:T(8,128)S(1)}, f32[2,72,2560]{2,1,0:T(8,128)S(1)}, u32[]{:S(2)}, u32[]{:S(2)}) %collective-permute-start.6) | collective-permute-done | bytes 1474592 | tf_op jit(solution)/shard_map/ppermute | solution.py:511
  645.3 0.2 bitcast_add_fusion
  645.5 2.5 collective-permute-start.7
  648.0 7.0 collective-permute-done.5
  655.2 0.7 slice_reduce_fusion
  655.9 0.6 slice_bitcast_fusion
  656.5 1.0 collective-permute-done.7
  657.6 0.7 fusion.81
  658.3 0.8 fusion.80
  659.1 1.0 fusion.82
  660.1 40.4 %scatter_rows.3.refs_0_ = f32[36960,128]{1,0:T(8,128)} custom-call(s32[8192]{0:T(1024)S(1)} %get-tuple-element.136.ids_ref, s32[512]{0:T(512)S(1)} %convert_bitcast_fusion.clash_ref, f32[36864,128]{1,0:T(8,128)} %all-gather.13.cloned.1.call-done.rows_ref), custom_call_target="tpu_custom_call" | custom-call | flops 20000000000 | bytes 60000000 | tf_op jit(solution)/shard_map/scatter_rows/pallas_call | solution.py:446
  700.5 46.2 %scatter_rows.4.refs_0_ = f32[36960,128]{1,0:T(8,128)} custom-call(s32[8192]{0:T(1024)S(1)} %get-tuple-element.151.ids_ref, s32[512]{0:T(512)S(1)} %convert_bitcast_fusion.1.clash_ref, f32[36864,128]{1,0:T(8,128)} %all-gather.11.cloned.1.call-done.rows_ref, f32[36960,128]{1,0:T(8,128)} %scatter_rows.3.refs_0_), custom_call_target="tpu_custom_call", output_to_operand_aliasing={{}: (3, {})} | custom-call | flops 20000000000 | bytes 60000000 | tf_op jit(solution)/shard_map/scatter_rows/pallas_call | solution.py:446
  746.7 49.2 %scatter_rows.5 = f32[576,6144]{1,0:T(8,128)} custom-call(s32[8192]{0:T(1024)S(1)} %get-tuple-element.149.ids_ref, s32[512]{0:T(512)S(1)} %convert_bitcast_fusion.2.clash_ref, f32[36864,128]{1,0:T(8,128)} %all-gather.9.cloned.1.call-done.rows_ref, f32[36960,128]{1,0:T(8,128)} %scatter_rows.4.refs_0_), custom_call_target="tpu_custom_call" | custom-call | flops 20000000000 | bytes 60000000 | tf_op jit(solution)/shard_map/scatter_rows/pallas_call | solution.py:446
  (86 shorter events, 1.6 us)
Async XLA Ops:
  7.2 3.8 copy-start.8
  7.2 150.7 %all-gather.7.cloned.1.call-start = ((), (), s32[]{:S(2)}) async-start(), calls=%async_computation.4 | async-start | bytes 6303744 | tf_op jit(solution)/shard_map/all_gather | solution.py:560
  10.9 148.7 %reduce-scatter.8.cloned.1.call-start = ((), (), s32[]{:S(2)}) async-start(), calls=%async_computation.6 | async-start | bytes 10616832 | tf_op jit(solution)/shard_map/reduce_scatter | solution.py:590
  25.8 0.6 copy-start.1
  25.8 0.6 copy-start.3
  25.8 0.6 copy-start.5
  55.0 232.2 %reduce-scatter.6.cloned.1.call-start = ((), (), s32[]{:S(2)}) async-start(), calls=%async_computation.5 | async-start | bytes 10616832 | tf_op jit(solution)/shard_map/reduce_scatter | solution.py:590
  102.5 276.1 %reduce-scatter.4.cloned.1.call-start = ((), (), s32[]{:S(2)}) async-start(), calls=%async_computation.3 | async-start | bytes 10616832 | tf_op jit(solution)/shard_map/reduce_scatter | solution.py:590
  102.6 0.9 copy-start.7
  102.6 0.9 copy-start.9
  103.1 557.0 %all-gather.13.cloned.1.call-start = ((), (), s32[]{:S(2)}) async-start(), calls=%async_computation.9 | async-start | bytes 21233664 | tf_op jit(solution)/shard_map/all_gather | solution.py:597
  103.5 6.2 collective-permute-start
  103.5 6.1 copy-start.10
  103.5 6.1 copy-start.11
  109.8 22.8 %collective-permute-start.1 = (bf16[384,576]{1,0:T(8,128)(2,1)S(1)}, bf16[384,576]{1,0:T(8,128)(2,1)S(1)}, u32[]{:S(2)}, u32[]{:S(2)}) collective-permute-start(bf16[384,576]{1,0:T(8,128)(2,1)S(1)} %maximum_select_fusion.2), channel_id=1, source_target_pairs={{0,2},{1,3},{2,0},{3,1},{4,6},{5,7},{6,4},{7,5}} | collective-permute-start | bytes 1327112 | tf_op jit(solution)/shard_map/ppermute | solution.py:511
  133.6 21.6 %collective-permute-start.2 = (bf16[768,576]{0,1:T(8,128)(2,1)S(1)}, bf16[768,576]{0,1:T(8,128)(2,1)S(1)}, u32[]{:S(2)}, u32[]{:S(2)}) collective-permute-start(bf16[768,576]{0,1:T(8,128)(2,1)S(1)} %copy.67), channel_id=1, source_target_pairs={{0,4},{1,5},{2,6},{3,7},{4,0},{5,1},{6,2},{7,3}} | collective-permute-start | bytes 2654216 | tf_op jit(solution)/shard_map/ppermute | solution.py:511
  287.1 413.4 %all-gather.11.cloned.1.call-start = ((), (), s32[]{:S(2)}) async-start(), calls=%async_computation.8 | async-start | bytes 21233664 | tf_op jit(solution)/shard_map/all_gather | solution.py:597
  378.5 368.2 %all-gather.9.cloned.1.call-start = ((), (), s32[]{:S(2)}) async-start(), calls=%async_computation.7 | async-start | bytes 21233664 | tf_op jit(solution)/shard_map/all_gather | solution.py:597
  495.2 0.8 copy-start.6
  495.3 0.8 copy-start.4
  495.3 0.8 copy-start.2
  495.3 12.6 %copy-start = (f32[4,192,576]{2,1,0:T(8,128)S(1)}, f32[4,192,576]{2,1,0:T(8,128)}, u32[]{:S(2)}) copy-start(f32[4,192,576]{2,1,0:T(8,128)} %get-tuple-element.43) | copy-start | bytes 5308420
  495.3 39.1 %collective-permute-start.3 = (f32[4,72,4992]{2,1,0:T(8,128)}, f32[4,72,4992]{2,1,0:T(8,128)}, u32[]{:S(2)}, u32[]{:S(2)}) collective-permute-start(f32[4,72,4992]{2,1,0:T(8,128)} %get-tuple-element.42), channel_id=1, source_target_pairs={{0,1},{1,0},{2,3},{3,2},{4,5},{5,4},{6,7},{7,6}} | collective-permute-start | bytes 17252360 | tf_op jit(solution)/shard_map/ppermute | solution.py:511
  495.3 12.5 %collective-permute-start.8 = (f32[4,192,576]{2,1,0:T(8,128)}, f32[4,192,576]{2,1,0:T(8,128)}, u32[]{:S(2)}, u32[]{:S(2)}) collective-permute-start(f32[4,192,576]{2,1,0:T(8,128)} %get-tuple-element.44), channel_id=1, source_target_pairs={{0,1},{1,0},{2,3},{3,2},{4,5},{5,4},{6,7},{7,6}} | collective-permute-start | bytes 5308424 | tf_op jit(solution)/shard_map/ppermute | solution.py:511
  509.9 24.4 %collective-permute-start.9 = (f32[2,96,576]{2,1,0:T(8,128)S(1)}, f32[2,96,576]{2,1,0:T(8,128)S(1)}, u32[]{:S(2)}, u32[]{:S(2)}) collective-permute-start(f32[2,96,576]{2,1,0:T(8,128)S(1)} %dynamic-slice_bitcast_fusion.5), channel_id=1, source_target_pairs={{0,2},{1,3},{2,0},{3,1},{4,6},{5,7},{6,4},{7,5}} | collective-permute-start | bytes 1327112 | tf_op jit(solution)/shard_map/ppermute | solution.py:511
  516.8 24.9 %collective-permute-start.11 = (f32[2,96,576]{2,1,0:T(8,128)S(1)}, f32[2,96,576]{2,1,0:T(8,128)S(1)}, u32[]{:S(2)}, u32[]{:S(2)}) collective-permute-start(f32[2,96,576]{2,1,0:T(8,128)S(1)} %dynamic-slice_bitcast_fusion.4), channel_id=1, source_target_pairs={{0,4},{1,5},{2,6},{3,7},{4,0},{5,1},{6,2},{7,3}} | collective-permute-start | bytes 1327112 | tf_op jit(solution)/shard_map/ppermute | solution.py:511
  539.6 71.4 %collective-permute-start.4 = (f32[2,72,2432]{2,1,0:T(8,128)S(1)}, f32[2,72,2432]{2,1,0:T(8,128)S(1)}, u32[]{:S(2)}, u32[]{:S(2)}) collective-permute-start(f32[2,72,2432]{2,1,0:T(8,128)S(1)} %dynamic-slice_bitcast_fusion.1), channel_id=1, source_target_pairs={{0,4},{1,5},{2,6},{3,7},{4,0},{5,1},{6,2},{7,3}} | collective-permute-start | bytes 4202504 | tf_op jit(solution)/shard_map/ppermute | solution.py:511
  541.2 68.4 %collective-permute-start.10 = (f32[96,576]{1,0:T(8,128)S(1)}, f32[96,576]{1,0:T(8,128)S(1)}, u32[]{:S(2)}, u32[]{:S(2)}) collective-permute-start(f32[96,576]{1,0:T(8,128)S(1)} %dynamic-slice_bitcast_fusion.7), channel_id=1, source_target_pairs={{0,4},{1,5},{2,6},{3,7},{4,0},{5,1},{6,2},{7,3}} | collective-permute-start | bytes 663560 | tf_op jit(solution)/shard_map/ppermute | solution.py:511
  541.8 68.4 %collective-permute-start.12 = (f32[96,576]{1,0:T(8,128)S(1)}, f32[96,576]{1,0:T(8,128)S(1)}, u32[]{:S(2)}, u32[]{:S(2)}) collective-permute-start(f32[96,576]{1,0:T(8,128)S(1)} %dynamic-slice_bitcast_fusion.6), channel_id=1, source_target_pairs={{0,2},{1,3},{2,0},{3,1},{4,6},{5,7},{6,4},{7,5}} | collective-permute-start | bytes 663560 | tf_op jit(solution)/shard_map/ppermute | solution.py:511
  610.1 35.2 %collective-permute-start.6 = (f32[2,72,2560]{2,1,0:T(8,128)S(1)}, f32[2,72,2560]{2,1,0:T(8,128)S(1)}, u32[]{:S(2)}, u32[]{:S(2)}) collective-permute-start(f32[2,72,2560]{2,1,0:T(8,128)S(1)} %dynamic-slice_bitcast_fusion), channel_id=1, source_target_pairs={{0,2},{1,3},{2,0},{3,1},{4,6},{5,7},{6,4},{7,5}} | collective-permute-start | bytes 4423688 | tf_op jit(solution)/shard_map/ppermute | solution.py:511
  611.2 43.9 %collective-permute-start.5 = (f32[72,2432]{1,0:T(8,128)S(1)}, f32[72,2432]{1,0:T(8,128)S(1)}, u32[]{:S(2)}, u32[]{:S(2)}) collective-permute-start(f32[72,2432]{1,0:T(8,128)S(1)} %dynamic-slice_bitcast_fusion.3), channel_id=1, source_target_pairs={{0,2},{1,3},{2,0},{3,1},{4,6},{5,7},{6,4},{7,5}} | collective-permute-start | bytes 2101256 | tf_op jit(solution)/shard_map/ppermute | solution.py:511
  645.5 11.9 %collective-permute-start.7 = (f32[72,2560]{1,0:T(8,128)S(1)}, f32[72,2560]{1,0:T(8,128)S(1)}, u32[]{:S(2)}, u32[]{:S(2)}) collective-permute-start(f32[72,2560]{1,0:T(8,128)S(1)} %dynamic-slice_bitcast_fusion.2), channel_id=1, source_target_pairs={{0,4},{1,5},{2,6},{3,7},{4,0},{5,1},{6,2},{7,3}} | collective-permute-start | bytes 2211848 | tf_op jit(solution)/shard_map/ppermute | solution.py:511
Sparse Core Ops, SparseCore 0:
  11.0 40.0 all-gather.6
  55.2 77.6 reduce-scatter.7
  136.3 69.7 reduce-scatter.5
  209.4 68.4 reduce-scatter.3
  287.2 93.0 all-gather.12
  382.0 93.0 all-gather.10
  495.4 134.7 all-gather.8

commit v3 on v2

--- a/solution.py
+++ b/solution.py
@@ -12,7 +12,7 @@
 AXIS_NAME = 'fsdp'
 SEQ = 256
 HALF_SEQ = SEQ // 2
-SEQS = 2
+SEQS = 1
 LANES = 128
 D = 576
 FF = 1536
@@ -520,25 +520,17 @@
     return shard
 
 
-def reduce_grads(grads):
+def reduce_by_swaps(kept, sent, axis, cut):
     index = lax.axis_index(AXIS_NAME)
     x, y = (index // 2) % 2, index // 4
-    parts = [(grads[i], swap_with(1, grads[i + 1])) for i in (0, 2)]
-    summed = [(kept + got).reshape(2, 2, *kept.shape[1:]) for kept, got in parts]
     at = lambda values, axis, idx: lax.dynamic_index_in_dim(values, idx, axis, keepdims=False)
-    results = []
-    for grads in summed:
-        axis, cut = (-1, 2560) if grads.shape[-1] == G_COLS else (-2, 96)
-        size = grads.shape[axis]
-        one, two = lax.slice_in_dim(grads, 0, cut, axis=axis), lax.slice_in_dim(grads, cut, size, axis=axis)
-        one_got = swap_with(2, at(one, 1, 1 - x))
-        two_got = swap_with(4, at(two, 0, 1 - y))
-        results.append((at(one, 1, x), one_got, at(two, 0, y), two_got, axis))
-    finals = []
-    for one, one_got, two, two_got, axis in results:
-        one, two = one + one_got, two + two_got
-        finals.append((at(one, 0, y), swap_with(4, at(one, 0, 1 - y)), at(two, 0, x), swap_with(2, at(two, 0, 1 - x)), axis))
-    return [jnp.concatenate([one + one_got, two + two_got], axis=axis) for one, one_got, two, two_got, axis in finals]
+    got = swap_with(1, sent)
+    summed = (kept + got).reshape(2, 2, *kept.shape[1:])
+    one, two = lax.slice_in_dim(summed, 0, cut, axis=axis), lax.slice_in_dim(summed, cut, summed.shape[axis], axis=axis)
+    one_got, two_got = swap_with(2, at(one, 1, 1 - x)), swap_with(4, at(two, 0, 1 - y))
+    one, two = at(one, 1, x) + one_got, at(two, 0, y) + two_got
+    one_got, two_got = swap_with(4, at(one, 0, 1 - y)), swap_with(2, at(two, 0, 1 - x))
+    return jnp.concatenate([at(one, 0, y) + one_got, at(two, 0, x) + two_got], axis=axis)
 
 
 def solution(mesh):
@@ -585,9 +577,19 @@
             clashes.append(functools.reduce(jnp.logical_or, same).astype(jnp.int32).reshape(-1))
 
         table_t = table_shard.T
+        parity = lax.axis_index(AXIS_NAME) % 2
+        *mids, last_ids = take_from[1:]
+        by_core = last_ids.reshape(devices // 2, 2, -1)
+        kept = jnp.where(parity == 0, by_core[:, 0], by_core[:, 1]).reshape(-1)
+        sent = jnp.where(parity == 0, by_core[:, 1], by_core[:, 0]).reshape(-1)
         picked = gather_rows(take_from[0], table_t, (devices * CHUNKS[0],))
-        picked += gather_rows(jnp.concatenate(take_from[1:]), table_t, tuple(devices * n for n in CHUNKS[1:]))
+        half_rows = devices // 2 * CHUNKS[-1]
+        picked += gather_rows(jnp.concatenate(mids + [kept, sent]), table_t, tuple(devices * n for n in CHUNKS[1:-1]) + (half_rows, half_rows))
+        *picked, kept, sent = picked
         xs = [lax.psum_scatter(rows, AXIS_NAME, scatter_dimension=0, tiled=True) for rows in picked]
+        pair_rows = CHUNKS[-1] * HALF_SEQ
+        split = lambda rows: rows.reshape(devices // 2, pair_rows, 2 * D)
+        xs.append(reduce_by_swaps(split(kept), split(sent), -2, pair_rows // 2))
         core = lax.rem(lax.axis_index(AXIS_NAME), 2).reshape(1)
         carry = None
         rows_of = []
@@ -600,7 +602,8 @@
         for idx in range(len(CHUNKS)):
             d_table = scatter_rows(add_to[idx], clashes[idx], rows_of[idx], rows_local, d_table, idx == len(CHUNKS) - 1)
         d_table = d_table.T
-        g_pack, d_w_down = reduce_grads(grads)
+        g_pack = reduce_by_swaps(grads[0], grads[1], -1, 2560)
+        d_w_down = reduce_by_swaps(grads[2], grads[3], -2, 96)
         kv_cols = w_key.shape[1]
         return (y.reshape(batch_len, seq_len, D), d_table, g_pack[:, C_NORM], g_pack[:, :D], g_pack[:, D:D + kv_cols], g_pack[:, D + kv_cols:D + 2 * kv_cols],
                 g_pack[0, C_HEAD:C_HEAD + HEAD], g_pack[0, C_HEAD + HEAD:C_HEAD + 2 * HEAD], g_pack[:, C_OUT:C_OUT + D], g_pack[:, C_NORM + 1],

time: 810 us -> 848 us (1.047)
  waiting for transfers between devices: 169 us -> 254 us
  Pallas kernels: 547 us -> 482 us
  other arithmetic: 22.3 us -> 33.1 us
    ppermute x13 -> x18, waiting for transfers between devices: 168 us -> 254 us  [swap_with(): return lax.ppermute(values, AXIS_NAME, [(i, i ^ bit) for i in range(8)])]
    pallas_call x3, Pallas kernels: 335 us -> 272 us  [layer_chunk(): pl.pallas_call(functools.partial(layer_kernel, first, last, steps), grid=...]
    add x10 -> x15, other arithmetic: 7.38 us -> 17.1 us  [the longest x3 13.1 us: reduce_by_swaps(): summed = (kept + got).reshape(2, 2, *kept.shape[1:])]
  transfers between devices with their start and end apart: 20 -> 24, of which waited for: 8 -> 12; matrix products, arithmetic and copies ran while one was open for 5% -> 6% of each run, Pallas kernels for 62% -> 51%
where the time goes in v3:
time: 848 us; the launch traced here: 841 us
  Pallas kernels  482 us (57%)
  waiting for transfers between devices  254 us (30%)
  other arithmetic  33.1 us (4%)
  local copies, waits for them, and re-layouts  29.9 us (4%)
  between operations  15.2 us (2%)
  blocking collectives  14.8 us (2%)
  starting transfers between devices  12.6 us (1%)
    pallas_call x3, Pallas kernels, layer_chunk(): pl.pallas_call(functools.partial(layer_kernel, first, last, steps), grid=...  272 us
    ppermute x18, waiting for transfers between devices, swap_with(): return lax.ppermute(values, AXIS_NAME, [(i, i ^ bit) for i in range(8)])  254 us
    pallas_call x3, Pallas kernels, scatter_rows(): pl.pallas_call(functools.partial(scatter_kernel, first, last, blocks), gr...  136 us
    pallas_call x2, Pallas kernels, gather_rows(): pl.pallas_call(functools.partial(gather_kernel, blocks), grid_spec=pltpu....  74.3 us
    unnamed x30, local copies, waits for them, and re-layouts  18.3 us
  transfers between devices with their start and end apart: 24, of which 12 were waited for; matrix products, arithmetic and copies ran while one was open for 6% of the time, Pallas kernels for 51%

profile of v3, /device:TPU:0, one launch (start us, length us, event | category | flops | bytes accessed | tf_op | source)
XLA Modules:
  0.0 841.2 jit_solution(1120683592143294269)
XLA Ops:
  7.2 0.8 copy.65
  8.0 0.8 copy.66
  8.8 2.1 concatenate.51
  11.0 14.8 %all-gather.1 = s32[8,12,256]{2,1,0:T(8,128)S(1)} all-gather(s32[1,12,256]{2,1,0:T(8,128)S(1)} %bitcast.125), channel_id=2, replica_groups=mesh['fsdp'=8] {'fsdp'}, dimensions={0}, use_global_device_ids=true | all-gather | bytes 110592 | tf_op jit(solution)/shard_map/all_gather | solution.py:548
  25.9 0.5 copy-done.3
  26.5 28.4 %gather_rows.3 = bf16[4096,1152]{1,0:T(8,128)(2,1)} custom-call(s32[8192]{0:T(1024)S(1)} %get-tuple-element.141.ids_ref, bf16[576,6144]{1,0:T(8,128)(2,1)} %bitcast.133), custom_call_target="tpu_custom_call" | custom-call | flops 40000000000 | bytes 40000000 | tf_op jit(solution)/shard_map/gather_rows/pallas_call | solution.py:347
  55.2 45.9 %gather_rows.2 = (bf16[4096,1152]{1,0:T(8,128)(2,1)}, bf16[2048,1152]{1,0:T(8,128)(2,1)S(1)}, bf16[2048,1152]{1,0:T(8,128)(2,1)}) custom-call(s32[16384]{0:T(1024)S(1)} %pad_add_fusion.ids_ref, bf16[576,6144]{1,0:T(8,128)(2,1)} %bitcast.134), custom_call_target="tpu_custom_call" | custom-call | flops 40000000000 | bytes 40000000 | tf_op jit(solution)/shard_map/gather_rows/pallas_call | solution.py:347
  101.0 2.2 copy-done
  103.3 0.9 copy-done.7
  104.2 6.1 copy.63
  110.6 0.6 pad_maximum_fusion.4.refs_6_
  111.3 21.3 %collective-permute-done.6 = bf16[384,576]{1,0:T(8,128)(2,1)S(1)} collective-permute-done((bf16[384,576]{1,0:T(8,128)(2,1)S(1)}, bf16[384,576]{1,0:T(8,128)(2,1)S(1)}, u32[]{:S(2)}, u32[]{:S(2)}) %collective-permute-start.6) | collective-permute-done | bytes 442400 | tf_op jit(solution)/shard_map/ppermute | solution.py:511
  133.0 0.6 copy.67
  133.6 1.5 collective-permute-start.7
  135.1 5.8 multiply_cosine_fusion
  140.9 2.5 pad_maximum_fusion.refs_2_
  143.3 11.8 %collective-permute-done.7 = bf16[768,576]{0,1:T(8,128)(2,1)S(1)} collective-permute-done((bf16[768,576]{0,1:T(8,128)(2,1)S(1)}, bf16[768,576]{0,1:T(8,128)(2,1)S(1)}, u32[]{:S(2)}, u32[]{:S(2)}) %collective-permute-start.7) | collective-permute-done | bytes 884768 | tf_op jit(solution)/shard_map/ppermute | solution.py:511
  155.2 0.6 copy.68
  155.8 2.0 maximum_select_fusion.refs_4_
  157.8 1.0 slice_convert_fusion
  158.8 0.7 copy.76
  159.6 87.6 %layer_chunk.3 = (bf16[3072,576]{1,0:T(8,128)(2,1)}, f32[4608,128]{1,0:T(8,128)}, f32[576,4992]{1,0:T(8,128)}, f32[576,1536]{1,0:T(8,128)}) custom-call(bf16[512,1152]{1,0:T(8,128)(2,1)} %reduce-scatter.5.cloned.1.call-done.refs_0_, bf16[3072,576]{1,0:T(8,128)(2,1)} %bitcast.113, f32[3072,128]{1,0:T(8,128)} %pad_maximum_fusion.refs_2_, ...), custom_call_target="tpu_custom_call" | custom-call | flops 24000000000 | bytes 55000000 | tf_op jit(solution)/shard_map/layer_chunk/pallas_call | solution.py:483
  247.3 92.2 %layer_chunk.4 = (bf16[3072,576]{1,0:T(8,128)(2,1)}, f32[4608,128]{1,0:T(8,128)}, f32[576,4992]{1,0:T(8,128)}, f32[576,1536]{1,0:T(8,128)}) custom-call(bf16[512,1152]{1,0:T(8,128)(2,1)} %reduce-scatter.3.cloned.1.call-done.refs_0_, bf16[3072,576]{1,0:T(8,128)(2,1)} %bitcast.114, ...), custom_call_target="tpu_custom_call", output_to_operand_aliasing={{2}: (8, {}), {3}: (9, {}), {0}: (10, {})} | custom-call | flops 24000000000 | bytes 55000000 | tf_op jit(solution)/shard_map/layer_chunk/pallas_call | solution.py:483
  339.6 8.2 collective-permute-done
  347.8 6.3 add.190
  354.5 1.5 copy-done.1
  356.0 1.1 dynamic-slice_bitcast_fusion.3
  357.1 0.7 collective-permute-start.1
  357.9 1.1 dynamic-slice_bitcast_fusion.2
  359.0 1.2 collective-permute-start.3
  360.2 45.9 %collective-permute-done.1 = bf16[2,256,1152]{2,1,0:T(8,128)(2,1)} collective-permute-done((bf16[2,256,1152]{2,1,0:T(8,128)(2,1)}, bf16[2,256,1152]{2,1,0:T(8,128)(2,1)}, u32[]{:S(2)}, u32[]{:S(2)}) %collective-permute-start.1) | collective-permute-done | bytes 1179680 | tf_op jit(solution)/shard_map/ppermute | solution.py:511
  406.0 1.8 bitcast_add_fusion.3
  407.9 1.5 collective-permute-start.2
  409.4 1.4 bitcast_add_fusion.2
  410.8 0.6 collective-permute-start.4
  411.4 24.9 %collective-permute-done.2 = bf16[256,1152]{1,0:T(8,128)(2,1)S(1)} collective-permute-done((bf16[256,1152]{1,0:T(8,128)(2,1)S(1)}, bf16[256,1152]{1,0:T(8,128)(2,1)S(1)}, u32[]{:S(2)}, u32[]{:S(2)}) %collective-permute-start.2) | collective-permute-done | bytes 589856 | tf_op jit(solution)/shard_map/ppermute | solution.py:511
  436.3 2.8 collective-permute-done.4
  439.2 1.1 pad_maximum_fusion.1.refs_0_
  440.3 92.1 %layer_chunk.5 = (bf16[3072,576]{1,0:T(8,128)(2,1)}, f32[4608,128]{1,0:T(8,128)}, f32[4,72,4992]{2,1,0:T(8,128)}, f32[4,72,4992]{2,1,0:T(8,128)}, f32[4,192,576]{2,1,0:T(8,128)}, /*index=5*/f32[4,192,576]{2,1,0:T(8,128)}) custom-call(bf16[512,1152]{1,0:T(8,128)(2,1)} %pad_maximum_fusion.1.refs_0_, ...), custom_call_target="tpu_custom_call", output_to_operand_aliasing={{0}: (10, {})} | custom-call | flops 24000000000 | bytes 55000000 | tf_op jit(solution)/shard_map/layer_chunk/pallas_call | solution.py:483
  532.5 0.5 collective-permute-start.13
  533.6 11.5 %collective-permute-done.13 = f32[4,192,576]{2,1,0:T(8,128)} collective-permute-done((f32[4,192,576]{2,1,0:T(8,128)}, f32[4,192,576]{2,1,0:T(8,128)}, u32[]{:S(2)}, u32[]{:S(2)}) %collective-permute-start.13) | collective-permute-done | bytes 1769504 | tf_op jit(solution)/shard_map/ppermute | solution.py:511
  545.0 1.8 add.215
  547.1 0.5 collective-permute-start.14
  547.7 6.1 copy.71
  554.3 17.2 %collective-permute-done.14 = f32[2,96,576]{2,1,0:T(8,128)S(1)} collective-permute-done((f32[2,96,576]{2,1,0:T(8,128)S(1)}, f32[2,96,576]{2,1,0:T(8,128)S(1)}, u32[]{:S(2)}, u32[]{:S(2)}) %collective-permute-start.14) | collective-permute-done | bytes 442400 | tf_op jit(solution)/shard_map/ppermute | solution.py:511
  571.5 4.9 add.210
  576.8 0.6 collective-permute-start.9
  577.3 1.5 collective-permute-start.15
  578.9 0.5 collective-permute-start.17
  579.4 68.6 %collective-permute-done.15 = f32[96,576]{1,0:T(8,128)S(1)} collective-permute-done((f32[96,576]{1,0:T(8,128)S(1)}, f32[96,576]{1,0:T(8,128)S(1)}, u32[]{:S(2)}, u32[]{:S(2)}) %collective-permute-start.15) | collective-permute-done | bytes 221216 | tf_op jit(solution)/shard_map/ppermute | solution.py:511
  648.6 0.8 pad_maximum_fusion.2
  649.7 2.0 collective-permute-start.10
  651.7 32.0 %collective-permute-done.11 = f32[2,72,2560]{2,1,0:T(8,128)S(1)} collective-permute-done((f32[2,72,2560]{2,1,0:T(8,128)S(1)}, f32[2,72,2560]{2,1,0:T(8,128)S(1)}, u32[]{:S(2)}, u32[]{:S(2)}) %collective-permute-start.11) | collective-permute-done | bytes 1474592 | tf_op jit(solution)/shard_map/ppermute | solution.py:511
  684.0 0.8 collective-permute-start.12
  684.8 8.8 %collective-permute-done.10 = f32[72,2432]{1,0:T(8,128)S(1)} collective-permute-done((f32[72,2432]{1,0:T(8,128)S(1)}, f32[72,2432]{1,0:T(8,128)S(1)}, u32[]{:S(2)}, u32[]{:S(2)}) %collective-permute-start.10) | collective-permute-done | bytes 700448 | tf_op jit(solution)/shard_map/ppermute | solution.py:511
  693.7 0.7 slice_reduce_fusion
  694.4 0.6 slice_bitcast_fusion
  695.0 0.4 collective-permute-done.12
  695.5 0.7 fusion.83
  696.3 0.8 fusion.82
  697.0 1.0 fusion.84
  698.0 40.4 %scatter_rows.3.refs_0_ = f32[36960,128]{1,0:T(8,128)} custom-call(s32[8192]{0:T(1024)S(1)} %get-tuple-element.140.ids_ref, s32[512]{0:T(512)S(1)} %convert_bitcast_fusion.clash_ref, f32[36864,128]{1,0:T(8,128)} %all-gather.13.cloned.1.call-done.rows_ref), custom_call_target="tpu_custom_call" | custom-call | flops 20000000000 | bytes 60000000 | tf_op jit(solution)/shard_map/scatter_rows/pallas_call | solution.py:446
  738.5 46.2 %scatter_rows.4.refs_0_ = f32[36960,128]{1,0:T(8,128)} custom-call(s32[8192]{0:T(1024)S(1)} %get-tuple-element.154.ids_ref, s32[512]{0:T(512)S(1)} %convert_bitcast_fusion.1.clash_ref, f32[36864,128]{1,0:T(8,128)} %all-gather.11.cloned.1.call-done.rows_ref, f32[36960,128]{1,0:T(8,128)} %scatter_rows.3.refs_0_), custom_call_target="tpu_custom_call", output_to_operand_aliasing={{}: (3, {})} | custom-call | flops 20000000000 | bytes 60000000 | tf_op jit(solution)/shard_map/scatter_rows/pallas_call | solution.py:446
  784.7 49.2 %scatter_rows.5 = f32[576,6144]{1,0:T(8,128)} custom-call(s32[8192]{0:T(1024)S(1)} %get-tuple-element.152.ids_ref, s32[512]{0:T(512)S(1)} %convert_bitcast_fusion.2.clash_ref, f32[36864,128]{1,0:T(8,128)} %all-gather.9.cloned.1.call-done.rows_ref, f32[36960,128]{1,0:T(8,128)} %scatter_rows.4.refs_0_), custom_call_target="tpu_custom_call" | custom-call | flops 20000000000 | bytes 60000000 | tf_op jit(solution)/shard_map/scatter_rows/pallas_call | solution.py:446
  (107 shorter events, 5.0 us)
Async XLA Ops:
  7.2 3.8 copy-start.8
  7.2 150.7 %all-gather.7.cloned.1.call-start = ((), (), s32[]{:S(2)}) async-start(), calls=%async_computation.2 | async-start | bytes 6303744 | tf_op jit(solution)/shard_map/all_gather | solution.py:552
  10.9 148.7 %reduce-scatter.5.cloned.1.call-start = ((), (), s32[]{:S(2)}) async-start(), calls=%async_computation.4 | async-start | bytes 10616832 | tf_op jit(solution)/shard_map/reduce_scatter | solution.py:589
  25.8 0.6 copy-start.3
  25.8 0.6 copy-start.5
  55.0 192.3 %reduce-scatter.3.cloned.1.call-start = ((), (), s32[]{:S(2)}) async-start(), calls=%async_computation.3 | async-start | bytes 10616832 | tf_op jit(solution)/shard_map/reduce_scatter | solution.py:589
  101.0 2.2 copy-start
  103.2 0.9 copy-start.7
  103.2 0.9 copy-start.9
  103.3 594.8 %all-gather.13.cloned.1.call-start = ((), (), s32[]{:S(2)}) async-start(), calls=%async_computation.7 | async-start | bytes 21233664 | tf_op jit(solution)/shard_map/all_gather | solution.py:599
  104.2 6.2 collective-permute-start.5
  104.2 6.1 copy-start.10
  104.2 6.1 copy-start.11
  110.5 22.1 %collective-permute-start.6 = (bf16[384,576]{1,0:T(8,128)(2,1)S(1)}, bf16[384,576]{1,0:T(8,128)(2,1)S(1)}, u32[]{:S(2)}, u32[]{:S(2)}) collective-permute-start(bf16[384,576]{1,0:T(8,128)(2,1)S(1)} %maximum_select_fusion.2), channel_id=1, source_target_pairs={{0,2},{1,3},{2,0},{3,1},{4,6},{5,7},{6,4},{7,5}} | collective-permute-start | bytes 1327112 | tf_op jit(solution)/shard_map/ppermute | solution.py:511
  133.6 21.6 %collective-permute-start.7 = (bf16[768,576]{0,1:T(8,128)(2,1)S(1)}, bf16[768,576]{0,1:T(8,128)(2,1)S(1)}, u32[]{:S(2)}, u32[]{:S(2)}) collective-permute-start(bf16[768,576]{0,1:T(8,128)(2,1)S(1)} %copy.67), channel_id=1, source_target_pairs={{0,4},{1,5},{2,6},{3,7},{4,0},{5,1},{6,2},{7,3}} | collective-permute-start | bytes 2654216 | tf_op jit(solution)/shard_map/ppermute | solution.py:511
  247.2 491.2 %all-gather.11.cloned.1.call-start = ((), (), s32[]{:S(2)}) async-start(), calls=%async_computation.6 | async-start | bytes 21233664 | tf_op jit(solution)/shard_map/all_gather | solution.py:599
  339.5 445.2 %all-gather.9.cloned.1.call-start = ((), (), s32[]{:S(2)}) async-start(), calls=%async_computation.5 | async-start | bytes 21233664 | tf_op jit(solution)/shard_map/all_gather | solution.py:599
  339.6 8.3 collective-permute-start
  354.5 1.5 copy-start.1
  357.1 48.9 %collective-permute-start.1 = (bf16[2,256,1152]{2,1,0:T(8,128)(2,1)}, bf16[2,256,1152]{2,1,0:T(8,128)(2,1)}, u32[]{:S(2)}, u32[]{:S(2)}) collective-permute-start(bf16[2,256,1152]{2,1,0:T(8,128)(2,1)} %dynamic-slice_bitcast_fusion.3), channel_id=1, source_target_pairs={{0,2},{1,3},{2,0},{3,1},{4,6},{5,7},{6,4},{7,5}} | collective-permute-start | bytes 3538952 | tf_op jit(solution)/shard_map/ppermute | solution.py:511
  359.0 50.4 %collective-permute-start.3 = (bf16[2,256,1152]{2,1,0:T(8,128)(2,1)}, bf16[2,256,1152]{2,1,0:T(8,128)(2,1)}, u32[]{:S(2)}, u32[]{:S(2)}) collective-permute-start(bf16[2,256,1152]{2,1,0:T(8,128)(2,1)} %dynamic-slice_bitcast_fusion.2), channel_id=1, source_target_pairs={{0,4},{1,5},{2,6},{3,7},{4,0},{5,1},{6,2},{7,3}} | collective-permute-start | bytes 3538952 | tf_op jit(solution)/shard_map/ppermute | solution.py:511
  407.9 28.4 %collective-permute-start.2 = (bf16[256,1152]{1,0:T(8,128)(2,1)S(1)}, bf16[256,1152]{1,0:T(8,128)(2,1)S(1)}, u32[]{:S(2)}, u32[]{:S(2)}) collective-permute-start(bf16[256,1152]{1,0:T(8,128)(2,1)S(1)} %dynamic-slice_bitcast_fusion.7), channel_id=1, source_target_pairs={{0,4},{1,5},{2,6},{3,7},{4,0},{5,1},{6,2},{7,3}} | collective-permute-start | bytes 1769480 | tf_op jit(solution)/shard_map/ppermute | solution.py:511
  410.8 28.3 %collective-permute-start.4 = (bf16[256,1152]{1,0:T(8,128)(2,1)S(1)}, bf16[256,1152]{1,0:T(8,128)(2,1)S(1)}, u32[]{:S(2)}, u32[]{:S(2)}) collective-permute-start(bf16[256,1152]{1,0:T(8,128)(2,1)S(1)} %dynamic-slice_bitcast_fusion.6), channel_id=1, source_target_pairs={{0,2},{1,3},{2,0},{3,1},{4,6},{5,7},{6,4},{7,5}} | collective-permute-start | bytes 1769480 | tf_op jit(solution)/shard_map/ppermute | solution.py:511
  532.4 0.8 copy-start.6
  532.4 0.8 copy-start.4
  532.5 12.6 %copy-start.2 = (f32[4,192,576]{2,1,0:T(8,128)S(1)}, f32[4,192,576]{2,1,0:T(8,128)}, u32[]{:S(2)}) copy-start(f32[4,192,576]{2,1,0:T(8,128)} %get-tuple-element.45) | copy-start | bytes 5308420
  532.5 39.1 %collective-permute-start.8 = (f32[4,72,4992]{2,1,0:T(8,128)}, f32[4,72,4992]{2,1,0:T(8,128)}, u32[]{:S(2)}, u32[]{:S(2)}) collective-permute-start(f32[4,72,4992]{2,1,0:T(8,128)} %get-tuple-element.44), channel_id=1, source_target_pairs={{0,1},{1,0},{2,3},{3,2},{4,5},{5,4},{6,7},{7,6}} | collective-permute-start | bytes 17252360 | tf_op jit(solution)/shard_map/ppermute | solution.py:511
  532.5 12.5 %collective-permute-start.13 = (f32[4,192,576]{2,1,0:T(8,128)}, f32[4,192,576]{2,1,0:T(8,128)}, u32[]{:S(2)}, u32[]{:S(2)}) collective-permute-start(f32[4,192,576]{2,1,0:T(8,128)} %get-tuple-element.46), channel_id=1, source_target_pairs={{0,1},{1,0},{2,3},{3,2},{4,5},{5,4},{6,7},{7,6}} | collective-permute-start | bytes 5308424 | tf_op jit(solution)/shard_map/ppermute | solution.py:511
  547.1 24.4 %collective-permute-start.14 = (f32[2,96,576]{2,1,0:T(8,128)S(1)}, f32[2,96,576]{2,1,0:T(8,128)S(1)}, u32[]{:S(2)}, u32[]{:S(2)}) collective-permute-start(f32[2,96,576]{2,1,0:T(8,128)S(1)} %dynamic-slice_bitcast_fusion.9), channel_id=1, source_target_pairs={{0,2},{1,3},{2,0},{3,1},{4,6},{5,7},{6,4},{7,5}} | collective-permute-start | bytes 1327112 | tf_op jit(solution)/shard_map/ppermute | solution.py:511
  553.9 25.0 %collective-permute-start.16 = (f32[2,96,576]{2,1,0:T(8,128)S(1)}, f32[2,96,576]{2,1,0:T(8,128)S(1)}, u32[]{:S(2)}, u32[]{:S(2)}) collective-permute-start(f32[2,96,576]{2,1,0:T(8,128)S(1)} %dynamic-slice_bitcast_fusion.8), channel_id=1, source_target_pairs={{0,4},{1,5},{2,6},{3,7},{4,0},{5,1},{6,2},{7,3}} | collective-permute-start | bytes 1327112 | tf_op jit(solution)/shard_map/ppermute | solution.py:511
  576.8 72.7 %collective-permute-start.9 = (f32[2,72,2432]{2,1,0:T(8,128)S(1)}, f32[2,72,2432]{2,1,0:T(8,128)S(1)}, u32[]{:S(2)}, u32[]{:S(2)}) collective-permute-start(f32[2,72,2432]{2,1,0:T(8,128)S(1)} %dynamic-slice_bitcast_fusion.1), channel_id=1, source_target_pairs={{0,4},{1,5},{2,6},{3,7},{4,0},{5,1},{6,2},{7,3}} | collective-permute-start | bytes 4202504 | tf_op jit(solution)/shard_map/ppermute | solution.py:511
  577.3 70.7 %collective-permute-start.15 = (f32[96,576]{1,0:T(8,128)S(1)}, f32[96,576]{1,0:T(8,128)S(1)}, u32[]{:S(2)}, u32[]{:S(2)}) collective-permute-start(f32[96,576]{1,0:T(8,128)S(1)} %dynamic-slice_bitcast_fusion.11), channel_id=1, source_target_pairs={{0,4},{1,5},{2,6},{3,7},{4,0},{5,1},{6,2},{7,3}} | collective-permute-start | bytes 663560 | tf_op jit(solution)/shard_map/ppermute | solution.py:511
  578.9 69.7 %collective-permute-start.17 = (f32[96,576]{1,0:T(8,128)S(1)}, f32[96,576]{1,0:T(8,128)S(1)}, u32[]{:S(2)}, u32[]{:S(2)}) collective-permute-start(f32[96,576]{1,0:T(8,128)S(1)} %dynamic-slice_bitcast_fusion.10), channel_id=1, source_target_pairs={{0,2},{1,3},{2,0},{3,1},{4,6},{5,7},{6,4},{7,5}} | collective-permute-start | bytes 663560 | tf_op jit(solution)/shard_map/ppermute | solution.py:511
  648.6 35.2 %collective-permute-start.11 = (f32[2,72,2560]{2,1,0:T(8,128)S(1)}, f32[2,72,2560]{2,1,0:T(8,128)S(1)}, u32[]{:S(2)}, u32[]{:S(2)}) collective-permute-start(f32[2,72,2560]{2,1,0:T(8,128)S(1)} %dynamic-slice_bitcast_fusion), channel_id=1, source_target_pairs={{0,2},{1,3},{2,0},{3,1},{4,6},{5,7},{6,4},{7,5}} | collective-permute-start | bytes 4423688 | tf_op jit(solution)/shard_map/ppermute | solution.py:511
  649.7 43.9 %collective-permute-start.10 = (f32[72,2432]{1,0:T(8,128)S(1)}, f32[72,2432]{1,0:T(8,128)S(1)}, u32[]{:S(2)}, u32[]{:S(2)}) collective-permute-start(f32[72,2432]{1,0:T(8,128)S(1)} %dynamic-slice_bitcast_fusion.5), channel_id=1, source_target_pairs={{0,2},{1,3},{2,0},{3,1},{4,6},{5,7},{6,4},{7,5}} | collective-permute-start | bytes 2101256 | tf_op jit(solution)/shard_map/ppermute | solution.py:511
  684.0 11.5 %collective-permute-start.12 = (f32[72,2560]{1,0:T(8,128)S(1)}, f32[72,2560]{1,0:T(8,128)S(1)}, u32[]{:S(2)}, u32[]{:S(2)}) collective-permute-start(f32[72,2560]{1,0:T(8,128)S(1)} %dynamic-slice_bitcast_fusion.4), channel_id=1, source_target_pairs={{0,4},{1,5},{2,6},{3,7},{4,0},{5,1},{6,2},{7,3}} | collective-permute-start | bytes 2211848 | tf_op jit(solution)/shard_map/ppermute | solution.py:511
Sparse Core Ops, SparseCore 0:
  11.0 40.0 all-gather.6
  55.2 77.0 reduce-scatter.4
  135.7 69.7 reduce-scatter.2
  247.3 93.1 all-gather.12
  342.2 126.9 all-gather.10
  532.6 134.7 all-gather.8

commit v4 on v3

--- a/solution.py
+++ b/solution.py
@@ -46,12 +46,12 @@
     head_f = head_ext.astype(F32)
     inv = lax.rsqrt(jnp.sum(head_f * head_f, axis=-1, keepdims=True) * (1.0 / LANES) + NORM_EPS)
     turned = head_f * inv * gain_ext * cs
-    return turned + pltpu.roll(turned, 64, 1), inv
+    return turned + pltpu.roll(turned, HEAD, 1), inv
 
 
 def head_norm_rope_bwd(grad_ext, head_ext, inv, gain_low, cs_bwd, low):
     turned = grad_ext * cs_bwd
-    grad_t = turned + pltpu.roll(turned, 64, 1)
+    grad_t = turned + pltpu.roll(turned, HEAD, 1)
     normed = jnp.where(low, head_ext.astype(F32), 0.0) * inv
     grad_normed = grad_t * gain_low
     mean_term = jnp.sum(grad_normed * normed, axis=-1, keepdims=True) * (1.0 / HEAD)
@@ -63,7 +63,7 @@
     for idx in range(0, len(heads), 2):
         tile = heads[idx]
         if idx + 1 < len(heads):
-            tile = tile + pltpu.roll(heads[idx + 1], 64, 1)
+            tile = tile + pltpu.roll(heads[idx + 1], HEAD, 1)
         tiles.append(tile.astype(BF))
     return tiles
 
@@ -76,9 +76,9 @@
         refs = refs[3:]
     y_ref, dx_ref = refs[:2]
     outs = refs[2:6] if last else refs[2:4]
-    (acc, accd, norm_acc, head_acc, wx, wox, qkv_s, upper_s, lower_s, tbuf, sems) = refs[2 + len(outs):]
+    (acc, accd, norm_acc, head_acc, wx, wox, qkv_s, upper_s, lower_s, cs_s, tbuf, sems) = refs[2 + len(outs):]
     step = pl.program_id(0)
-    low = lax.broadcasted_iota(jnp.int32, (1, LANES), 1) < 64
+    low = lax.broadcasted_iota(jnp.int32, (1, LANES), 1) < HEAD
 
     @pl.when(step == 0)
     def _():
@@ -94,7 +94,7 @@
         head_acc[...] = jnp.zeros_like(head_acc)
         for h in range(HEADS + 2 * KV):
             tile = w_ref[:, (h // 2) * LANES:(h // 2) * LANES + LANES].astype(F32)
-            moved = pltpu.roll(tile, 64, 1)
+            moved = pltpu.roll(tile, HEAD, 1)
             if h >= HEADS + KV:
                 both = jnp.where(low, moved if h % 2 else tile, 0.0)
             else:
@@ -102,8 +102,8 @@
                 both = jnp.where(low, twice, pltpu.roll(twice, 32, 1))
             wx[:, h * LANES:h * LANES + LANES] = both.astype(BF)
         for h in range(HEADS):
-            wox[h * LANES:h * LANES + 64, :] = w_ref[h * 64:h * 64 + 64, C_OUT:C_OUT + D]
-            wox[h * LANES + 64:h * LANES + LANES, :] = jnp.zeros((64, D), BF)
+            wox[h * LANES:h * LANES + HEAD, :] = w_ref[h * HEAD:h * HEAD + HEAD, C_OUT:C_OUT + D]
+            wox[h * LANES + HEAD:h * LANES + LANES, :] = jnp.zeros((HEAD, D), BF)
         if not first:
             load_acc.wait()
             load_accd.wait()
@@ -129,12 +129,15 @@
         expd = jnp.exp(scores - jnp.max(scores, axis=-1, keepdims=True))
         return expd * (1.0 / jnp.sum(expd, axis=-1, keepdims=True))
 
+    cos_t, sin_t = cs_ref[:HEAD // 2, :], cs_ref[HEAD // 2:, :]
+    cs_s[...] = jnp.concatenate([cos_t, cos_t, -sin_t, sin_t], axis=0).T
+
     parts = []
     for s in range(SEQS):
         pairs = x_ref[s * HALF_SEQ:(s + 1) * HALF_SEQ, :].astype(F32)
         tails = pairs[:, 512:640]
-        parts.append(jnp.concatenate([pairs[:, :512], tails[:, :64]], axis=1))
-        parts.append(jnp.concatenate([pairs[:, 640:], pltpu.roll(tails, 64, 1)[:, :64]], axis=1))
+        parts.append(jnp.concatenate([pairs[:, :512], tails[:, :HEAD]], axis=1))
+        parts.append(jnp.concatenate([pairs[:, 640:], pltpu.roll(tails, HEAD, 1)[:, :HEAD]], axis=1))
     x = jnp.concatenate(parts, axis=0)
     inv1 = lax.rsqrt(jnp.mean(x * x, axis=-1, keepdims=True) + NORM_EPS)
     m1 = (x * inv1 * gain1).astype(BF)
@@ -142,7 +145,7 @@
     saved, packed = [], []
     for s in range(SEQS):
         rows = slice(s * SEQ, (s + 1) * SEQ)
-        cs = cs_ref[rows, :]
+        cs = cs_s[...]
         heads = []
         for g in range(KV):
             ke = qkv_s[rows, X_K + g * LANES:X_K + (g + 1) * LANES]
@@ -172,9 +175,9 @@
     inv2 = lax.rsqrt(jnp.mean(hidden * hidden, axis=-1, keepdims=True) + NORM_EPS)
     m2 = (hidden * inv2 * gain2).astype(BF)
 
-    dy = dy_ref[...]
+    dy_t = dy_ref[...]
+    dy = dy_t.T
     m2_t = m2.T
-    dy_t = dy.T
     y = hidden
     dm2 = jnp.zeros((SEQS * SEQ, D), F32)
     for f in range(0, FF, FF_STEP):
@@ -205,7 +208,7 @@
     packed = []
     for s in range(SEQS):
         rows = slice(s * SEQ, (s + 1) * SEQ)
-        cs = cs_ref[rows, :]
+        cs = cs_s[...]
         cs_bwd = jnp.where(low, cs, -cs)
         dqs, dks, dvs = [], [], []
         for g in range(KV):
@@ -258,7 +261,7 @@
             acc[c:c + width, C_NORM:C_NORM + LANES] += both[:, c:c + width].T
         head_q = jnp.sum(head_acc[0], axis=0, keepdims=True)
         head_k = jnp.sum(head_acc[1], axis=0, keepdims=True)
-        head_row = jnp.where(low, head_q, pltpu.roll(head_k, 64, 1))
+        head_row = jnp.where(low, head_q, pltpu.roll(head_k, HEAD, 1))
         acc[:, C_HEAD:C_HEAD + LANES] += jnp.broadcast_to(head_row, (D, LANES))
         if last:
             mine = core_ref[0]
@@ -334,7 +337,7 @@
             for j in range(4):
                 out[:, j * LANES:j * LANES + LANES] = buf[pl.ds(j, HALF_SEQ, stride=ROW_WORDS), :].astype(BF)
                 out[:, 640 + j * LANES:768 + j * LANES] = buf[pl.ds(half + j, HALF_SEQ, stride=ROW_WORDS), :].astype(BF)
-            tails = buf[pl.ds(4, HALF_SEQ, stride=ROW_WORDS), :] + pltpu.roll(buf[pl.ds(half + 4, HALF_SEQ, stride=ROW_WORDS), :], 64, 1)
+            tails = buf[pl.ds(4, HALF_SEQ, stride=ROW_WORDS), :] + pltpu.roll(buf[pl.ds(half + 4, HALF_SEQ, stride=ROW_WORDS), :], HEAD, 1)
             out[:, 512:640] = tails.astype(BF)
 
         first += count
@@ -417,8 +420,8 @@
                 for r in range(0, wide, LANES):
                     for j in range(4):
                         tbuf[slot, j * LANES:j * LANES + LANES, r:r + LANES] = word(1 + j, r).T
-                    tail = word(5, r) + pltpu.roll(word(0, r), 64, 1)
-                    tbuf[slot, 512:D, r:r + LANES] = tail.T[:64]
+                    tail = word(5, r) + pltpu.roll(word(0, r), HEAD, 1)
+                    tbuf[slot, 512:D, r:r + LANES] = tail.T[:HEAD]
                 store.start()
                 return 0
 
@@ -467,7 +470,7 @@
     whole = lambda shape: pl.BlockSpec(shape, lambda i: (0,) * len(shape), pipeline_mode=pl.Buffered(1))
     here = lambda cols: pl.BlockSpec((SEQS * SEQ, cols), lambda i: (i + start, 0))
     anyspec = pl.BlockSpec(memory_space=pl.ANY)
-    in_specs = [pl.BlockSpec((SEQS * HALF_SEQ, 2 * D), lambda i: (i, 0)), here(D), here(LANES), whole(w_pack.shape), whole(w_down.shape), whole(gains.shape), whole(head_gains.shape), pl.BlockSpec(memory_space=pltpu.SMEM)]
+    in_specs = [pl.BlockSpec((SEQS * HALF_SEQ, 2 * D), lambda i: (i, 0)), pl.BlockSpec((D, SEQ), lambda i: (i + start, 0)), pl.BlockSpec((HEAD, SEQ), lambda i: (0, i + start)), whole(w_pack.shape), whole(w_down.shape), whole(gains.shape), whole(head_gains.shape), pl.BlockSpec(memory_space=pltpu.SMEM)]
     args = [x, dy, cs, w_pack, w_down, gains, head_gains, core]
     aliases = {}
     if not first:
@@ -496,6 +499,7 @@
             pltpu.VMEM((SEQS * SEQ, X_COLS), BF),
             pltpu.VMEM((SEQS * KV, GRP * HALF_SEQ, HALF_SEQ), F32),
             pltpu.VMEM((SEQS * KV, GRP * HALF_SEQ, SEQ), F32),
+            pltpu.VMEM((SEQ, LANES), F32),
             pltpu.VMEM((FF // 2, D) if last else (8, LANES), F32),
             pltpu.SemaphoreType.DMA((2,)),
         ],
@@ -547,7 +551,7 @@
         shard = w_query.shape[0]
         all_ids = lax.all_gather(tokens, AXIS_NAME)
         norms = jnp.concatenate([attn_norm[:, None], mlp_norm[:, None], jnp.zeros((shard, W_COLS - C_NORM - 2), BF)], axis=1)
-        pad = jnp.zeros((shard, 64), BF)
+        pad = jnp.zeros((shard, HEAD), BF)
         packed = jnp.concatenate([w_query, w_key, w_value, pad, w_out, pad, w_gate, w_up, norms], axis=1)
         w_pack = lax.all_gather(packed, AXIS_NAME, tiled=True)
         w_down_full = gather_by_swaps(w_down)
@@ -557,10 +561,9 @@
         head_gains = jnp.concatenate([head_gains, swapped], axis=1)
 
         inv_freq = jnp.exp(jnp.arange(HEAD // 2, dtype=F32) * (-2.0 * math.log(ROPE_THETA) / HEAD))
-        angles = positions.reshape(-1, 1).astype(F32) * inv_freq
-        cos_t, sin_t = jnp.cos(angles), jnp.sin(angles)
-        cs = jnp.concatenate([cos_t, cos_t, -sin_t, sin_t], axis=1)
-        dy = dy_out.reshape(-1, D)
+        angles = inv_freq[:, None] * positions.reshape(1, -1).astype(F32)
+        cs = jnp.concatenate([jnp.cos(angles), jnp.sin(angles)], axis=0)
+        dy_t = dy_out.swapaxes(1, 2).reshape(-1, seq_len)
 
         starts = [sum(CHUNKS[:c]) for c in range(len(CHUNKS))]
         take_from, add_to, clashes = [], [], []
@@ -595,7 +598,7 @@
         rows_of = []
         for idx in range(len(CHUNKS)):
             x_chunk = xs[idx]
-            dx, carry = layer_chunk(x_chunk, dy, cs, w_pack, w_down_full, gains, head_gains, core, starts[idx], carry, idx == len(CHUNKS) - 1, batch_len * seq_len)
+            dx, carry = layer_chunk(x_chunk, dy_t, cs, w_pack, w_down_full, gains, head_gains, core, starts[idx], carry, idx == len(CHUNKS) - 1, batch_len * seq_len)
             rows_of.append(lax.all_gather(dx, AXIS_NAME, tiled=True))
         *grads, y = carry
         d_table = None

time: 848 us -> 842 us (level)
    unnamed x30 -> x29, local copies, waits for them, and re-layouts: 18.3 us -> 12.1 us
  transfers between devices with their start and end apart: 24 -> 24, of which waited for: 12 -> 13; matrix products, arithmetic and copies ran while one was open for 6% -> 5% of each run, Pallas kernels for 51% -> 52%
where the time goes in v4:
time: 842 us; the launch traced here: 837 us
  Pallas kernels  485 us (58%)
  waiting for transfers between devices  260 us (31%)
  other arithmetic  26.6 us (3%)
  local copies, waits for them, and re-layouts  23.7 us (3%)
  between operations  15 us (2%)
  blocking collectives  14.8 us (2%)
  starting transfers between devices  11.6 us (1%)
    pallas_call x3, Pallas kernels, layer_chunk(): pl.pallas_call(functools.partial(layer_kernel, first, last, steps), grid=...  275 us
    ppermute x18, waiting for transfers between devices, swap_with(): return lax.ppermute(values, AXIS_NAME, [(i, i ^ bit) for i in range(8)])  260 us
    pallas_call x3, Pallas kernels, scatter_rows(): pl.pallas_call(functools.partial(scatter_kernel, first, last, blocks), gr...  136 us
    pallas_call x2, Pallas kernels, gather_rows(): pl.pallas_call(functools.partial(gather_kernel, blocks), grid_spec=pltpu....  74.3 us
  transfers between devices with their start and end apart: 24, of which 13 were waited for; matrix products, arithmetic and copies ran while one was open for 5% of the time, Pallas kernels for 52%

profile of v4, /device:TPU:0, one launch (start us, length us, event | category | flops | bytes accessed | tf_op | source)
XLA Modules:
  0.0 837.1 jit_solution(2986238062622635896)
XLA Ops:
  7.2 0.8 copy.53
  8.0 0.8 copy.54
  8.8 2.1 concatenate.51
  11.0 14.8 %all-gather.1 = s32[8,12,256]{2,1,0:T(8,128)S(1)} all-gather(s32[1,12,256]{2,1,0:T(8,128)S(1)} %bitcast.124), channel_id=2, replica_groups=mesh['fsdp'=8] {'fsdp'}, dimensions={0}, use_global_device_ids=true | all-gather | bytes 110592 | tf_op jit(solution)/shard_map/all_gather | solution.py:552
  25.9 0.5 copy-done.3
  26.5 28.4 %gather_rows.3 = bf16[4096,1152]{1,0:T(8,128)(2,1)} custom-call(s32[8192]{0:T(1024)S(1)} %get-tuple-element.128.ids_ref, bf16[576,6144]{1,0:T(8,128)(2,1)} %bitcast.132), custom_call_target="tpu_custom_call" | custom-call | flops 40000000000 | bytes 40000000 | tf_op jit(solution)/shard_map/gather_rows/pallas_call | solution.py:350
  55.2 45.9 %gather_rows.2 = (bf16[4096,1152]{1,0:T(8,128)(2,1)}, bf16[2048,1152]{1,0:T(8,128)(2,1)S(1)}, bf16[2048,1152]{1,0:T(8,128)(2,1)}) custom-call(s32[16384]{0:T(1024)S(1)} %pad_add_fusion.ids_ref, bf16[576,6144]{1,0:T(8,128)(2,1)} %bitcast.133), custom_call_target="tpu_custom_call" | custom-call | flops 40000000000 | bytes 40000000 | tf_op jit(solution)/shard_map/gather_rows/pallas_call | solution.py:350
  101.0 2.2 copy-done
  103.3 0.9 copy-done.7
  104.2 1.5 collective-permute-done.5
  106.0 0.6 pad_maximum_fusion.4.refs_6_
  106.6 23.0 %collective-permute-done.6 = bf16[384,576]{1,0:T(8,128)(2,1)S(1)} collective-permute-done((bf16[384,576]{1,0:T(8,128)(2,1)S(1)}, bf16[384,576]{1,0:T(8,128)(2,1)S(1)}, u32[]{:S(2)}, u32[]{:S(2)}) %collective-permute-start.6) | collective-permute-done | bytes 442400 | tf_op jit(solution)/shard_map/ppermute | solution.py:515
  130.0 0.6 copy.55
  130.6 1.4 multiply_cosine_fusion
  132.0 0.9 pad_maximum_fusion.1.refs_2_
  133.0 16.9 %collective-permute-done.7 = bf16[768,576]{0,1:T(8,128)(2,1)S(1)} collective-permute-done((bf16[768,576]{0,1:T(8,128)(2,1)S(1)}, bf16[768,576]{0,1:T(8,128)(2,1)S(1)}, u32[]{:S(2)}, u32[]{:S(2)}) %collective-permute-start.7) | collective-permute-done | bytes 884768 | tf_op jit(solution)/shard_map/ppermute | solution.py:515
  149.9 0.6 copy.56
  150.5 2.0 maximum_select_fusion.refs_4_
  152.5 0.9 slice_convert_fusion
  153.5 0.7 copy.64
  154.2 88.9 %layer_chunk.3 = (bf16[3072,576]{1,0:T(8,128)(2,1)}, f32[4608,128]{1,0:T(8,128)}, f32[576,4992]{1,0:T(8,128)}, f32[576,1536]{1,0:T(8,128)}) custom-call(bf16[512,1152]{1,0:T(8,128)(2,1)} %reduce-scatter.5.cloned.1.call-done.refs_0_, bf16[6912,256]{1,0:T(8,128)(2,1)} %bitcast.135, f32[64,3072]{1,0:T(8,128)} %pad_maximum_fusion.1.refs_2_, ...), custom_call_target="tpu_custom_call" | custom-call | flops 24000000000 | bytes 55000000 | tf_op jit(solution)/shard_map/layer_chunk/pallas_call | solution.py:486
  243.2 92.9 %layer_chunk.4 = (bf16[3072,576]{1,0:T(8,128)(2,1)}, f32[4608,128]{1,0:T(8,128)}, f32[576,4992]{1,0:T(8,128)}, f32[576,1536]{1,0:T(8,128)}) custom-call(bf16[512,1152]{1,0:T(8,128)(2,1)} %reduce-scatter.3.cloned.1.call-done.refs_0_, bf16[6912,256]{1,0:T(8,128)(2,1)} %bitcast.136, ...), custom_call_target="tpu_custom_call", output_to_operand_aliasing={{2}: (8, {}), {3}: (9, {}), {0}: (10, {})} | custom-call | flops 24000000000 | bytes 55000000 | tf_op jit(solution)/shard_map/layer_chunk/pallas_call | solution.py:486
  336.2 8.2 collective-permute-done
  344.5 5.7 add.190
  350.2 0.4 fusion.79
  350.6 1.4 copy-done.1
  352.0 1.1 dynamic-slice_bitcast_fusion.3
  353.1 1.2 collective-permute-start.1
  354.3 1.1 dynamic-slice_bitcast_fusion.2
  355.4 1.1 collective-permute-start.3
  356.6 44.6 %collective-permute-done.1 = bf16[2,256,1152]{2,1,0:T(8,128)(2,1)} collective-permute-done((bf16[2,256,1152]{2,1,0:T(8,128)(2,1)}, bf16[2,256,1152]{2,1,0:T(8,128)(2,1)}, u32[]{:S(2)}, u32[]{:S(2)}) %collective-permute-start.1) | collective-permute-done | bytes 1179680 | tf_op jit(solution)/shard_map/ppermute | solution.py:515
  401.2 1.8 bitcast_add_fusion.3
  403.0 1.5 collective-permute-start.2
  404.5 1.5 bitcast_add_fusion.2
  406.1 0.5 collective-permute-start.4
  406.6 24.8 %collective-permute-done.2 = bf16[256,1152]{1,0:T(8,128)(2,1)S(1)} collective-permute-done((bf16[256,1152]{1,0:T(8,128)(2,1)S(1)}, bf16[256,1152]{1,0:T(8,128)(2,1)S(1)}, u32[]{:S(2)}, u32[]{:S(2)}) %collective-permute-start.2) | collective-permute-done | bytes 589856 | tf_op jit(solution)/shard_map/ppermute | solution.py:515
  431.5 2.8 collective-permute-done.4
  434.4 1.1 pad_maximum_fusion.refs_0_
  435.6 93.0 %layer_chunk.5 = (bf16[3072,576]{1,0:T(8,128)(2,1)}, f32[4608,128]{1,0:T(8,128)}, f32[4,72,4992]{2,1,0:T(8,128)}, f32[4,72,4992]{2,1,0:T(8,128)}, f32[4,192,576]{2,1,0:T(8,128)}, /*index=5*/f32[4,192,576]{2,1,0:T(8,128)}) custom-call(bf16[512,1152]{1,0:T(8,128)(2,1)} %pad_maximum_fusion.refs_0_, ...), custom_call_target="tpu_custom_call", output_to_operand_aliasing={{0}: (10, {})} | custom-call | flops 24000000000 | bytes 55000000 | tf_op jit(solution)/shard_map/layer_chunk/pallas_call | solution.py:486
  528.7 0.5 collective-permute-start.13
  529.7 11.5 %collective-permute-done.13 = f32[4,192,576]{2,1,0:T(8,128)} collective-permute-done((f32[4,192,576]{2,1,0:T(8,128)}, f32[4,192,576]{2,1,0:T(8,128)}, u32[]{:S(2)}, u32[]{:S(2)}) %collective-permute-start.13) | collective-permute-done | bytes 1769504 | tf_op jit(solution)/shard_map/ppermute | solution.py:515
  541.2 1.8 add.215
  543.2 0.5 collective-permute-start.14
  543.8 6.1 copy.59
  550.4 17.2 %collective-permute-done.14 = f32[2,96,576]{2,1,0:T(8,128)S(1)} collective-permute-done((f32[2,96,576]{2,1,0:T(8,128)S(1)}, f32[2,96,576]{2,1,0:T(8,128)S(1)}, u32[]{:S(2)}, u32[]{:S(2)}) %collective-permute-start.14) | collective-permute-done | bytes 442400 | tf_op jit(solution)/shard_map/ppermute | solution.py:515
  567.7 4.9 add.210
  572.9 0.6 collective-permute-start.9
  573.5 1.5 collective-permute-start.15
  575.1 0.5 collective-permute-start.17
  575.6 68.5 %collective-permute-done.15 = f32[96,576]{1,0:T(8,128)S(1)} collective-permute-done((f32[96,576]{1,0:T(8,128)S(1)}, f32[96,576]{1,0:T(8,128)S(1)}, u32[]{:S(2)}, u32[]{:S(2)}) %collective-permute-start.15) | collective-permute-done | bytes 221216 | tf_op jit(solution)/shard_map/ppermute | solution.py:515
  644.7 0.8 pad_maximum_fusion.2
  645.8 2.0 collective-permute-start.10
  647.8 32.0 %collective-permute-done.11 = f32[2,72,2560]{2,1,0:T(8,128)S(1)} collective-permute-done((f32[2,72,2560]{2,1,0:T(8,128)S(1)}, f32[2,72,2560]{2,1,0:T(8,128)S(1)}, u32[]{:S(2)}, u32[]{:S(2)}) %collective-permute-start.11) | collective-permute-done | bytes 1474592 | tf_op jit(solution)/shard_map/ppermute | solution.py:515
  680.1 0.9 collective-permute-start.12
  680.9 8.8 %collective-permute-done.10 = f32[72,2432]{1,0:T(8,128)S(1)} collective-permute-done((f32[72,2432]{1,0:T(8,128)S(1)}, f32[72,2432]{1,0:T(8,128)S(1)}, u32[]{:S(2)}, u32[]{:S(2)}) %collective-permute-start.10) | collective-permute-done | bytes 700448 | tf_op jit(solution)/shard_map/ppermute | solution.py:515
  689.8 0.7 slice_reduce_fusion
  690.5 0.6 slice_bitcast_fusion
  691.1 0.4 collective-permute-done.12
  691.6 0.7 fusion.82
  692.4 0.8 fusion.81
  693.1 1.0 fusion.83
  694.1 40.4 %scatter_rows.3.refs_0_ = f32[36960,128]{1,0:T(8,128)} custom-call(s32[8192]{0:T(1024)S(1)} %get-tuple-element.127.ids_ref, s32[512]{0:T(512)S(1)} %convert_bitcast_fusion.clash_ref, f32[36864,128]{1,0:T(8,128)} %all-gather.13.cloned.1.call-done.rows_ref), custom_call_target="tpu_custom_call" | custom-call | flops 20000000000 | bytes 60000000 | tf_op jit(solution)/shard_map/scatter_rows/pallas_call | solution.py:449
  734.5 46.2 %scatter_rows.4.refs_0_ = f32[36960,128]{1,0:T(8,128)} custom-call(s32[8192]{0:T(1024)S(1)} %get-tuple-element.140.ids_ref, s32[512]{0:T(512)S(1)} %convert_bitcast_fusion.1.clash_ref, f32[36864,128]{1,0:T(8,128)} %all-gather.11.cloned.1.call-done.rows_ref, f32[36960,128]{1,0:T(8,128)} %scatter_rows.3.refs_0_), custom_call_target="tpu_custom_call", output_to_operand_aliasing={{}: (3, {})} | custom-call | flops 20000000000 | bytes 60000000 | tf_op jit(solution)/shard_map/scatter_rows/pallas_call | solution.py:449
  780.8 49.2 %scatter_rows.5 = f32[576,6144]{1,0:T(8,128)} custom-call(s32[8192]{0:T(1024)S(1)} %get-tuple-element.138.ids_ref, s32[512]{0:T(512)S(1)} %convert_bitcast_fusion.2.clash_ref, f32[36864,128]{1,0:T(8,128)} %all-gather.9.cloned.1.call-done.rows_ref, f32[36960,128]{1,0:T(8,128)} %scatter_rows.4.refs_0_), custom_call_target="tpu_custom_call" | custom-call | flops 20000000000 | bytes 60000000 | tf_op jit(solution)/shard_map/scatter_rows/pallas_call | solution.py:449
  (106 shorter events, 4.6 us)
Async XLA Ops:
  7.2 3.8 copy-start.8
  7.2 145.3 %all-gather.7.cloned.1.call-start = ((), (), s32[]{:S(2)}) async-start(), calls=%async_computation.2 | async-start | bytes 6303744 | tf_op jit(solution)/shard_map/all_gather | solution.py:556
  10.9 143.3 %reduce-scatter.5.cloned.1.call-start = ((), (), s32[]{:S(2)}) async-start(), calls=%async_computation.4 | async-start | bytes 10616832 | tf_op jit(solution)/shard_map/reduce_scatter | solution.py:592
  25.8 0.6 copy-start.3
  25.8 0.6 copy-start.5
  55.0 188.2 %reduce-scatter.3.cloned.1.call-start = ((), (), s32[]{:S(2)}) async-start(), calls=%async_computation.3 | async-start | bytes 10616832 | tf_op jit(solution)/shard_map/reduce_scatter | solution.py:592
  101.0 2.2 copy-start
  103.2 0.9 copy-start.7
  103.2 0.9 copy-start.9
  103.2 1.0 copy-start.10
  103.2 1.0 copy-start.11
  103.3 590.8 %all-gather.13.cloned.1.call-start = ((), (), s32[]{:S(2)}) async-start(), calls=%async_computation.7 | async-start | bytes 21233664 | tf_op jit(solution)/shard_map/all_gather | solution.py:602
  104.2 1.5 collective-permute-start.5
  105.8 23.7 %collective-permute-start.6 = (bf16[384,576]{1,0:T(8,128)(2,1)S(1)}, bf16[384,576]{1,0:T(8,128)(2,1)S(1)}, u32[]{:S(2)}, u32[]{:S(2)}) collective-permute-start(bf16[384,576]{1,0:T(8,128)(2,1)S(1)} %maximum_select_fusion.2), channel_id=1, source_target_pairs={{0,2},{1,3},{2,0},{3,1},{4,6},{5,7},{6,4},{7,5}} | collective-permute-start | bytes 1327112 | tf_op jit(solution)/shard_map/ppermute | solution.py:515
  130.6 19.3 %collective-permute-start.7 = (bf16[768,576]{0,1:T(8,128)(2,1)S(1)}, bf16[768,576]{0,1:T(8,128)(2,1)S(1)}, u32[]{:S(2)}, u32[]{:S(2)}) collective-permute-start(bf16[768,576]{0,1:T(8,128)(2,1)S(1)} %copy.55), channel_id=1, source_target_pairs={{0,4},{1,5},{2,6},{3,7},{4,0},{5,1},{6,2},{7,3}} | collective-permute-start | bytes 2654216 | tf_op jit(solution)/shard_map/ppermute | solution.py:515
  243.1 491.4 %all-gather.11.cloned.1.call-start = ((), (), s32[]{:S(2)}) async-start(), calls=%async_computation.6 | async-start | bytes 21233664 | tf_op jit(solution)/shard_map/all_gather | solution.py:602
  336.1 444.6 %all-gather.9.cloned.1.call-start = ((), (), s32[]{:S(2)}) async-start(), calls=%async_computation.5 | async-start | bytes 21233664 | tf_op jit(solution)/shard_map/all_gather | solution.py:602
  336.2 8.3 collective-permute-start
  350.6 1.4 copy-start.1
  353.1 48.1 %collective-permute-start.1 = (bf16[2,256,1152]{2,1,0:T(8,128)(2,1)}, bf16[2,256,1152]{2,1,0:T(8,128)(2,1)}, u32[]{:S(2)}, u32[]{:S(2)}) collective-permute-start(bf16[2,256,1152]{2,1,0:T(8,128)(2,1)} %dynamic-slice_bitcast_fusion.3), channel_id=1, source_target_pairs={{0,2},{1,3},{2,0},{3,1},{4,6},{5,7},{6,4},{7,5}} | collective-permute-start | bytes 3538952 | tf_op jit(solution)/shard_map/ppermute | solution.py:515
  355.4 49.1 %collective-permute-start.3 = (bf16[2,256,1152]{2,1,0:T(8,128)(2,1)}, bf16[2,256,1152]{2,1,0:T(8,128)(2,1)}, u32[]{:S(2)}, u32[]{:S(2)}) collective-permute-start(bf16[2,256,1152]{2,1,0:T(8,128)(2,1)} %dynamic-slice_bitcast_fusion.2), channel_id=1, source_target_pairs={{0,4},{1,5},{2,6},{3,7},{4,0},{5,1},{6,2},{7,3}} | collective-permute-start | bytes 3538952 | tf_op jit(solution)/shard_map/ppermute | solution.py:515
  403.0 28.4 %collective-permute-start.2 = (bf16[256,1152]{1,0:T(8,128)(2,1)S(1)}, bf16[256,1152]{1,0:T(8,128)(2,1)S(1)}, u32[]{:S(2)}, u32[]{:S(2)}) collective-permute-start(bf16[256,1152]{1,0:T(8,128)(2,1)S(1)} %dynamic-slice_bitcast_fusion.7), channel_id=1, source_target_pairs={{0,4},{1,5},{2,6},{3,7},{4,0},{5,1},{6,2},{7,3}} | collective-permute-start | bytes 1769480 | tf_op jit(solution)/shard_map/ppermute | solution.py:515
  406.1 28.3 %collective-permute-start.4 = (bf16[256,1152]{1,0:T(8,128)(2,1)S(1)}, bf16[256,1152]{1,0:T(8,128)(2,1)S(1)}, u32[]{:S(2)}, u32[]{:S(2)}) collective-permute-start(bf16[256,1152]{1,0:T(8,128)(2,1)S(1)} %dynamic-slice_bitcast_fusion.6), channel_id=1, source_target_pairs={{0,2},{1,3},{2,0},{3,1},{4,6},{5,7},{6,4},{7,5}} | collective-permute-start | bytes 1769480 | tf_op jit(solution)/shard_map/ppermute | solution.py:515
  528.6 0.8 copy-start.6
  528.6 0.8 copy-start.4
  528.6 12.6 %copy-start.2 = (f32[4,192,576]{2,1,0:T(8,128)S(1)}, f32[4,192,576]{2,1,0:T(8,128)}, u32[]{:S(2)}) copy-start(f32[4,192,576]{2,1,0:T(8,128)} %get-tuple-element.45) | copy-start | bytes 5308420
  528.6 39.1 %collective-permute-start.8 = (f32[4,72,4992]{2,1,0:T(8,128)}, f32[4,72,4992]{2,1,0:T(8,128)}, u32[]{:S(2)}, u32[]{:S(2)}) collective-permute-start(f32[4,72,4992]{2,1,0:T(8,128)} %get-tuple-element.44), channel_id=1, source_target_pairs={{0,1},{1,0},{2,3},{3,2},{4,5},{5,4},{6,7},{7,6}} | collective-permute-start | bytes 17252360 | tf_op jit(solution)/shard_map/ppermute | solution.py:515
  528.7 12.5 %collective-permute-start.13 = (f32[4,192,576]{2,1,0:T(8,128)}, f32[4,192,576]{2,1,0:T(8,128)}, u32[]{:S(2)}, u32[]{:S(2)}) collective-permute-start(f32[4,192,576]{2,1,0:T(8,128)} %get-tuple-element.46), channel_id=1, source_target_pairs={{0,1},{1,0},{2,3},{3,2},{4,5},{5,4},{6,7},{7,6}} | collective-permute-start | bytes 5308424 | tf_op jit(solution)/shard_map/ppermute | solution.py:515
  543.2 24.4 %collective-permute-start.14 = (f32[2,96,576]{2,1,0:T(8,128)S(1)}, f32[2,96,576]{2,1,0:T(8,128)S(1)}, u32[]{:S(2)}, u32[]{:S(2)}) collective-permute-start(f32[2,96,576]{2,1,0:T(8,128)S(1)} %dynamic-slice_bitcast_fusion.9), channel_id=1, source_target_pairs={{0,2},{1,3},{2,0},{3,1},{4,6},{5,7},{6,4},{7,5}} | collective-permute-start | bytes 1327112 | tf_op jit(solution)/shard_map/ppermute | solution.py:515
  550.0 25.0 %collective-permute-start.16 = (f32[2,96,576]{2,1,0:T(8,128)S(1)}, f32[2,96,576]{2,1,0:T(8,128)S(1)}, u32[]{:S(2)}, u32[]{:S(2)}) collective-permute-start(f32[2,96,576]{2,1,0:T(8,128)S(1)} %dynamic-slice_bitcast_fusion.8), channel_id=1, source_target_pairs={{0,4},{1,5},{2,6},{3,7},{4,0},{5,1},{6,2},{7,3}} | collective-permute-start | bytes 1327112 | tf_op jit(solution)/shard_map/ppermute | solution.py:515
  572.9 72.7 %collective-permute-start.9 = (f32[2,72,2432]{2,1,0:T(8,128)S(1)}, f32[2,72,2432]{2,1,0:T(8,128)S(1)}, u32[]{:S(2)}, u32[]{:S(2)}) collective-permute-start(f32[2,72,2432]{2,1,0:T(8,128)S(1)} %dynamic-slice_bitcast_fusion.1), channel_id=1, source_target_pairs={{0,4},{1,5},{2,6},{3,7},{4,0},{5,1},{6,2},{7,3}} | collective-permute-start | bytes 4202504 | tf_op jit(solution)/shard_map/ppermute | solution.py:515
  573.5 70.6 %collective-permute-start.15 = (f32[96,576]{1,0:T(8,128)S(1)}, f32[96,576]{1,0:T(8,128)S(1)}, u32[]{:S(2)}, u32[]{:S(2)}) collective-permute-start(f32[96,576]{1,0:T(8,128)S(1)} %dynamic-slice_bitcast_fusion.11), channel_id=1, source_target_pairs={{0,4},{1,5},{2,6},{3,7},{4,0},{5,1},{6,2},{7,3}} | collective-permute-start | bytes 663560 | tf_op jit(solution)/shard_map/ppermute | solution.py:515
  575.1 69.6 %collective-permute-start.17 = (f32[96,576]{1,0:T(8,128)S(1)}, f32[96,576]{1,0:T(8,128)S(1)}, u32[]{:S(2)}, u32[]{:S(2)}) collective-permute-start(f32[96,576]{1,0:T(8,128)S(1)} %dynamic-slice_bitcast_fusion.10), channel_id=1, source_target_pairs={{0,2},{1,3},{2,0},{3,1},{4,6},{5,7},{6,4},{7,5}} | collective-permute-start | bytes 663560 | tf_op jit(solution)/shard_map/ppermute | solution.py:515
  644.6 35.2 %collective-permute-start.11 = (f32[2,72,2560]{2,1,0:T(8,128)S(1)}, f32[2,72,2560]{2,1,0:T(8,128)S(1)}, u32[]{:S(2)}, u32[]{:S(2)}) collective-permute-start(f32[2,72,2560]{2,1,0:T(8,128)S(1)} %dynamic-slice_bitcast_fusion), channel_id=1, source_target_pairs={{0,2},{1,3},{2,0},{3,1},{4,6},{5,7},{6,4},{7,5}} | collective-permute-start | bytes 4423688 | tf_op jit(solution)/shard_map/ppermute | solution.py:515
  645.8 43.9 %collective-permute-start.10 = (f32[72,2432]{1,0:T(8,128)S(1)}, f32[72,2432]{1,0:T(8,128)S(1)}, u32[]{:S(2)}, u32[]{:S(2)}) collective-permute-start(f32[72,2432]{1,0:T(8,128)S(1)} %dynamic-slice_bitcast_fusion.5), channel_id=1, source_target_pairs={{0,2},{1,3},{2,0},{3,1},{4,6},{5,7},{6,4},{7,5}} | collective-permute-start | bytes 2101256 | tf_op jit(solution)/shard_map/ppermute | solution.py:515
  680.1 11.5 %collective-permute-start.12 = (f32[72,2560]{1,0:T(8,128)S(1)}, f32[72,2560]{1,0:T(8,128)S(1)}, u32[]{:S(2)}, u32[]{:S(2)}) collective-permute-start(f32[72,2560]{1,0:T(8,128)S(1)} %dynamic-slice_bitcast_fusion.4), channel_id=1, source_target_pairs={{0,4},{1,5},{2,6},{3,7},{4,0},{5,1},{6,2},{7,3}} | collective-permute-start | bytes 2211848 | tf_op jit(solution)/shard_map/ppermute | solution.py:515
Sparse Core Ops, SparseCore 0:
  11.0 40.0 all-gather.6
  55.2 78.1 reduce-scatter.4
  136.8 68.4 reduce-scatter.2
  243.2 92.6 all-gather.12
  337.6 126.1 all-gather.10
  528.7 134.7 all-gather.8

commit v5 on v4

--- a/solution.py
+++ b/solution.py
@@ -24,6 +24,7 @@
 W_COLS, G_COLS = 4864, 4992
 X_K, X_V, X_COLS = HEADS * LANES, (HEADS + KV) * LANES, (HEADS + 2 * KV) * LANES
 FF_STEP = 512
+DOWN = FF // 8
 CHUNKS = (4, 4, 4)
 PAIR_WORDS = 9
 BF, F32 = jnp.bfloat16, jnp.float32
@@ -279,13 +280,11 @@
 
             stores = [send_block(d, acc.at[pl.ds(d * 72, 72), :], outs[0], outs[1], sems.at[0]) for d in range(8)]
             for part in range(0, 8, 4):
-                moved = []
-                for d in range(4):
-                    f = (part + d) * 192
+                for c in range(0, 4 * DOWN, LANES):
                     for t in range(0, D, LANES):
                         width = min(LANES, D - t)
-                        tbuf[d * 192:d * 192 + 192, t:t + width] = accd[t:t + width, f:f + 192].T
-                    moved.append(send_block(part + d, tbuf.at[pl.ds(d * 192, 192), :], outs[2], outs[3], sems.at[1]))
+                        tbuf[c:c + LANES, t:t + width] = accd[t:t + width, part * DOWN + c:part * DOWN + c + LANES].T
+                moved = [send_block(part + d, tbuf.at[pl.ds(d * DOWN, DOWN), :], outs[2], outs[3], sems.at[1]) for d in range(4)]
                 for store in moved:
                     store.wait()
         else:
@@ -481,7 +480,7 @@
         jax.ShapeDtypeStruct((total, D), BF),
         jax.ShapeDtypeStruct((steps * SEQS * HALF_SEQ * PAIR_WORDS, LANES), F32),
     ]
-    grad_shapes = [(4, 72, G_COLS)] * 2 + [(4, 192, D)] * 2 if last else [(D, G_COLS), (D, FF)]
+    grad_shapes = [(4, 72, G_COLS)] * 2 + [(4, DOWN, D)] * 2 if last else [(D, G_COLS), (D, FF)]
     out_shape += [jax.ShapeDtypeStruct(shape, F32) for shape in grad_shapes]
     y, dx, *grads = pl.pallas_call(
         functools.partial(layer_kernel, first, last, steps),

time: 842 us -> 842 us (level)
  no operation moved by 1% of the time
where the time goes in v5:
time: 842 us; the launch traced here: 837 us
  Pallas kernels  485 us (58%)
  waiting for transfers between devices  260 us (31%)
  other arithmetic  26.6 us (3%)
  local copies, waits for them, and re-layouts  23.7 us (3%)
  between operations  15 us (2%)
  blocking collectives  14.8 us (2%)
  starting transfers between devices  11.6 us (1%)
    pallas_call x3, Pallas kernels, layer_chunk(): pl.pallas_call(functools.partial(layer_kernel, first, last, steps), grid=...  274 us
    ppermute x18, waiting for transfers between devices, swap_with(): return lax.ppermute(values, AXIS_NAME, [(i, i ^ bit) for i in range(8)])  260 us
    pallas_call x3, Pallas kernels, scatter_rows(): pl.pallas_call(functools.partial(scatter_kernel, first, last, blocks), gr...  136 us
    pallas_call x2, Pallas kernels, gather_rows(): pl.pallas_call(functools.partial(gather_kernel, blocks), grid_spec=pltpu....  74.3 us
  transfers between devices with their start and end apart: 24, of which 13 were waited for; matrix products, arithmetic and copies ran while one was open for 5% of the time, Pallas kernels for 52%

profile of v5, /device:TPU:0, one launch (start us, length us, event | category | flops | bytes accessed | tf_op | source)
XLA Modules:
  0.0 836.8 jit_solution(6299459512231369896)
XLA Ops:
  7.2 0.8 copy.53
  8.0 0.8 copy.54
  8.8 2.1 concatenate.51
  11.0 14.8 %all-gather.1 = s32[8,12,256]{2,1,0:T(8,128)S(1)} all-gather(s32[1,12,256]{2,1,0:T(8,128)S(1)} %bitcast.124), channel_id=2, replica_groups=mesh['fsdp'=8] {'fsdp'}, dimensions={0}, use_global_device_ids=true | all-gather | bytes 110592 | tf_op jit(solution)/shard_map/all_gather | solution.py:551
  25.9 0.5 copy-done.3
  26.5 28.4 %gather_rows.3 = bf16[4096,1152]{1,0:T(8,128)(2,1)} custom-call(s32[8192]{0:T(1024)S(1)} %get-tuple-element.128.ids_ref, bf16[576,6144]{1,0:T(8,128)(2,1)} %bitcast.132), custom_call_target="tpu_custom_call" | custom-call | flops 40000000000 | bytes 40000000 | tf_op jit(solution)/shard_map/gather_rows/pallas_call | solution.py:349
  55.2 45.9 %gather_rows.2 = (bf16[4096,1152]{1,0:T(8,128)(2,1)}, bf16[2048,1152]{1,0:T(8,128)(2,1)S(1)}, bf16[2048,1152]{1,0:T(8,128)(2,1)}) custom-call(s32[16384]{0:T(1024)S(1)} %pad_add_fusion.ids_ref, bf16[576,6144]{1,0:T(8,128)(2,1)} %bitcast.133), custom_call_target="tpu_custom_call" | custom-call | flops 40000000000 | bytes 40000000 | tf_op jit(solution)/shard_map/gather_rows/pallas_call | solution.py:349
  101.0 2.2 copy-done
  103.3 0.9 copy-done.7
  104.2 1.5 collective-permute-done.5
  106.0 0.6 pad_maximum_fusion.4.refs_6_
  106.6 23.0 %collective-permute-done.6 = bf16[384,576]{1,0:T(8,128)(2,1)S(1)} collective-permute-done((bf16[384,576]{1,0:T(8,128)(2,1)S(1)}, bf16[384,576]{1,0:T(8,128)(2,1)S(1)}, u32[]{:S(2)}, u32[]{:S(2)}) %collective-permute-start.6) | collective-permute-done | bytes 442400 | tf_op jit(solution)/shard_map/ppermute | solution.py:514
  130.0 0.6 copy.55
  130.6 1.4 multiply_cosine_fusion
  132.0 0.9 pad_maximum_fusion.1.refs_2_
  133.0 16.9 %collective-permute-done.7 = bf16[768,576]{0,1:T(8,128)(2,1)S(1)} collective-permute-done((bf16[768,576]{0,1:T(8,128)(2,1)S(1)}, bf16[768,576]{0,1:T(8,128)(2,1)S(1)}, u32[]{:S(2)}, u32[]{:S(2)}) %collective-permute-start.7) | collective-permute-done | bytes 884768 | tf_op jit(solution)/shard_map/ppermute | solution.py:514
  149.9 0.6 copy.56
  150.5 2.0 maximum_select_fusion.refs_4_
  152.5 0.9 slice_convert_fusion
  153.5 0.7 copy.64
  154.2 88.9 %layer_chunk.3 = (bf16[3072,576]{1,0:T(8,128)(2,1)}, f32[4608,128]{1,0:T(8,128)}, f32[576,4992]{1,0:T(8,128)}, f32[576,1536]{1,0:T(8,128)}) custom-call(bf16[512,1152]{1,0:T(8,128)(2,1)} %reduce-scatter.5.cloned.1.call-done.refs_0_, bf16[6912,256]{1,0:T(8,128)(2,1)} %bitcast.135, f32[64,3072]{1,0:T(8,128)} %pad_maximum_fusion.1.refs_2_, ...), custom_call_target="tpu_custom_call" | custom-call | flops 24000000000 | bytes 55000000 | tf_op jit(solution)/shard_map/layer_chunk/pallas_call | solution.py:485
  243.2 92.9 %layer_chunk.4 = (bf16[3072,576]{1,0:T(8,128)(2,1)}, f32[4608,128]{1,0:T(8,128)}, f32[576,4992]{1,0:T(8,128)}, f32[576,1536]{1,0:T(8,128)}) custom-call(bf16[512,1152]{1,0:T(8,128)(2,1)} %reduce-scatter.3.cloned.1.call-done.refs_0_, bf16[6912,256]{1,0:T(8,128)(2,1)} %bitcast.136, ...), custom_call_target="tpu_custom_call", output_to_operand_aliasing={{2}: (8, {}), {3}: (9, {}), {0}: (10, {})} | custom-call | flops 24000000000 | bytes 55000000 | tf_op jit(solution)/shard_map/layer_chunk/pallas_call | solution.py:485
  336.2 8.2 collective-permute-done
  344.5 5.7 add.190
  350.2 0.4 fusion.79
  350.6 1.4 copy-done.1
  352.0 1.1 dynamic-slice_bitcast_fusion.3
  353.1 1.2 collective-permute-start.1
  354.3 1.1 dynamic-slice_bitcast_fusion.2
  355.4 1.1 collective-permute-start.3
  356.6 44.6 %collective-permute-done.1 = bf16[2,256,1152]{2,1,0:T(8,128)(2,1)} collective-permute-done((bf16[2,256,1152]{2,1,0:T(8,128)(2,1)}, bf16[2,256,1152]{2,1,0:T(8,128)(2,1)}, u32[]{:S(2)}, u32[]{:S(2)}) %collective-permute-start.1) | collective-permute-done | bytes 1179680 | tf_op jit(solution)/shard_map/ppermute | solution.py:514
  401.2 1.8 bitcast_add_fusion.3
  403.0 1.5 collective-permute-start.2
  404.5 1.5 bitcast_add_fusion.2
  406.1 0.5 collective-permute-start.4
  406.6 24.8 %collective-permute-done.2 = bf16[256,1152]{1,0:T(8,128)(2,1)S(1)} collective-permute-done((bf16[256,1152]{1,0:T(8,128)(2,1)S(1)}, bf16[256,1152]{1,0:T(8,128)(2,1)S(1)}, u32[]{:S(2)}, u32[]{:S(2)}) %collective-permute-start.2) | collective-permute-done | bytes 589856 | tf_op jit(solution)/shard_map/ppermute | solution.py:514
  431.5 2.8 collective-permute-done.4
  434.4 1.1 pad_maximum_fusion.refs_0_
  435.6 92.6 %layer_chunk.5 = (bf16[3072,576]{1,0:T(8,128)(2,1)}, f32[4608,128]{1,0:T(8,128)}, f32[4,72,4992]{2,1,0:T(8,128)}, f32[4,72,4992]{2,1,0:T(8,128)}, f32[4,192,576]{2,1,0:T(8,128)}, /*index=5*/f32[4,192,576]{2,1,0:T(8,128)}) custom-call(bf16[512,1152]{1,0:T(8,128)(2,1)} %pad_maximum_fusion.refs_0_, ...), custom_call_target="tpu_custom_call", output_to_operand_aliasing={{0}: (10, {})} | custom-call | flops 24000000000 | bytes 55000000 | tf_op jit(solution)/shard_map/layer_chunk/pallas_call | solution.py:485
  528.3 0.5 collective-permute-start.13
  529.4 11.5 %collective-permute-done.13 = f32[4,192,576]{2,1,0:T(8,128)} collective-permute-done((f32[4,192,576]{2,1,0:T(8,128)}, f32[4,192,576]{2,1,0:T(8,128)}, u32[]{:S(2)}, u32[]{:S(2)}) %collective-permute-start.13) | collective-permute-done | bytes 1769504 | tf_op jit(solution)/shard_map/ppermute | solution.py:514
  540.8 1.8 add.215
  542.9 0.5 collective-permute-start.14
  543.5 6.1 copy.59
  550.1 17.2 %collective-permute-done.14 = f32[2,96,576]{2,1,0:T(8,128)S(1)} collective-permute-done((f32[2,96,576]{2,1,0:T(8,128)S(1)}, f32[2,96,576]{2,1,0:T(8,128)S(1)}, u32[]{:S(2)}, u32[]{:S(2)}) %collective-permute-start.14) | collective-permute-done | bytes 442400 | tf_op jit(solution)/shard_map/ppermute | solution.py:514
  567.3 4.9 add.210
  572.5 0.6 collective-permute-start.9
  573.2 1.5 collective-permute-start.15
  574.7 0.5 collective-permute-start.17
  575.3 68.5 %collective-permute-done.15 = f32[96,576]{1,0:T(8,128)S(1)} collective-permute-done((f32[96,576]{1,0:T(8,128)S(1)}, f32[96,576]{1,0:T(8,128)S(1)}, u32[]{:S(2)}, u32[]{:S(2)}) %collective-permute-start.15) | collective-permute-done | bytes 221216 | tf_op jit(solution)/shard_map/ppermute | solution.py:514
  644.4 0.8 pad_maximum_fusion.2
  645.4 2.0 collective-permute-start.10
  647.4 32.0 %collective-permute-done.11 = f32[2,72,2560]{2,1,0:T(8,128)S(1)} collective-permute-done((f32[2,72,2560]{2,1,0:T(8,128)S(1)}, f32[2,72,2560]{2,1,0:T(8,128)S(1)}, u32[]{:S(2)}, u32[]{:S(2)}) %collective-permute-start.11) | collective-permute-done | bytes 1474592 | tf_op jit(solution)/shard_map/ppermute | solution.py:514
  679.7 0.9 collective-permute-start.12
  680.6 8.8 %collective-permute-done.10 = f32[72,2432]{1,0:T(8,128)S(1)} collective-permute-done((f32[72,2432]{1,0:T(8,128)S(1)}, f32[72,2432]{1,0:T(8,128)S(1)}, u32[]{:S(2)}, u32[]{:S(2)}) %collective-permute-start.10) | collective-permute-done | bytes 700448 | tf_op jit(solution)/shard_map/ppermute | solution.py:514
  689.5 0.7 slice_reduce_fusion
  690.2 0.6 slice_bitcast_fusion
  690.7 0.4 collective-permute-done.12
  691.3 0.7 fusion.82
  692.0 0.8 fusion.81
  692.8 1.0 fusion.83
  693.8 40.4 %scatter_rows.3.refs_0_ = f32[36960,128]{1,0:T(8,128)} custom-call(s32[8192]{0:T(1024)S(1)} %get-tuple-element.127.ids_ref, s32[512]{0:T(512)S(1)} %convert_bitcast_fusion.clash_ref, f32[36864,128]{1,0:T(8,128)} %all-gather.13.cloned.1.call-done.rows_ref), custom_call_target="tpu_custom_call" | custom-call | flops 20000000000 | bytes 60000000 | tf_op jit(solution)/shard_map/scatter_rows/pallas_call | solution.py:448
  734.2 46.2 %scatter_rows.4.refs_0_ = f32[36960,128]{1,0:T(8,128)} custom-call(s32[8192]{0:T(1024)S(1)} %get-tuple-element.140.ids_ref, s32[512]{0:T(512)S(1)} %convert_bitcast_fusion.1.clash_ref, f32[36864,128]{1,0:T(8,128)} %all-gather.11.cloned.1.call-done.rows_ref, f32[36960,128]{1,0:T(8,128)} %scatter_rows.3.refs_0_), custom_call_target="tpu_custom_call", output_to_operand_aliasing={{}: (3, {})} | custom-call | flops 20000000000 | bytes 60000000 | tf_op jit(solution)/shard_map/scatter_rows/pallas_call | solution.py:448
  780.4 49.2 %scatter_rows.5 = f32[576,6144]{1,0:T(8,128)} custom-call(s32[8192]{0:T(1024)S(1)} %get-tuple-element.138.ids_ref, s32[512]{0:T(512)S(1)} %convert_bitcast_fusion.2.clash_ref, f32[36864,128]{1,0:T(8,128)} %all-gather.9.cloned.1.call-done.rows_ref, f32[36960,128]{1,0:T(8,128)} %scatter_rows.4.refs_0_), custom_call_target="tpu_custom_call" | custom-call | flops 20000000000 | bytes 60000000 | tf_op jit(solution)/shard_map/scatter_rows/pallas_call | solution.py:448
  (106 shorter events, 4.6 us)
Async XLA Ops:
  7.2 3.8 copy-start.8
  7.2 145.3 %all-gather.7.cloned.1.call-start = ((), (), s32[]{:S(2)}) async-start(), calls=%async_computation.2 | async-start | bytes 6303744 | tf_op jit(solution)/shard_map/all_gather | solution.py:555
  10.9 143.3 %reduce-scatter.5.cloned.1.call-start = ((), (), s32[]{:S(2)}) async-start(), calls=%async_computation.4 | async-start | bytes 10616832 | tf_op jit(solution)/shard_map/reduce_scatter | solution.py:591
  25.8 0.6 copy-start.3
  25.8 0.6 copy-start.5
  55.0 188.2 %reduce-scatter.3.cloned.1.call-start = ((), (), s32[]{:S(2)}) async-start(), calls=%async_computation.3 | async-start | bytes 10616832 | tf_op jit(solution)/shard_map/reduce_scatter | solution.py:591
  101.0 2.2 copy-start
  103.2 0.9 copy-start.7
  103.2 0.9 copy-start.9
  103.2 1.0 copy-start.10
  103.2 1.0 copy-start.11
  103.3 590.5 %all-gather.13.cloned.1.call-start = ((), (), s32[]{:S(2)}) async-start(), calls=%async_computation.7 | async-start | bytes 21233664 | tf_op jit(solution)/shard_map/all_gather | solution.py:601
  104.2 1.5 collective-permute-start.5
  105.8 23.7 %collective-permute-start.6 = (bf16[384,576]{1,0:T(8,128)(2,1)S(1)}, bf16[384,576]{1,0:T(8,128)(2,1)S(1)}, u32[]{:S(2)}, u32[]{:S(2)}) collective-permute-start(bf16[384,576]{1,0:T(8,128)(2,1)S(1)} %maximum_select_fusion.2), channel_id=1, source_target_pairs={{0,2},{1,3},{2,0},{3,1},{4,6},{5,7},{6,4},{7,5}} | collective-permute-start | bytes 1327112 | tf_op jit(solution)/shard_map/ppermute | solution.py:514
  130.6 19.3 %collective-permute-start.7 = (bf16[768,576]{0,1:T(8,128)(2,1)S(1)}, bf16[768,576]{0,1:T(8,128)(2,1)S(1)}, u32[]{:S(2)}, u32[]{:S(2)}) collective-permute-start(bf16[768,576]{0,1:T(8,128)(2,1)S(1)} %copy.55), channel_id=1, source_target_pairs={{0,4},{1,5},{2,6},{3,7},{4,0},{5,1},{6,2},{7,3}} | collective-permute-start | bytes 2654216 | tf_op jit(solution)/shard_map/ppermute | solution.py:514
  243.1 491.1 %all-gather.11.cloned.1.call-start = ((), (), s32[]{:S(2)}) async-start(), calls=%async_computation.6 | async-start | bytes 21233664 | tf_op jit(solution)/shard_map/all_gather | solution.py:601
  336.1 444.3 %all-gather.9.cloned.1.call-start = ((), (), s32[]{:S(2)}) async-start(), calls=%async_computation.5 | async-start | bytes 21233664 | tf_op jit(solution)/shard_map/all_gather | solution.py:601
  336.2 8.3 collective-permute-start
  350.6 1.4 copy-start.1
  353.1 48.1 %collective-permute-start.1 = (bf16[2,256,1152]{2,1,0:T(8,128)(2,1)}, bf16[2,256,1152]{2,1,0:T(8,128)(2,1)}, u32[]{:S(2)}, u32[]{:S(2)}) collective-permute-start(bf16[2,256,1152]{2,1,0:T(8,128)(2,1)} %dynamic-slice_bitcast_fusion.3), channel_id=1, source_target_pairs={{0,2},{1,3},{2,0},{3,1},{4,6},{5,7},{6,4},{7,5}} | collective-permute-start | bytes 3538952 | tf_op jit(solution)/shard_map/ppermute | solution.py:514
  355.4 49.1 %collective-permute-start.3 = (bf16[2,256,1152]{2,1,0:T(8,128)(2,1)}, bf16[2,256,1152]{2,1,0:T(8,128)(2,1)}, u32[]{:S(2)}, u32[]{:S(2)}) collective-permute-start(bf16[2,256,1152]{2,1,0:T(8,128)(2,1)} %dynamic-slice_bitcast_fusion.2), channel_id=1, source_target_pairs={{0,4},{1,5},{2,6},{3,7},{4,0},{5,1},{6,2},{7,3}} | collective-permute-start | bytes 3538952 | tf_op jit(solution)/shard_map/ppermute | solution.py:514
  403.0 28.4 %collective-permute-start.2 = (bf16[256,1152]{1,0:T(8,128)(2,1)S(1)}, bf16[256,1152]{1,0:T(8,128)(2,1)S(1)}, u32[]{:S(2)}, u32[]{:S(2)}) collective-permute-start(bf16[256,1152]{1,0:T(8,128)(2,1)S(1)} %dynamic-slice_bitcast_fusion.7), channel_id=1, source_target_pairs={{0,4},{1,5},{2,6},{3,7},{4,0},{5,1},{6,2},{7,3}} | collective-permute-start | bytes 1769480 | tf_op jit(solution)/shard_map/ppermute | solution.py:514
  406.1 28.3 %collective-permute-start.4 = (bf16[256,1152]{1,0:T(8,128)(2,1)S(1)}, bf16[256,1152]{1,0:T(8,128)(2,1)S(1)}, u32[]{:S(2)}, u32[]{:S(2)}) collective-permute-start(bf16[256,1152]{1,0:T(8,128)(2,1)S(1)} %dynamic-slice_bitcast_fusion.6), channel_id=1, source_target_pairs={{0,2},{1,3},{2,0},{3,1},{4,6},{5,7},{6,4},{7,5}} | collective-permute-start | bytes 1769480 | tf_op jit(solution)/shard_map/ppermute | solution.py:514
  528.2 0.8 copy-start.6
  528.2 0.8 copy-start.4
  528.2 12.6 %copy-start.2 = (f32[4,192,576]{2,1,0:T(8,128)S(1)}, f32[4,192,576]{2,1,0:T(8,128)}, u32[]{:S(2)}) copy-start(f32[4,192,576]{2,1,0:T(8,128)} %get-tuple-element.45) | copy-start | bytes 5308420
  528.3 39.1 %collective-permute-start.8 = (f32[4,72,4992]{2,1,0:T(8,128)}, f32[4,72,4992]{2,1,0:T(8,128)}, u32[]{:S(2)}, u32[]{:S(2)}) collective-permute-start(f32[4,72,4992]{2,1,0:T(8,128)} %get-tuple-element.44), channel_id=1, source_target_pairs={{0,1},{1,0},{2,3},{3,2},{4,5},{5,4},{6,7},{7,6}} | collective-permute-start | bytes 17252360 | tf_op jit(solution)/shard_map/ppermute | solution.py:514
  528.3 12.5 %collective-permute-start.13 = (f32[4,192,576]{2,1,0:T(8,128)}, f32[4,192,576]{2,1,0:T(8,128)}, u32[]{:S(2)}, u32[]{:S(2)}) collective-permute-start(f32[4,192,576]{2,1,0:T(8,128)} %get-tuple-element.46), channel_id=1, source_target_pairs={{0,1},{1,0},{2,3},{3,2},{4,5},{5,4},{6,7},{7,6}} | collective-permute-start | bytes 5308424 | tf_op jit(solution)/shard_map/ppermute | solution.py:514
  542.9 24.4 %collective-permute-start.14 = (f32[2,96,576]{2,1,0:T(8,128)S(1)}, f32[2,96,576]{2,1,0:T(8,128)S(1)}, u32[]{:S(2)}, u32[]{:S(2)}) collective-permute-start(f32[2,96,576]{2,1,0:T(8,128)S(1)} %dynamic-slice_bitcast_fusion.9), channel_id=1, source_target_pairs={{0,2},{1,3},{2,0},{3,1},{4,6},{5,7},{6,4},{7,5}} | collective-permute-start | bytes 1327112 | tf_op jit(solution)/shard_map/ppermute | solution.py:514
  549.7 25.0 %collective-permute-start.16 = (f32[2,96,576]{2,1,0:T(8,128)S(1)}, f32[2,96,576]{2,1,0:T(8,128)S(1)}, u32[]{:S(2)}, u32[]{:S(2)}) collective-permute-start(f32[2,96,576]{2,1,0:T(8,128)S(1)} %dynamic-slice_bitcast_fusion.8), channel_id=1, source_target_pairs={{0,4},{1,5},{2,6},{3,7},{4,0},{5,1},{6,2},{7,3}} | collective-permute-start | bytes 1327112 | tf_op jit(solution)/shard_map/ppermute | solution.py:514
  572.5 72.7 %collective-permute-start.9 = (f32[2,72,2432]{2,1,0:T(8,128)S(1)}, f32[2,72,2432]{2,1,0:T(8,128)S(1)}, u32[]{:S(2)}, u32[]{:S(2)}) collective-permute-start(f32[2,72,2432]{2,1,0:T(8,128)S(1)} %dynamic-slice_bitcast_fusion.1), channel_id=1, source_target_pairs={{0,4},{1,5},{2,6},{3,7},{4,0},{5,1},{6,2},{7,3}} | collective-permute-start | bytes 4202504 | tf_op jit(solution)/shard_map/ppermute | solution.py:514
  573.2 70.6 %collective-permute-start.15 = (f32[96,576]{1,0:T(8,128)S(1)}, f32[96,576]{1,0:T(8,128)S(1)}, u32[]{:S(2)}, u32[]{:S(2)}) collective-permute-start(f32[96,576]{1,0:T(8,128)S(1)} %dynamic-slice_bitcast_fusion.11), channel_id=1, source_target_pairs={{0,4},{1,5},{2,6},{3,7},{4,0},{5,1},{6,2},{7,3}} | collective-permute-start | bytes 663560 | tf_op jit(solution)/shard_map/ppermute | solution.py:514
  574.7 69.6 %collective-permute-start.17 = (f32[96,576]{1,0:T(8,128)S(1)}, f32[96,576]{1,0:T(8,128)S(1)}, u32[]{:S(2)}, u32[]{:S(2)}) collective-permute-start(f32[96,576]{1,0:T(8,128)S(1)} %dynamic-slice_bitcast_fusion.10), channel_id=1, source_target_pairs={{0,2},{1,3},{2,0},{3,1},{4,6},{5,7},{6,4},{7,5}} | collective-permute-start | bytes 663560 | tf_op jit(solution)/shard_map/ppermute | solution.py:514
  644.3 35.2 %collective-permute-start.11 = (f32[2,72,2560]{2,1,0:T(8,128)S(1)}, f32[2,72,2560]{2,1,0:T(8,128)S(1)}, u32[]{:S(2)}, u32[]{:S(2)}) collective-permute-start(f32[2,72,2560]{2,1,0:T(8,128)S(1)} %dynamic-slice_bitcast_fusion), channel_id=1, source_target_pairs={{0,2},{1,3},{2,0},{3,1},{4,6},{5,7},{6,4},{7,5}} | collective-permute-start | bytes 4423688 | tf_op jit(solution)/shard_map/ppermute | solution.py:514
  645.4 43.9 %collective-permute-start.10 = (f32[72,2432]{1,0:T(8,128)S(1)}, f32[72,2432]{1,0:T(8,128)S(1)}, u32[]{:S(2)}, u32[]{:S(2)}) collective-permute-start(f32[72,2432]{1,0:T(8,128)S(1)} %dynamic-slice_bitcast_fusion.5), channel_id=1, source_target_pairs={{0,2},{1,3},{2,0},{3,1},{4,6},{5,7},{6,4},{7,5}} | collective-permute-start | bytes 2101256 | tf_op jit(solution)/shard_map/ppermute | solution.py:514
  679.7 11.5 %collective-permute-start.12 = (f32[72,2560]{1,0:T(8,128)S(1)}, f32[72,2560]{1,0:T(8,128)S(1)}, u32[]{:S(2)}, u32[]{:S(2)}) collective-permute-start(f32[72,2560]{1,0:T(8,128)S(1)} %dynamic-slice_bitcast_fusion.4), channel_id=1, source_target_pairs={{0,4},{1,5},{2,6},{3,7},{4,0},{5,1},{6,2},{7,3}} | collective-permute-start | bytes 2211848 | tf_op jit(solution)/shard_map/ppermute | solution.py:514
Sparse Core Ops, SparseCore 0:
  11.0 40.0 all-gather.6
  55.2 78.1 reduce-scatter.4
  136.8 68.4 reduce-scatter.2
  243.2 92.6 all-gather.12
  337.6 126.1 all-gather.10
  528.4 134.7 all-gather.8
